TPU v7x, 256 devices: a whole 4x4x8 slice. The times are simulated.
256 devices in a mesh: section: 8 (over z), tm: 32 (over y, x, core).
Axes of the slice: x: 4, y: 4, z: 8, core: 2. Of those that a mesh axis runs over, the one named last changes fastest.
Arguments:
- clean: float32 [4, 4, 2048], P(None, None, 'tm'), may hold values from -6 to 6
- noise: float32 [4, 4, 2048], P(None, None, 'tm'), may hold values from -6 to 6
- timestep: int32 [4], replicated, may hold values from 0 to 999
- lift: float32 [256], replicated, may hold values from -4 to 4
- norm_gain: float32 [8, 2, 256], P('section'), may hold values from 0.5 to 1.5
- norm_bias: float32 [8, 2, 256], P('section'), may hold values from -0.7 to 0.7
- conv_weight: bfloat16 [8, 2, 3, 3, 256, 256], P('section'), may hold values from -0.125 to 0.125
- time_proj: bfloat16 [8, 256, 256], P('section'), may hold values from -0.375 to 0.375
Outputs:
- skips: bfloat16 [8, 4, 4, 2048, 256], P('section', None, None, 'tm')
All inputs are finite; a program needn't handle non-finite values.
Results may differ from a plain program's by a relative error of at most 0.012.
Values may be sent and summed in bfloat16 or wider, within the bound.
No kernel may reach another device: no remote copies, remote signals or barrier semaphores. Data moves between devices by JAX's collectives and lax.ppermute only.
A program may use at most 64 MiB of HBM per device.

v0:
```python
import functools
import math

import jax
import jax.numpy as jnp
from jax import lax
from jax.experimental import pallas as pl
from jax.experimental.pallas import tpu as pltpu
from jax.sharding import Mesh
from jax.sharding import PartitionSpec as P

C = 256
STEPS = 1000
NZ, NY, NX, NC = 8, 4, 4, 2
FR = 4
OWN = 256
HALO = 16
STRIPS = 16
SPAN = (OWN + 2 * HALO) // STRIPS
ROWS = STRIPS * SPAN
POSITIONS = FR * OWN * NY * NC
COUNT = POSITIONS * 8
K = 9 * C
TM = ("y", "x", "c")
ROW = ("y", "c")


def group_total(x):
    lane = lax.broadcasted_iota(jnp.int32, x.shape, 1)
    for step in (1, 2, 4):
        up = pltpu.roll(x, C - step, 1)
        down = pltpu.roll(x, step, 1)
        x = x + jnp.where((lane & step) == 0, up, down)
    return x


def layer_kernel(index, slot, first, last, split, core, h_ref, part_ref, par_ref, valid_ref, own_ref, *refs):
    weights, rest = refs[: 1 + split], refs[1 + split :]
    out_ref, sums_ref = rest[:2]
    act, w_ref, sem = rest[2:]
    if split:
        size = K // 2
        lows = (core[0] * size, (1 - core[0]) * size)
        fetches = [
            pltpu.make_async_copy(w.at[slot], w_ref.at[pl.ds(pl.multiple_of(lo, size), size)], sem.at[n])
            for n, (w, lo) in enumerate(zip(weights, lows))
        ]
    else:
        fetches = [pltpu.make_async_copy(weights[0].at[slot], w_ref, sem.at[0])]
    for fetch in fetches:
        fetch.start()
    sums = jnp.sum(part_ref[...], axis=0)
    total, square = sums[0:1], sums[1:2]
    gain, bias, temb = par_ref[2 * index : 2 * index + 1], par_ref[2 * index + 1 : 2 * index + 2], par_ref[4:5]
    if first:
        square = square + 2.0 * temb * total + POSITIONS * temb * temb
        total = total + POSITIONS * temb
    both = group_total(jnp.concatenate([total, square, jnp.zeros((6, C), jnp.float32)], axis=0))
    mean = both[0:1] / COUNT
    var = both[1:2] / COUNT - mean * mean
    scale = lax.rsqrt(var + 1e-05) * gain

    def activate(f, _):
        for lo in range(0, ROWS, 2 * STRIPS):
            hi = lo + 2 * STRIPS
            h = h_ref[f, lo:hi].astype(jnp.float32)
            if first:
                h = h + temb
            x = (h - mean) * scale + bias
            half = 0.5 * x
            valid = valid_ref[lo:hi]
            a = (half + half * jnp.tanh(half)) * jnp.concatenate([valid, valid], axis=1)
            b = a.astype(jnp.bfloat16)
            act[f, lo:hi, C : 2 * C] = b
            if hi < ROWS:
                act[f, lo + STRIPS : hi + STRIPS, 0:C] = b
            else:
                act[f, hi - STRIPS : hi, 0:C] = b[:STRIPS]
                act[f, 0:STRIPS, 0:C] = pltpu.roll(a[STRIPS:], 1, 0).astype(jnp.bfloat16)
            if lo > 0:
                act[f, lo - STRIPS : hi - STRIPS, 2 * C : 3 * C] = b
            else:
                act[f, 0:STRIPS, 2 * C : 3 * C] = b[STRIPS:]
                act[f, ROWS - STRIPS : ROWS, 2 * C : 3 * C] = pltpu.roll(a[:STRIPS], STRIPS - 1, 0).astype(jnp.bfloat16)
        return 0

    lax.fori_loop(0, FR, activate, 0)
    for fetch in fetches:
        fetch.wait()
    total = jnp.zeros((8, C), jnp.float32)
    square = jnp.zeros((8, C), jnp.float32)
    mine = jnp.concatenate([own_ref[...], own_ref[...]], axis=1)
    for f in range(FR):
        h = h_ref[f].astype(jnp.float32)
        if first:
            h = h + temb
        for i in range(3):
            if 0 <= f + i - 1 < FR:
                h = h + jnp.dot(
                    act[f + i - 1], w_ref[3 * C * i : 3 * C * (i + 1)], preferred_element_type=jnp.float32
                )
        if last:
            low = h.astype(jnp.bfloat16)
            out_ref[f] = low
            h = low.astype(jnp.float32)
        else:
            out_ref[f] = h
        counted = h * mine
        total = total + jnp.sum(counted.reshape(ROWS // 8, 8, C), axis=0)
        square = square + jnp.sum((counted * h).reshape(ROWS // 8, 8, C), axis=0)
    sums = jnp.concatenate([jnp.sum(total, axis=0, keepdims=True), jnp.sum(square, axis=0, keepdims=True)], axis=0)
    for n in range(NY * NC):
        sums_ref[n] = sums


def layer(index, first, last, core, h, part, par, valid, own, weights):
    vmem = pl.BlockSpec(memory_space=pltpu.VMEM)
    hbm = pl.BlockSpec(memory_space=pltpu.HBM)
    out_shape = [
        jax.ShapeDtypeStruct((FR, ROWS, C), jnp.bfloat16 if last else jnp.float32),
        jax.ShapeDtypeStruct((NY * NC, 2, C), jnp.float32),
    ]
    return pl.pallas_call(
        functools.partial(layer_kernel, index, min(index, weights[0].shape[0] - 1), first, last, len(weights) - 1),
        out_shape=tuple(out_shape),
        in_specs=[pl.BlockSpec(memory_space=pltpu.SMEM)] + [vmem] * 5 + [hbm] * len(weights),
        out_specs=(vmem, vmem),
        scratch_shapes=[
            pltpu.VMEM((FR, ROWS, 3 * C), jnp.bfloat16),
            pltpu.VMEM((K, C), jnp.bfloat16),
            pltpu.SemaphoreType.DMA((2,)),
        ],
        compiler_params=pltpu.CompilerParams(vmem_limit_bytes=16 * 1024 * 1024),
        cost_estimate=pl.CostEstimate(flops=1200000000, bytes_accessed=4000000, transcendentals=300000),
        name="layer",
    )(core, h, part, par, valid, own, *weights)


def ordered_kernel(where, *refs):
    sources, (keep_ref, send_ref, x_ref, wide, line, sem) = refs[:NZ], refs[NZ:]
    for z in range(NZ):

        @pl.when(where[0] == z)
        def _():
            copy = pltpu.make_async_copy(sources[z], x_ref, sem)
            copy.start()
            copy.wait()

    core = where[1]
    for f in range(FR):
        for lane in range(0, C, 128):
            wide[...] = x_ref[f, :, lane : lane + 128].astype(jnp.float32)
            for a in range(STRIPS):
                line[a * SPAN : (a + 1) * SPAN] = wide[pl.ds(a, SPAN, stride=STRIPS)]
            for k in range(2):
                lo = pl.multiple_of(HALO + 128 * k + 64 * core, 16)
                keep_ref[k, f, :, lane : lane + 128] = line[pl.ds(lo, 64)].astype(jnp.bfloat16)
                lo = pl.multiple_of(HALO + 128 * k + 64 * (1 - core), 16)
                send_ref[k, f, :, lane : lane + 128] = line[pl.ds(lo, 64)].astype(jnp.bfloat16)


def ordered(where, sources):
    vmem = pl.BlockSpec(memory_space=pltpu.VMEM)
    half = jax.ShapeDtypeStruct((2, FR, 64, C), jnp.bfloat16)
    return pl.pallas_call(
        ordered_kernel,
        out_shape=(half, half),
        in_specs=[pl.BlockSpec(memory_space=pltpu.SMEM)] + [pl.BlockSpec(memory_space=pl.ANY)] * NZ,
        out_specs=(vmem, vmem),
        scratch_shapes=[
            pltpu.VMEM((FR, ROWS, C), jnp.bfloat16),
            pltpu.VMEM((ROWS, 128), jnp.float32),
            pltpu.VMEM((ROWS, 128), jnp.float32),
            pltpu.SemaphoreType.DMA,
        ],
        compiler_params=pltpu.CompilerParams(vmem_limit_bytes=8 * 1024 * 1024),
        cost_estimate=pl.CostEstimate(flops=2000000, bytes_accessed=2000000, transcendentals=0),
        name="ordered",
    )(where, *sources)


def halves_kernel(where, w_hbm, two_hbm, one_hbm, held, sem):
    size = K // 2
    z, core = where[0], where[1]
    rows = pl.ds(pl.multiple_of(core * size, size), size)

    def carry(index, target):
        take = pltpu.make_async_copy(w_hbm.at[index, rows], held.at[index], sem.at[index])
        take.start()
        take.wait()
        give = pltpu.make_async_copy(held.at[index], target.at[index], sem.at[index])
        give.start()
        give.wait()

    @pl.when((z == 2) | (z == 3) | (z == 6))
    def _():
        carry(0, two_hbm)

    @pl.when((z == 2) | (z == 3))
    def _():
        carry(1, two_hbm)

    @pl.when((z == 4) | (z == 5))
    def _():
        carry(0, one_hbm)


def halves(where, weight):
    hbm = pl.BlockSpec(memory_space=pltpu.HBM)
    return pl.pallas_call(
        halves_kernel,
        out_shape=tuple(jax.ShapeDtypeStruct((n, K // 2, C), jnp.bfloat16) for n in (2, 1)),
        in_specs=[pl.BlockSpec(memory_space=pltpu.SMEM), hbm],
        out_specs=(hbm, hbm),
        scratch_shapes=[pltpu.VMEM((2, K // 2, C), jnp.bfloat16), pltpu.SemaphoreType.DMA((2,))],
        compiler_params=pltpu.CompilerParams(vmem_limit_bytes=4 * 1024 * 1024),
        cost_estimate=pl.CostEstimate(flops=1000000, bytes_accessed=5000000, transcendentals=0),
        name="halves",
    )(where, weight)


def moved(value, moves, axis="z"):
    return lax.ppermute(value, axis, moves)


def swapped(value):
    return moved(value, [(0, 1), (1, 0)], "c")


def program(clean, noise, timestep, lift, norm_gain, norm_bias, conv_weight, time_proj):
    z, y, c = (lax.axis_index(a) for a in ("z", "y", "c"))
    place = 2 * y + c
    core = c.reshape(1).astype(jnp.int32)
    own_w = conv_weight[0].reshape(2, K, C)
    where = jnp.stack([z, c]).astype(jnp.int32)
    half, one = halves(where, own_w)
    near = moved(half, [(2, 1), (6, 7)])

    steps_f = timestep.astype(jnp.float32)
    level = jnp.cos(math.pi / 2.0 * (steps_f / STEPS + 0.008) / 1.008) ** 2
    noisy = jnp.sqrt(level)[:, None, None] * clean + jnp.sqrt(1.0 - level)[:, None, None] * noise
    sent = jnp.broadcast_to(noisy[None, :, None], (NY, NX, NC, FR, 64)).reshape(NY * NX * NC, FR * 64)
    lifts = jnp.stack([lift, lift * lift])
    line = lax.all_to_all(sent, TM, 0, 0, tiled=True)
    part = (jnp.stack([line.sum(), (line * line).sum()])[:, None] * lifts)[None]
    line = line.reshape(NY * NX * NC, FR, 64).transpose(1, 0, 2).reshape(FR, -1)
    line = jnp.pad(line, ((0, 0), (HALO, HALO)))
    mine = lax.dynamic_slice_in_dim(line, place * OWN, ROWS, axis=1)
    mine = mine.reshape(FR, STRIPS, SPAN).transpose(0, 2, 1).reshape(FR, ROWS)
    h = (mine[..., None] * lift).astype(jnp.bfloat16)

    row = lax.broadcasted_iota(jnp.int32, (ROWS, 128), 0)
    frame = (row % STRIPS) * SPAN + row // STRIPS
    when = frame + place * OWN - HALO
    valid = ((when >= 0) & (when < OWN * NY * NC)).astype(jnp.float32)
    own = ((frame >= HALO) & (frame < HALO + OWN)).astype(jnp.float32)

    few = C // 2
    freqs = jnp.exp(-math.log(10000.0) * jnp.arange(few, dtype=jnp.float32) / few)
    angles = steps_f[:, None] * freqs[None, :]
    emb = jnp.concatenate([jnp.sin(angles), jnp.cos(angles)], axis=1).astype(jnp.bfloat16)
    temb = jnp.dot(emb, time_proj[0], preferred_element_type=jnp.float32)
    temb = lax.dynamic_slice_in_dim(temb, lax.axis_index("x"), 1, axis=0)
    own_p = jnp.concatenate(
        [norm_gain[0, 0:1], norm_bias[0, 0:1], norm_gain[0, 1:2], norm_bias[0, 1:2], temb, jnp.zeros((3, C), jnp.float32)]
    )
    p3 = moved(own_p, [(3, 1), (5, 7)])
    p4 = moved(own_p, [(4, 1)])
    h, part, valid, own, own_p, p3, p4, where, core = lax.optimization_barrier(
        (h, part, valid, own, own_p, p3, p4, where, core)
    )

    def run(index, last, h, part, p, weights):
        return layer(index, index == 0, last, core, h, part, p, valid, own, weights)

    def stats(part, *settled):
        part, *settled = lax.optimization_barrier((part, *settled))
        part = lax.all_to_all(part, ROW, 0, 0, tiled=True)
        return (part, *settled) if settled else part

    own_w = (own_w,)
    h, part = run(0, False, h, part, own_p, own_w)
    part, half = lax.optimization_barrier((stats(part), half))
    mid = moved(half, [(3, 1)])
    h, part = run(1, True, h, part, own_p, own_w)
    ret0 = h
    part = moved(part, [(0, 1)])
    hopped = moved(h, [(0, 1)])
    part, later_p, one = lax.optimization_barrier((stats(part), own_p, one))
    p2 = moved(later_p, [(2, 1), (6, 7)])
    w4 = moved(one, [(4, 1)])
    w5 = moved(one, [(5, 7)])
    h, part = lax.optimization_barrier((hopped, part))
    h, part = run(0, False, h, part, own_p, own_w)
    part, p2, near = stats(part, p2, near)
    part, near = lax.optimization_barrier((part, near))
    h, part = run(1, True, h, part, own_p, own_w)
    ret1 = h
    nears = swapped(near)
    part, nears = stats(part, nears)
    near = (near, nears)
    h, part = run(0, False, h, part, p2, near)
    part, mid = stats(part, mid)
    part, mid = lax.optimization_barrier((part, mid))
    h, part = run(1, True, h, part, p2, near)
    ret2 = moved(h, [(1, 2)])
    mids = swapped(mid)
    part, mids = stats(part, mids)
    mid = (mid, mids)
    h, part = run(0, False, h, part, p3, mid)
    part, w4 = stats(part, w4)
    part, w4 = lax.optimization_barrier((part, w4))
    h, part = run(1, True, h, part, p3, mid)
    ret3 = moved(h, [(1, 3)])
    w4s = swapped(w4)
    part, w4s, w5 = stats(part, w4s, w5)
    part, w5 = lax.optimization_barrier((part, w5))
    h, part = run(0, True, h, part, p4, (w4, w4s))
    w5s = swapped(w5)
    part, w5s = lax.optimization_barrier((part, w5s))
    part = moved(part, [(1, 7)])
    ret4 = moved(h, [(1, 4)])
    h, part = lax.optimization_barrier((moved(h, [(1, 7)]), stats(part)))
    h, part = run(0, True, h, part, p3, (w5, w5s))
    ret5 = moved(h, [(7, 5)])
    h, part = run(0, True, h, stats(part), p2, near)
    ret6 = moved(h, [(7, 6)])
    h, part = run(0, True, h, stats(part), own_p, own_w)
    ret7 = h

    keep, send = ordered(where, [ret0, ret1, ret2, ret3, ret4, ret5, ret6, ret7])
    got = swapped(send)
    blocks = jnp.where(c == 0, jnp.concatenate([keep, got]), jnp.concatenate([got, keep]))
    return lax.all_to_all(blocks, "x", 0, 0, tiled=True)[None]


def solution(mesh):
    grid = Mesh(mesh.devices.reshape(NZ, NY, NX, NC), ("z", "y", "x", "c"))
    in_specs = (
        P(None, None, TM),
        P(None, None, TM),
        P(),
        P(),
        P("z", None, None),
        P("z", None, None),
        P("z", None, None, None, None, None),
        P("z", None, None),
    )
    return jax.shard_map(program, mesh=grid, in_specs=in_specs, out_specs=P("z", None, None, TM, None), check_vma=False)
```

profile of v0, /device:TPU:128, one launch (start us, length us, event | category | flops | bytes accessed | tf_op | source)
XLA Modules:
  0.0 253.8 jit_solution(13291738060280686345)
XLA Ops:
  2.5 1.7 collective-permute-start.1
  6.5 7.3 %all-to-all-start = ((f32[32,1,256]{2,1,0:T(1,128)}), f32[32,1,256]{2,1,0:T(1,128)S(1)}, u32[]{:S(2)}, u32[]{:S(2)}) async-start(f32[32,1,256]{2,1,0:T(1,128)} %all_to_all.42), calls=%async_computation | async-start | bytes 65536 | tf_op jit(solution)/shard_map/all_to_all | solution.py:244
  19.4 1.9 all-to-all-done
  24.3 2.3 layer.12
  26.6 7.8 %all_to_all.69.part_ref = f32[8,2,256]{2,1,0:T(2,128)S(1)} all-to-all(f32[8,2,256]{2,1,0:T(2,128)S(1)} %get-tuple-element.82), channel_id=1, replica_groups=mesh['z'=8,'y'=4,'x'=4,'c'=2] {'y','c'}, dimensions={0} | all-to-all | bytes 32768 | tf_op jit(solution)/shard_map/all_to_all | solution.py:278
  34.5 2.3 layer.13
  38.2 7.7 %all_to_all.70.part_ref = f32[8,2,256]{2,1,0:T(2,128)S(1)} all-to-all(f32[8,2,256]{2,1,0:T(2,128)S(1)} %collective-permute-done.3), channel_id=1, replica_groups=mesh['z'=8,'y'=4,'x'=4,'c'=2] {'y','c'}, dimensions={0} | all-to-all | bytes 32768 | tf_op jit(solution)/shard_map/all_to_all | solution.py:278
  46.6 2.3 layer.14
  48.9 7.7 %all_to_all.71.part_ref = f32[8,2,256]{2,1,0:T(2,128)S(1)} all-to-all(f32[8,2,256]{2,1,0:T(2,128)S(1)} %get-tuple-element.94), channel_id=1, replica_groups=mesh['z'=8,'y'=4,'x'=4,'c'=2] {'y','c'}, dimensions={0} | all-to-all | bytes 32768 | tf_op jit(solution)/shard_map/all_to_all | solution.py:278
  57.4 2.3 layer.15
  59.7 7.7 %all_to_all.72.part_ref = f32[8,2,256]{2,1,0:T(2,128)S(1)} all-to-all(f32[8,2,256]{2,1,0:T(2,128)S(1)} %get-tuple-element.100), channel_id=1, replica_groups=mesh['z'=8,'y'=4,'x'=4,'c'=2] {'y','c'}, dimensions={0} | all-to-all | bytes 32768 | tf_op jit(solution)/shard_map/all_to_all | solution.py:278
  67.4 2.5 layer.16
  70.0 7.7 %all_to_all.73.part_ref = f32[8,2,256]{2,1,0:T(2,128)S(1)} all-to-all(f32[8,2,256]{2,1,0:T(2,128)S(1)} %get-tuple-element.106), channel_id=1, replica_groups=mesh['z'=8,'y'=4,'x'=4,'c'=2] {'y','c'}, dimensions={0} | all-to-all | bytes 32768 | tf_op jit(solution)/shard_map/all_to_all | solution.py:278
  77.7 37.8 %collective-permute-start.10 = (bf16[1,1152,256]{2,1,0:T(8,128)(2,1)S(1)}, bf16[1,1152,256]{2,1,0:T(8,128)(2,1)S(1)}, u32[]{:S(2)}, u32[]{:S(2)}) collective-permute-start(bf16[1,1152,256]{2,1,0:T(8,128)(2,1)S(1)} %copy-done.12), channel_id=1, source_target_pairs={{128,32},{129,33},{130,34},{131,35},{132,36},{133,37},{134,38},{13... | collective-permute-start | bytes 1769480 | tf_op jit(solution)/shard_map/ppermute | solution.py:223
  115.6 2.5 layer.17
  118.1 7.7 %all_to_all.74.part_ref = f32[8,2,256]{2,1,0:T(2,128)S(1)} all-to-all(f32[8,2,256]{2,1,0:T(2,128)S(1)} %get-tuple-element.112), channel_id=1, replica_groups=mesh['z'=8,'y'=4,'x'=4,'c'=2] {'y','c'}, dimensions={0} | all-to-all | bytes 32768 | tf_op jit(solution)/shard_map/all_to_all | solution.py:278
  125.8 2.9 %layer.18 = (f32[4,288,256]{2,1,0:T(8,128)S(1)}, f32[8,2,256]{2,1,0:T(2,128)}) custom-call(s32[1]{0:T(128)} %bitcast.12.core, bf16[4,288,256]{2,1,0:T(8,128)(2,1)S(1)} %get-tuple-element.109.h_ref, f32[8,2,256]{2,1,0:T(2,128)S(1)} %all_to_all.74.part_ref, f32[8,256]{1,0:T(8,128)S(1)} %collective-permute-done.par_ref, ...), custom_call_target="tpu_custom_call" | custom-call | flops 1200000000 | bytes 4000000 | tf_op jit(solution)/shard_map/layer/pallas_call | solution.py:123
  130.7 3.3 %all-to-all-start.7 = ((f32[8,2,256]{2,1,0:T(2,128)}), f32[8,2,256]{2,1,0:T(2,128)S(1)}, u32[]{:S(2)}, u32[]{:S(2)}) async-start(f32[8,2,256]{2,1,0:T(2,128)} %get-tuple-element.118), calls=%async_computation.7 | async-start | bytes 32768 | tf_op jit(solution)/shard_map/all_to_all | solution.py:278
  135.6 3.7 %all-to-all-done.7.part_ref = f32[8,2,256]{2,1,0:T(2,128)S(1)} async-done(((f32[8,2,256]{2,1,0:T(2,128)}), f32[8,2,256]{2,1,0:T(2,128)S(1)}, u32[]{:S(2)}, u32[]{:S(2)}) %all-to-all-start.7) | async-done | bytes 16416 | tf_op jit(solution)/shard_map/all_to_all | solution.py:278
  143.1 2.3 layer.19
  145.4 7.7 %all_to_all.75.part_ref = f32[8,2,256]{2,1,0:T(2,128)S(1)} all-to-all(f32[8,2,256]{2,1,0:T(2,128)S(1)} %get-tuple-element.124), channel_id=1, replica_groups=mesh['z'=8,'y'=4,'x'=4,'c'=2] {'y','c'}, dimensions={0} | all-to-all | bytes 32768 | tf_op jit(solution)/shard_map/all_to_all | solution.py:278
  153.2 3.2 %layer.20 = (bf16[4,288,256]{2,1,0:T(8,128)(2,1)}, f32[8,2,256]{2,1,0:T(2,128)S(1)}) custom-call(s32[1]{0:T(128)} %bitcast.12.core, bf16[4,288,256]{2,1,0:T(8,128)(2,1)S(1)} %get-tuple-element.121.h_ref, f32[8,2,256]{2,1,0:T(2,128)S(1)} %all_to_all.75.part_ref, f32[8,256]{1,0:T(8,128)S(1)} %collective-permute-done.1.par_ref, ...), custom_call_target="tpu_custom_call" | custom-call | flops 1200000000 | bytes 4000000 | tf_op jit(solution)/shard_map/layer/pallas_call | solution.py:123
  160.0 3.3 %all-to-all-start.9 = ((f32[8,2,256]{2,1,0:T(2,128)}), f32[8,2,256]{2,1,0:T(2,128)S(1)}, u32[]{:S(2)}, u32[]{:S(2)}) async-start(f32[8,2,256]{2,1,0:T(2,128)} %collective-permute-done.17), calls=%async_computation.9 | async-start | bytes 32768 | tf_op jit(solution)/shard_map/all_to_all | solution.py:278
  163.3 5.3 %all-to-all-done.9.part_ref = f32[8,2,256]{2,1,0:T(2,128)S(1)} async-done(((f32[8,2,256]{2,1,0:T(2,128)}), f32[8,2,256]{2,1,0:T(2,128)S(1)}, u32[]{:S(2)}, u32[]{:S(2)}) %all-to-all-start.9) | async-done | bytes 16416 | tf_op jit(solution)/shard_map/all_to_all | solution.py:278
  169.7 4.2 %layer.21 = (bf16[4,288,256]{2,1,0:T(8,128)(2,1)S(1)}, f32[8,2,256]{2,1,0:T(2,128)}) custom-call(s32[1]{0:T(128)} %bitcast.12.core, bf16[4,288,256]{2,1,0:T(8,128)(2,1)} %collective-permute-done.15.h_ref, f32[8,2,256]{2,1,0:T(2,128)S(1)} %all-to-all-done.9.part_ref, f32[8,256]{1,0:T(8,128)S(1)} %collective-permute-done.par_ref, ...), custom_call_target="tpu_custom_call" | custom-call | flops 1200000000 | bytes 4000000 | tf_op jit(solution)/shard_map/layer/pallas_call | solution.py:123
  174.7 3.3 %all-to-all-start.10 = ((f32[8,2,256]{2,1,0:T(2,128)}), f32[8,2,256]{2,1,0:T(2,128)S(1)}, u32[]{:S(2)}, u32[]{:S(2)}) async-start(f32[8,2,256]{2,1,0:T(2,128)} %get-tuple-element.137), calls=%async_computation.10 | async-start | bytes 32768 | tf_op jit(solution)/shard_map/all_to_all | solution.py:278
  186.2 2.5 layer.22
  189.4 9.9 %all_to_all.76.part_ref = f32[8,2,256]{2,1,0:T(2,128)S(1)} all-to-all(f32[8,2,256]{2,1,0:T(2,128)S(1)} %get-tuple-element.139), channel_id=1, replica_groups=mesh['z'=8,'y'=4,'x'=4,'c'=2] {'y','c'}, dimensions={0} | all-to-all | bytes 32768 | tf_op jit(solution)/shard_map/all_to_all | solution.py:278
  199.3 3.0 %layer.23 = (bf16[4,288,256]{2,1,0:T(8,128)(2,1)S(1)}, f32[8,2,256]{2,1,0:T(2,128)}) custom-call(s32[1]{0:T(128)} %bitcast.12.core, bf16[4,288,256]{2,1,0:T(8,128)(2,1)S(1)} %get-tuple-element.138.h_ref, f32[8,2,256]{2,1,0:T(2,128)S(1)} %all_to_all.76.part_ref, f32[8,256]{1,0:T(8,128)S(1)} %concatenate.21.par_ref, ...), custom_call_target="tpu_custom_call" | custom-call | flops 1200000000 | bytes 4000000 | tf_op jit(solution)/shard_map/layer/pallas_call | solution.py:123
  202.3 32.6 %collective-permute-done.14.refs_4_ = bf16[4,288,256]{2,1,0:T(8,128)(2,1)} collective-permute-done((bf16[4,288,256]{2,1,0:T(8,128)(2,1)}, bf16[4,288,256]{2,1,0:T(8,128)(2,1)}, u32[]{:S(2)}, u32[]{:S(2)}) %collective-permute-start.14) | collective-permute-done | bytes 589856 | tf_op jit(solution)/shard_map/ppermute | solution.py:223
  234.9 2.9 %ordered.1 = (bf16[2,4,64,256]{3,2,1,0:T(8,128)(2,1)S(1)}, bf16[2,4,64,256]{3,2,1,0:T(8,128)(2,1)}) custom-call(s32[2]{0:T(128)S(1)} %pad_add_fusion.where, bf16[4,288,256]{2,1,0:T(8,128)(2,1)S(1)} %get-tuple-element.85.refs_0_, bf16[4,288,256]{2,1,0:T(8,128)(2,1)S(1)} %copy-done.4, bf16[4,288,256]{2,1,0:T(8,128)(2,1)} %collective-permute-done.8.refs_2_, ...), custom_call_target="tpu_custom_call" | custom-call | flops 2000000 | bytes 2000000 | tf_op jit(solution)/shard_map/ordered/pallas_call | solution.py:165
  239.7 13.3 %all_to_all.77 = bf16[4,4,64,256]{3,2,1,0:T(8,128)(2,1)S(1)} all-to-all(bf16[4,4,64,256]{3,2,1,0:T(8,128)(2,1)S(1)} %maximum_select_fusion), channel_id=1, replica_groups=mesh['z'=8,'y'=4,'x'=4,'c'=2] {'x'}, dimensions={0} | all-to-all | bytes 1048576 | tf_op jit(solution)/shard_map/all_to_all | solution.py:334
  (120 shorter events, 40.4 us)
Async XLA Ops:
  1.9 22.4 %collective-permute-start = (f32[8,256]{1,0:T(8,128)S(1)}, f32[8,256]{1,0:T(8,128)S(1)}, u32[]{:S(2)}, u32[]{:S(2)}) collective-permute-start(f32[8,256]{1,0:T(8,128)S(1)} %concatenate.21.par_ref), channel_id=1, source_target_pairs={{96,32},{160,224},{97,33},{161,225},{98,34},{162,226},{99,35},{163... | collective-permute-start | bytes 24584 | tf_op jit(solution)/shard_map/ppermute | solution.py:223
  2.5 21.8 %collective-permute-start.1 = (f32[8,256]{1,0:T(8,128)S(1)}, f32[8,256]{1,0:T(8,128)S(1)}, u32[]{:S(2)}, u32[]{:S(2)}) collective-permute-start(f32[8,256]{1,0:T(8,128)S(1)} %concatenate.21.par_ref), channel_id=1, source_target_pairs={{128,32},{129,33},{130,34},{131,35},{132,36},{133,37},{134,38},{13... | collective-permute-start | bytes 24584 | tf_op jit(solution)/shard_map/ppermute | solution.py:223
  6.5 14.7 %all-to-all-start = ((f32[32,1,256]{2,1,0:T(1,128)}), f32[32,1,256]{2,1,0:T(1,128)S(1)}, u32[]{:S(2)}, u32[]{:S(2)}) async-start(f32[32,1,256]{2,1,0:T(1,128)} %all_to_all.42), calls=%async_computation | async-start | bytes 65536 | tf_op jit(solution)/shard_map/all_to_all | solution.py:244
  17.3 31.6 %collective-permute-start.5 = (bf16[2,1152,256]{2,1,0:T(8,128)(2,1)}, bf16[2,1152,256]{2,1,0:T(8,128)(2,1)}, u32[]{:S(2)}, u32[]{:S(2)}) collective-permute-start(bf16[2,1152,256]{2,1,0:T(8,128)(2,1)} %get-tuple-element.105), channel_id=1, source_target_pairs={{64,32},{192,224},{65,33},{193,225},{66,34},{194,226},{67,35},{195... | collective-permute-start | bytes 3538952 | tf_op jit(solution)/shard_map/ppermute | solution.py:223
  36.8 9.8 %collective-permute-start.2 = (bf16[4,288,256]{2,1,0:T(8,128)(2,1)S(1)}, bf16[4,288,256]{2,1,0:T(8,128)(2,1)S(1)}, u32[]{:S(2)}, u32[]{:S(2)}) collective-permute-start(bf16[4,288,256]{2,1,0:T(8,128)(2,1)S(1)} %get-tuple-element.85.refs_0_), channel_id=1, source_target_pairs={{0,32},{1,33},{2,34},{3,35},{4,36},{5,37},{6,38},{7,39},{8,40},{9,... | collective-permute-start | bytes 1769480 | tf_op jit(solution)/shard_map/ppermute | solution.py:223
  37.5 0.7 collective-permute-start.3
  45.9 3.0 %collective-permute-start.4 = (f32[8,256]{1,0:T(8,128)S(1)}, f32[8,256]{1,0:T(8,128)S(1)}, u32[]{:S(2)}, u32[]{:S(2)}) collective-permute-start(f32[8,256]{1,0:T(8,128)S(1)} %concatenate.21.par_ref), channel_id=1, source_target_pairs={{64,32},{192,224},{65,33},{193,225},{66,34},{194,226},{67,35},{195... | collective-permute-start | bytes 24584 | tf_op jit(solution)/shard_map/ppermute | solution.py:223
  56.6 3.1 %collective-permute-start.6 = (bf16[2,1152,256]{2,1,0:T(8,128)(2,1)}, bf16[2,1152,256]{2,1,0:T(8,128)(2,1)S(1)}, u32[]{:S(2)}, u32[]{:S(2)}) collective-permute-start(bf16[2,1152,256]{2,1,0:T(8,128)(2,1)} %collective-permute-done.5.refs_0_), channel_id=1, source_target_pairs={{0,1},{1,0},{2,3},{3,2},{4,5},{5,4},{6,7},{7,6},{8,9},{9,8},{10,11... | collective-permute-start | bytes 3538952 | tf_op jit(solution)/shard_map/ppermute | solution.py:223
  56.6 13.3 %collective-permute-start.7 = (bf16[2,1152,256]{2,1,0:T(8,128)(2,1)}, bf16[2,1152,256]{2,1,0:T(8,128)(2,1)S(1)}, u32[]{:S(2)}, u32[]{:S(2)}) collective-permute-start(bf16[2,1152,256]{2,1,0:T(8,128)(2,1)} %get-tuple-element.105), channel_id=1, source_target_pairs={{96,32},{97,33},{98,34},{99,35},{100,36},{101,37},{102,38},{103,39... | collective-permute-start | bytes 3538952 | tf_op jit(solution)/shard_map/ppermute | solution.py:223
  59.7 55.9 %copy-start.5 = (bf16[2,1152,256]{2,1,0:T(8,128)(2,1)}, bf16[2,1152,256]{2,1,0:T(8,128)(2,1)S(1)}, u32[]{:S(2)}) copy-start(bf16[2,1152,256]{2,1,0:T(8,128)(2,1)S(1)} %collective-permute-done.6.refs_1_) | copy-start | bytes 3538948
  67.4 10.3 %copy-start.12 = (bf16[1,1152,256]{2,1,0:T(8,128)(2,1)S(1)}, bf16[1,1152,256]{2,1,0:T(8,128)(2,1)}, u32[]{:S(2)}) copy-start(bf16[1,1152,256]{2,1,0:T(8,128)(2,1)} %copy-done.11) | copy-start | bytes 1769476
  70.0 55.9 %copy-start.7 = (bf16[2,1152,256]{2,1,0:T(8,128)(2,1)}, bf16[2,1152,256]{2,1,0:T(8,128)(2,1)S(1)}, u32[]{:S(2)}) copy-start(bf16[2,1152,256]{2,1,0:T(8,128)(2,1)S(1)} %collective-permute-done.7.refs_0_) | copy-start | bytes 3538948
  77.7 40.4 %collective-permute-start.9 = (bf16[2,1152,256]{2,1,0:T(8,128)(2,1)S(1)}, bf16[2,1152,256]{2,1,0:T(8,128)(2,1)S(1)}, u32[]{:S(2)}, u32[]{:S(2)}) collective-permute-start(bf16[2,1152,256]{2,1,0:T(8,128)(2,1)S(1)} %collective-permute-done.7.refs_0_), channel_id=1, source_target_pairs={{0,1},{1,0},{2,3},{3,2},{4,5},{5,4},{6,7},{7,6},{8,9},{9,8},{10,11... | collective-permute-start | bytes 3538952 | tf_op jit(solution)/shard_map/ppermute | solution.py:223
  77.7 52.2 %collective-permute-start.10 = (bf16[1,1152,256]{2,1,0:T(8,128)(2,1)S(1)}, bf16[1,1152,256]{2,1,0:T(8,128)(2,1)S(1)}, u32[]{:S(2)}, u32[]{:S(2)}) collective-permute-start(bf16[1,1152,256]{2,1,0:T(8,128)(2,1)S(1)} %copy-done.12), channel_id=1, source_target_pairs={{128,32},{129,33},{130,34},{131,35},{132,36},{133,37},{134,38},{13... | collective-permute-start | bytes 1769480 | tf_op jit(solution)/shard_map/ppermute | solution.py:223
  118.1 10.7 %copy-start.13 = (bf16[4,288,256]{2,1,0:T(8,128)(2,1)}, bf16[4,288,256]{2,1,0:T(8,128)(2,1)S(1)}, u32[]{:S(2)}) copy-start(bf16[4,288,256]{2,1,0:T(8,128)(2,1)S(1)} %get-tuple-element.109.h_ref) | copy-start | bytes 1769476
  118.1 10.7 %copy-start.9 = (bf16[2,1152,256]{2,1,0:T(8,128)(2,1)}, bf16[2,1152,256]{2,1,0:T(8,128)(2,1)S(1)}, u32[]{:S(2)}) copy-start(bf16[2,1152,256]{2,1,0:T(8,128)(2,1)S(1)} %collective-permute-done.9.refs_1_) | copy-start | bytes 3538948
  130.7 8.6 %all-to-all-start.7 = ((f32[8,2,256]{2,1,0:T(2,128)}), f32[8,2,256]{2,1,0:T(2,128)S(1)}, u32[]{:S(2)}, u32[]{:S(2)}) async-start(f32[8,2,256]{2,1,0:T(2,128)} %get-tuple-element.118), calls=%async_computation.7 | async-start | bytes 32768 | tf_op jit(solution)/shard_map/all_to_all | solution.py:278
  134.0 11.4 %collective-permute-start.13 = (bf16[1,1152,256]{2,1,0:T(8,128)(2,1)}, bf16[1,1152,256]{2,1,0:T(8,128)(2,1)}, u32[]{:S(2)}, u32[]{:S(2)}) collective-permute-start(bf16[1,1152,256]{2,1,0:T(8,128)(2,1)} %copy-done.11), channel_id=1, source_target_pairs={{160,224},{161,225},{162,226},{163,227},{164,228},{165,229},{166,2... | collective-permute-start | bytes 1769480 | tf_op jit(solution)/shard_map/ppermute | solution.py:223
  139.3 6.1 %collective-permute-start.12 = (bf16[1,1152,256]{2,1,0:T(8,128)(2,1)}, bf16[1,1152,256]{2,1,0:T(8,128)(2,1)S(1)}, u32[]{:S(2)}, u32[]{:S(2)}) collective-permute-start(bf16[1,1152,256]{2,1,0:T(8,128)(2,1)} %copy-done.17), channel_id=1, source_target_pairs={{0,1},{1,0},{2,3},{3,2},{4,5},{5,4},{6,7},{7,6},{8,9},{9,8},{10,11... | collective-permute-start | bytes 1769480 | tf_op jit(solution)/shard_map/ppermute | solution.py:223
  145.4 10.9 %copy-start.14 = (bf16[4,288,256]{2,1,0:T(8,128)(2,1)}, bf16[4,288,256]{2,1,0:T(8,128)(2,1)S(1)}, u32[]{:S(2)}) copy-start(bf16[4,288,256]{2,1,0:T(8,128)(2,1)S(1)} %get-tuple-element.121.h_ref) | copy-start | bytes 1769476
  153.2 4.7 %collective-permute-start.16 = (bf16[1,1152,256]{2,1,0:T(8,128)(2,1)}, bf16[1,1152,256]{2,1,0:T(8,128)(2,1)S(1)}, u32[]{:S(2)}, u32[]{:S(2)}) collective-permute-start(bf16[1,1152,256]{2,1,0:T(8,128)(2,1)} %collective-permute-done.13.refs_0_), channel_id=1, source_target_pairs={{0,1},{1,0},{2,3},{3,2},{4,5},{5,4},{6,7},{7,6},{8,9},{9,8},{10,11... | collective-permute-start | bytes 1769480 | tf_op jit(solution)/shard_map/ppermute | solution.py:223
  156.3 7.0 %collective-permute-start.15 = (bf16[4,288,256]{2,1,0:T(8,128)(2,1)}, bf16[4,288,256]{2,1,0:T(8,128)(2,1)}, u32[]{:S(2)}, u32[]{:S(2)}) collective-permute-start(bf16[4,288,256]{2,1,0:T(8,128)(2,1)} %get-tuple-element.129), channel_id=1, source_target_pairs={{32,224},{33,225},{34,226},{35,227},{36,228},{37,229},{38,230},{39... | collective-permute-start | bytes 1769480 | tf_op jit(solution)/shard_map/ppermute | solution.py:223
  158.7 1.3 collective-permute-start.17
  160.0 8.6 %all-to-all-start.9 = ((f32[8,2,256]{2,1,0:T(2,128)}), f32[8,2,256]{2,1,0:T(2,128)S(1)}, u32[]{:S(2)}, u32[]{:S(2)}) async-start(f32[8,2,256]{2,1,0:T(2,128)} %collective-permute-done.17), calls=%async_computation.9 | async-start | bytes 32768 | tf_op jit(solution)/shard_map/all_to_all | solution.py:278
  174.7 9.2 %all-to-all-start.10 = ((f32[8,2,256]{2,1,0:T(2,128)}), f32[8,2,256]{2,1,0:T(2,128)S(1)}, u32[]{:S(2)}, u32[]{:S(2)}) async-start(f32[8,2,256]{2,1,0:T(2,128)} %get-tuple-element.137), calls=%async_computation.10 | async-start | bytes 32768 | tf_op jit(solution)/shard_map/all_to_all | solution.py:278
  178.0 24.2 %collective-permute-start.8 = (bf16[4,288,256]{2,1,0:T(8,128)(2,1)}, bf16[4,288,256]{2,1,0:T(8,128)(2,1)}, u32[]{:S(2)}, u32[]{:S(2)}) collective-permute-start(bf16[4,288,256]{2,1,0:T(8,128)(2,1)} %copy-done.13), channel_id=1, source_target_pairs={{32,64},{33,65},{34,66},{35,67},{36,68},{37,69},{38,70},{39,71},{4... | collective-permute-start | bytes 1769480 | tf_op jit(solution)/shard_map/ppermute | solution.py:223
  179.6 22.7 %collective-permute-start.11 = (bf16[4,288,256]{2,1,0:T(8,128)(2,1)}, bf16[4,288,256]{2,1,0:T(8,128)(2,1)}, u32[]{:S(2)}, u32[]{:S(2)}) collective-permute-start(bf16[4,288,256]{2,1,0:T(8,128)(2,1)} %copy-done.14), channel_id=1, source_target_pairs={{32,96},{33,97},{34,98},{35,99},{36,100},{37,101},{38,102},{39,103... | collective-permute-start | bytes 1769480 | tf_op jit(solution)/shard_map/ppermute | solution.py:223
  181.1 53.8 %collective-permute-start.14 = (bf16[4,288,256]{2,1,0:T(8,128)(2,1)}, bf16[4,288,256]{2,1,0:T(8,128)(2,1)}, u32[]{:S(2)}, u32[]{:S(2)}) collective-permute-start(bf16[4,288,256]{2,1,0:T(8,128)(2,1)} %get-tuple-element.129), channel_id=1, source_target_pairs={{32,128},{33,129},{34,130},{35,131},{36,132},{37,133},{38,134},{39... | collective-permute-start | bytes 1769480 | tf_op jit(solution)/shard_map/ppermute | solution.py:223
  182.3 52.6 %collective-permute-start.18 = (bf16[4,288,256]{2,1,0:T(8,128)(2,1)}, bf16[4,288,256]{2,1,0:T(8,128)(2,1)}, u32[]{:S(2)}, u32[]{:S(2)}) collective-permute-start(bf16[4,288,256]{2,1,0:T(8,128)(2,1)} %copy-done.15), channel_id=1, source_target_pairs={{224,160},{225,161},{226,162},{227,163},{228,164},{229,165},{230,1... | collective-permute-start | bytes 1769480 | tf_op jit(solution)/shard_map/ppermute | solution.py:223
  188.7 46.2 %collective-permute-start.19 = (bf16[4,288,256]{2,1,0:T(8,128)(2,1)S(1)}, bf16[4,288,256]{2,1,0:T(8,128)(2,1)S(1)}, u32[]{:S(2)}, u32[]{:S(2)}) collective-permute-start(bf16[4,288,256]{2,1,0:T(8,128)(2,1)S(1)} %get-tuple-element.138.h_ref), channel_id=1, source_target_pairs={{224,192},{225,193},{226,194},{227,195},{228,196},{229,197},{230,1... | collective-permute-start | bytes 1769480 | tf_op jit(solution)/shard_map/ppermute | solution.py:223
  199.3 35.6 %copy-start.4 = (bf16[4,288,256]{2,1,0:T(8,128)(2,1)S(1)}, bf16[4,288,256]{2,1,0:T(8,128)(2,1)}, u32[]{:S(2)}) copy-start(bf16[4,288,256]{2,1,0:T(8,128)(2,1)} %copy-done.3) | copy-start | bytes 1769476
  237.8 1.8 collective-permute-start.20
  (17 other events, 47.0 us)
where the time goes:
time: 255 us; the launch traced here: 254 us
  blocking collectives  77.3 us (30%)
  starting transfers between devices  72.9 us (29%)
  waiting for transfers between devices  45.3 us (18%)
  Pallas kernels  36 us (14%)
  local copies, waits for them, and re-layouts  16.4 us (6%)
  other arithmetic  5.23 us (2%)
    all_to_all x8, blocking collectives, stats(): part = lax.all_to_all(part, ROW, 0, 0, tiled=True)  64 us
    ppermute x21, starting transfers between devices, moved(): return lax.ppermute(value, axis, moves)  55.6 us
    ppermute x21, waiting for transfers between devices, moved(): return lax.ppermute(value, axis, moves)  34.4 us
    pallas_call x12, Pallas kernels, layer(): pl.pallas_call(functools.partial(layer_kernel, index, min(index, weights[...  32.3 us
    unnamed x49, local copies, waits for them, and re-layouts  14.3 us
    all_to_all x1, blocking collectives, program(): return lax.all_to_all(blocks, 'x', 0, 0, tiled=True)[None]  13.3 us
    all_to_all x3, starting transfers between devices, stats(): part = lax.all_to_all(part, ROW, 0, 0, tiled=True)  9.99 us
    all_to_all x3, waiting for transfers between devices, stats(): part = lax.all_to_all(part, ROW, 0, 0, tiled=True)  9 us
  transfers between devices with their start and end apart: 25, of which 5 were waited for; matrix products, arithmetic and copies ran while one was open for 2% of the time, Pallas kernels for 11%

commit v1 on v0

--- a/solution.py
+++ b/solution.py
@@ -213,7 +213,7 @@
         in_specs=[pl.BlockSpec(memory_space=pltpu.SMEM), hbm],
         out_specs=(hbm, hbm),
         scratch_shapes=[pltpu.VMEM((2, K // 2, C), jnp.bfloat16), pltpu.SemaphoreType.DMA((2,))],
-        compiler_params=pltpu.CompilerParams(vmem_limit_bytes=4 * 1024 * 1024),
+        compiler_params=pltpu.CompilerParams(vmem_limit_bytes=60 * 1024 * 1024),
         cost_estimate=pl.CostEstimate(flops=1000000, bytes_accessed=5000000, transcendentals=0),
         name="halves",
     )(where, weight)
@@ -242,7 +242,7 @@
     sent = jnp.broadcast_to(noisy[None, :, None], (NY, NX, NC, FR, 64)).reshape(NY * NX * NC, FR * 64)
     lifts = jnp.stack([lift, lift * lift])
     line = lax.all_to_all(sent, TM, 0, 0, tiled=True)
-    part = (jnp.stack([line.sum(), (line * line).sum()])[:, None] * lifts)[None]
+    part = (jnp.stack([line, line * line]).sum(axis=(1, 2))[:, None] * lifts)[None]
     line = line.reshape(NY * NX * NC, FR, 64).transpose(1, 0, 2).reshape(FR, -1)
     line = jnp.pad(line, ((0, 0), (HALO, HALO)))
     mine = lax.dynamic_slice_in_dim(line, place * OWN, ROWS, axis=1)
@@ -264,10 +264,11 @@
     own_p = jnp.concatenate(
         [norm_gain[0, 0:1], norm_bias[0, 0:1], norm_gain[0, 1:2], norm_bias[0, 1:2], temb, jnp.zeros((3, C), jnp.float32)]
     )
+    p2 = moved(own_p, [(2, 1), (6, 7)])
     p3 = moved(own_p, [(3, 1), (5, 7)])
     p4 = moved(own_p, [(4, 1)])
-    h, part, valid, own, own_p, p3, p4, where, core = lax.optimization_barrier(
-        (h, part, valid, own, own_p, p3, p4, where, core)
+    h, part, valid, own, own_p, p2, p3, p4, where, core = lax.optimization_barrier(
+        (h, part, valid, own, own_p, p2, p3, p4, where, core)
     )
 
     def run(index, last, h, part, p, weights):
@@ -280,19 +281,17 @@
 
     own_w = (own_w,)
     h, part = run(0, False, h, part, own_p, own_w)
-    part, half = lax.optimization_barrier((stats(part), half))
-    mid = moved(half, [(3, 1)])
-    h, part = run(1, True, h, part, own_p, own_w)
+    h, part = run(1, True, h, stats(part), own_p, own_w)
     ret0 = h
     part = moved(part, [(0, 1)])
     hopped = moved(h, [(0, 1)])
-    part, later_p, one = lax.optimization_barrier((stats(part), own_p, one))
-    p2 = moved(later_p, [(2, 1), (6, 7)])
+    part, half, one = lax.optimization_barrier((stats(part), half, one))
+    mid = moved(half, [(3, 1)])
     w4 = moved(one, [(4, 1)])
     w5 = moved(one, [(5, 7)])
     h, part = lax.optimization_barrier((hopped, part))
     h, part = run(0, False, h, part, own_p, own_w)
-    part, p2, near = stats(part, p2, near)
+    part, near = stats(part, near)
     part, near = lax.optimization_barrier((part, near))
     h, part = run(1, True, h, part, own_p, own_w)
     ret1 = h
@@ -300,24 +299,14 @@
     part, nears = stats(part, nears)
     near = (near, nears)
     h, part = run(0, False, h, part, p2, near)
-    part, mid = stats(part, mid)
-    part, mid = lax.optimization_barrier((part, mid))
-    h, part = run(1, True, h, part, p2, near)
+    h, part = run(1, True, h, stats(part), p2, near)
     ret2 = moved(h, [(1, 2)])
-    mids = swapped(mid)
-    part, mids = stats(part, mids)
-    mid = (mid, mids)
-    h, part = run(0, False, h, part, p3, mid)
-    part, w4 = stats(part, w4)
-    part, w4 = lax.optimization_barrier((part, w4))
-    h, part = run(1, True, h, part, p3, mid)
+    mid = (mid, swapped(mid))
+    h, part = run(0, False, h, stats(part), p3, mid)
+    h, part = run(1, True, h, stats(part), p3, mid)
     ret3 = moved(h, [(1, 3)])
-    w4s = swapped(w4)
-    part, w4s, w5 = stats(part, w4s, w5)
-    part, w5 = lax.optimization_barrier((part, w5))
-    h, part = run(0, True, h, part, p4, (w4, w4s))
+    h, part = run(0, True, h, stats(part), p4, (w4, swapped(w4)))
     w5s = swapped(w5)
-    part, w5s = lax.optimization_barrier((part, w5s))
     part = moved(part, [(1, 7)])
     ret4 = moved(h, [(1, 4)])
     h, part = lax.optimization_barrier((moved(h, [(1, 7)]), stats(part)))

time: 255 us -> 253 us (level)
  waiting for transfers between devices: 45.3 us -> 60.3 us
  starting transfers between devices: 72.9 us -> 60.4 us
  local copies, waits for them, and re-layouts: 16.4 us -> 12.2 us
    ppermute x21, waiting for transfers between devices: 34.4 us -> 49.3 us  [moved(): return lax.ppermute(value, axis, moves)]
    ppermute x21, starting transfers between devices: 55.6 us -> 43.1 us  [moved(): return lax.ppermute(value, axis, moves)]
    unnamed x49 -> x39, local copies, waits for them, and re-layouts: 14.3 us -> 10.1 us
  transfers between devices with their start and end apart: 25 -> 25, of which waited for: 5 -> 6; matrix products, arithmetic and copies ran while one was open for 2% -> 1% of each run, Pallas kernels for 11% -> 13%
where the time goes in v1:
time: 253 us; the launch traced here: 252 us
  blocking collectives  76.4 us (30%)
  starting transfers between devices  60.4 us (24%)
  waiting for transfers between devices  60.3 us (24%)
  Pallas kernels  37.8 us (15%)
  local copies, waits for them, and re-layouts  12.2 us (5%)
  other arithmetic  3.9 us (2%)
    all_to_all x8, blocking collectives, stats(): part = lax.all_to_all(part, ROW, 0, 0, tiled=True)  63.9 us
    ppermute x21, waiting for transfers between devices, moved(): return lax.ppermute(value, axis, moves)  49.3 us
    ppermute x21, starting transfers between devices, moved(): return lax.ppermute(value, axis, moves)  43.1 us
    pallas_call x12, Pallas kernels, layer(): pl.pallas_call(functools.partial(layer_kernel, index, min(index, weights[...  32.2 us
    all_to_all x1, blocking collectives, program(): return lax.all_to_all(blocks, 'x', 0, 0, tiled=True)[None]  12.5 us
    unnamed x39, local copies, waits for them, and re-layouts  10.1 us
    all_to_all x3, starting transfers between devices, stats(): part = lax.all_to_all(part, ROW, 0, 0, tiled=True)  10 us
    all_to_all x3, waiting for transfers between devices, stats(): part = lax.all_to_all(part, ROW, 0, 0, tiled=True)  9 us
  transfers between devices with their start and end apart: 25, of which 6 were waited for; matrix products, arithmetic and copies ran while one was open for 1% of the time, Pallas kernels for 13%

profile of v1, /device:TPU:128, one launch (start us, length us, event | category | flops | bytes accessed | tf_op | source)
XLA Modules:
  0.0 251.6 jit_solution(6411875132182529880)
XLA Ops:
  3.2 2.4 collective-permute-start.2
  7.8 7.3 %all-to-all-start = ((f32[32,1,256]{2,1,0:T(1,128)}), f32[32,1,256]{2,1,0:T(1,128)S(1)}, u32[]{:S(2)}, u32[]{:S(2)}) async-start(f32[32,1,256]{2,1,0:T(1,128)} %all_to_all.42), calls=%async_computation | async-start | bytes 65536 | tf_op jit(solution)/shard_map/all_to_all | solution.py:244
  15.8 2.7 %halves.1 = (bf16[2,1152,256]{2,1,0:T(8,128)(2,1)}, bf16[1,1152,256]{2,1,0:T(8,128)(2,1)}) custom-call(s32[2]{0:T(128)} %pad_add_fusion.where, bf16[2,2304,256]{2,1,0:T(8,128)(2,1)} %bitcast.21), custom_call_target="tpu_custom_call" | custom-call | flops 1000000 | bytes 5000000 | tf_op jit(solution)/shard_map/halves/pallas_call | solution.py:210
  23.8 2.3 layer.12
  26.1 7.8 %all_to_all.69.part_ref = f32[8,2,256]{2,1,0:T(2,128)S(1)} all-to-all(f32[8,2,256]{2,1,0:T(2,128)S(1)} %get-tuple-element.63), channel_id=1, replica_groups=mesh['z'=8,'y'=4,'x'=4,'c'=2] {'y','c'}, dimensions={0} | all-to-all | bytes 32768 | tf_op jit(solution)/shard_map/all_to_all | solution.py:279
  36.8 7.7 %all_to_all.70.part_ref = f32[8,2,256]{2,1,0:T(2,128)S(1)} all-to-all(f32[8,2,256]{2,1,0:T(2,128)S(1)} %collective-permute-done.4), channel_id=1, replica_groups=mesh['z'=8,'y'=4,'x'=4,'c'=2] {'y','c'}, dimensions={0} | all-to-all | bytes 32768 | tf_op jit(solution)/shard_map/all_to_all | solution.py:279
  47.1 2.3 layer.14
  49.4 7.7 %all_to_all.71.part_ref = f32[8,2,256]{2,1,0:T(2,128)S(1)} all-to-all(f32[8,2,256]{2,1,0:T(2,128)S(1)} %get-tuple-element.73), channel_id=1, replica_groups=mesh['z'=8,'y'=4,'x'=4,'c'=2] {'y','c'}, dimensions={0} | all-to-all | bytes 32768 | tf_op jit(solution)/shard_map/all_to_all | solution.py:279
  57.7 24.5 %collective-permute-start.11 = (bf16[1,1152,256]{2,1,0:T(8,128)(2,1)S(1)}, bf16[1,1152,256]{2,1,0:T(8,128)(2,1)}, u32[]{:S(2)}, u32[]{:S(2)}) collective-permute-start(bf16[1,1152,256]{2,1,0:T(8,128)(2,1)S(1)} %copy-done.18), channel_id=1, source_target_pairs={{128,32},{129,33},{130,34},{131,35},{132,36},{133,37},{134,38},{13... | collective-permute-start | bytes 1769480 | tf_op jit(solution)/shard_map/ppermute | solution.py:223
  82.1 12.4 %collective-permute-done.11.refs_0_ = bf16[1,1152,256]{2,1,0:T(8,128)(2,1)} collective-permute-done((bf16[1,1152,256]{2,1,0:T(8,128)(2,1)S(1)}, bf16[1,1152,256]{2,1,0:T(8,128)(2,1)}, u32[]{:S(2)}, u32[]{:S(2)}) %collective-permute-start.11) | collective-permute-done | bytes 589856 | tf_op jit(solution)/shard_map/ppermute | solution.py:223
  94.6 2.9 %layer.15 = (bf16[4,288,256]{2,1,0:T(8,128)(2,1)S(1)}, f32[8,2,256]{2,1,0:T(2,128)}) custom-call(s32[1]{0:T(128)} %bitcast.11.core, f32[4,288,256]{2,1,0:T(8,128)S(1)} %get-tuple-element.71.h_ref, f32[8,2,256]{2,1,0:T(2,128)S(1)} %all_to_all.71.part_ref, f32[8,256]{1,0:T(8,128)S(1)} %concatenate.21.par_ref, f32[288,128]{1,0:T(8,128)S(1)} %get-tuple-element.60.valid_ref, ...), custom_call_target="tpu_custom_call" | custom-call | flops 1200000000 | bytes 4000000 | tf_op jit(solution)/shard_map/layer/pallas_call | solution.py:123
  99.3 3.3 %all-to-all-start.4 = ((f32[8,2,256]{2,1,0:T(2,128)}), f32[8,2,256]{2,1,0:T(2,128)S(1)}, u32[]{:S(2)}, u32[]{:S(2)}) async-start(f32[8,2,256]{2,1,0:T(2,128)} %get-tuple-element.79), calls=%async_computation.4 | async-start | bytes 32768 | tf_op jit(solution)/shard_map/all_to_all | solution.py:279
  104.2 3.7 %all-to-all-done.4.part_ref = f32[8,2,256]{2,1,0:T(2,128)S(1)} async-done(((f32[8,2,256]{2,1,0:T(2,128)}), f32[8,2,256]{2,1,0:T(2,128)S(1)}, u32[]{:S(2)}, u32[]{:S(2)}) %all-to-all-start.4) | async-done | bytes 16416 | tf_op jit(solution)/shard_map/all_to_all | solution.py:279
  110.2 2.6 %layer.16 = (f32[4,288,256]{2,1,0:T(8,128)S(1)}, f32[8,2,256]{2,1,0:T(2,128)S(1)}) custom-call(s32[1]{0:T(128)} %bitcast.11.core, bf16[4,288,256]{2,1,0:T(8,128)(2,1)S(1)} %copy-done.3, f32[8,2,256]{2,1,0:T(2,128)S(1)} %all-to-all-done.4.part_ref, f32[8,256]{1,0:T(8,128)S(1)} %collective-permute-done.par_ref, f32[288,128]{1,0:T(8,128)S(1)} %get-tuple-element.60.valid_ref, ...), custom_call_target="tpu_custom_call" | custom-call | flops 1200000000 | bytes 4000000 | tf_op jit(solution)/shard_map/layer/pallas_call | solution.py:123
  112.8 7.7 %all_to_all.72.part_ref = f32[8,2,256]{2,1,0:T(2,128)S(1)} all-to-all(f32[8,2,256]{2,1,0:T(2,128)S(1)} %get-tuple-element.83), channel_id=1, replica_groups=mesh['z'=8,'y'=4,'x'=4,'c'=2] {'y','c'}, dimensions={0} | all-to-all | bytes 32768 | tf_op jit(solution)/shard_map/all_to_all | solution.py:279
  120.5 2.5 layer.17
  123.1 7.7 %all_to_all.73.part_ref = f32[8,2,256]{2,1,0:T(2,128)S(1)} all-to-all(f32[8,2,256]{2,1,0:T(2,128)S(1)} %get-tuple-element.85), channel_id=1, replica_groups=mesh['z'=8,'y'=4,'x'=4,'c'=2] {'y','c'}, dimensions={0} | all-to-all | bytes 32768 | tf_op jit(solution)/shard_map/all_to_all | solution.py:279
  130.8 2.7 %layer.18 = (f32[4,288,256]{2,1,0:T(8,128)S(1)}, f32[8,2,256]{2,1,0:T(2,128)S(1)}) custom-call(s32[1]{0:T(128)} %bitcast.11.core, bf16[4,288,256]{2,1,0:T(8,128)(2,1)S(1)} %get-tuple-element.84.h_ref, f32[8,2,256]{2,1,0:T(2,128)S(1)} %all_to_all.73.part_ref, f32[8,256]{1,0:T(8,128)S(1)} %collective-permute-done.1.par_ref, ...), custom_call_target="tpu_custom_call" | custom-call | flops 1200000000 | bytes 4000000 | tf_op jit(solution)/shard_map/layer/pallas_call | solution.py:123
  133.4 7.7 %all_to_all.74.part_ref = f32[8,2,256]{2,1,0:T(2,128)S(1)} all-to-all(f32[8,2,256]{2,1,0:T(2,128)S(1)} %get-tuple-element.89), channel_id=1, replica_groups=mesh['z'=8,'y'=4,'x'=4,'c'=2] {'y','c'}, dimensions={0} | all-to-all | bytes 32768 | tf_op jit(solution)/shard_map/all_to_all | solution.py:279
  141.2 3.3 %layer.19 = (bf16[4,288,256]{2,1,0:T(8,128)(2,1)S(1)}, f32[8,2,256]{2,1,0:T(2,128)}) custom-call(s32[1]{0:T(128)} %bitcast.11.core, f32[4,288,256]{2,1,0:T(8,128)S(1)} %get-tuple-element.88.h_ref, f32[8,2,256]{2,1,0:T(2,128)S(1)} %all_to_all.74.part_ref, f32[8,256]{1,0:T(8,128)S(1)} %collective-permute-done.1.par_ref, ...), custom_call_target="tpu_custom_call" | custom-call | flops 1200000000 | bytes 4000000 | tf_op jit(solution)/shard_map/layer/pallas_call | solution.py:123
  145.3 3.3 %all-to-all-start.8 = ((f32[8,2,256]{2,1,0:T(2,128)}), f32[8,2,256]{2,1,0:T(2,128)S(1)}, u32[]{:S(2)}, u32[]{:S(2)}) async-start(f32[8,2,256]{2,1,0:T(2,128)} %get-tuple-element.91), calls=%async_computation.8 | async-start | bytes 32768 | tf_op jit(solution)/shard_map/all_to_all | solution.py:279
  148.7 5.3 %all-to-all-done.8.part_ref = f32[8,2,256]{2,1,0:T(2,128)S(1)} async-done(((f32[8,2,256]{2,1,0:T(2,128)}), f32[8,2,256]{2,1,0:T(2,128)S(1)}, u32[]{:S(2)}, u32[]{:S(2)}) %all-to-all-start.8) | async-done | bytes 16416 | tf_op jit(solution)/shard_map/all_to_all | solution.py:279
  155.0 2.7 %layer.20 = (bf16[4,288,256]{2,1,0:T(8,128)(2,1)S(1)}, f32[8,2,256]{2,1,0:T(2,128)S(1)}) custom-call(s32[1]{0:T(128)} %bitcast.11.core, bf16[4,288,256]{2,1,0:T(8,128)(2,1)S(1)} %copy-done.12, f32[8,2,256]{2,1,0:T(2,128)S(1)} %all-to-all-done.8.part_ref, f32[8,256]{1,0:T(8,128)S(1)} %collective-permute-done.2.par_ref, ...), custom_call_target="tpu_custom_call" | custom-call | flops 1200000000 | bytes 4000000 | tf_op jit(solution)/shard_map/layer/pallas_call | solution.py:123
  159.2 7.7 %all_to_all.75.part_ref = f32[8,2,256]{2,1,0:T(2,128)S(1)} all-to-all(f32[8,2,256]{2,1,0:T(2,128)S(1)} %collective-permute-done.15), channel_id=1, replica_groups=mesh['z'=8,'y'=4,'x'=4,'c'=2] {'y','c'}, dimensions={0} | all-to-all | bytes 32768 | tf_op jit(solution)/shard_map/all_to_all | solution.py:279
  167.0 3.1 %layer.21 = (bf16[4,288,256]{2,1,0:T(8,128)(2,1)S(1)}, f32[8,2,256]{2,1,0:T(2,128)}) custom-call(s32[1]{0:T(128)} %bitcast.11.core, bf16[4,288,256]{2,1,0:T(8,128)(2,1)S(1)} %collective-permute-done.14.h_ref, f32[8,2,256]{2,1,0:T(2,128)S(1)} %all_to_all.75.part_ref, f32[8,256]{1,0:T(8,128)S(1)} %collective-permute-done.1.par_ref, ...), custom_call_target="tpu_custom_call" | custom-call | flops 1200000000 | bytes 4000000 | tf_op jit(solution)/shard_map/layer/pallas_call | solution.py:123
  170.9 3.3 %all-to-all-start.10 = ((f32[8,2,256]{2,1,0:T(2,128)}), f32[8,2,256]{2,1,0:T(2,128)S(1)}, u32[]{:S(2)}, u32[]{:S(2)}) async-start(f32[8,2,256]{2,1,0:T(2,128)} %get-tuple-element.99), calls=%async_computation.10 | async-start | bytes 32768 | tf_op jit(solution)/shard_map/all_to_all | solution.py:279
  182.4 2.5 layer.22
  185.6 9.9 %all_to_all.76.part_ref = f32[8,2,256]{2,1,0:T(2,128)S(1)} all-to-all(f32[8,2,256]{2,1,0:T(2,128)S(1)} %get-tuple-element.101), channel_id=1, replica_groups=mesh['z'=8,'y'=4,'x'=4,'c'=2] {'y','c'}, dimensions={0} | all-to-all | bytes 32768 | tf_op jit(solution)/shard_map/all_to_all | solution.py:279
  195.5 3.0 %layer.23 = (bf16[4,288,256]{2,1,0:T(8,128)(2,1)S(1)}, f32[8,2,256]{2,1,0:T(2,128)}) custom-call(s32[1]{0:T(128)} %bitcast.11.core, bf16[4,288,256]{2,1,0:T(8,128)(2,1)S(1)} %get-tuple-element.100.h_ref, f32[8,2,256]{2,1,0:T(2,128)S(1)} %all_to_all.76.part_ref, f32[8,256]{1,0:T(8,128)S(1)} %concatenate.21.par_ref, ...), custom_call_target="tpu_custom_call" | custom-call | flops 1200000000 | bytes 4000000 | tf_op jit(solution)/shard_map/layer/pallas_call | solution.py:123
  198.5 35.1 %collective-permute-done.13.refs_4_ = bf16[4,288,256]{2,1,0:T(8,128)(2,1)} collective-permute-done((bf16[4,288,256]{2,1,0:T(8,128)(2,1)}, bf16[4,288,256]{2,1,0:T(8,128)(2,1)}, u32[]{:S(2)}, u32[]{:S(2)}) %collective-permute-start.13) | collective-permute-done | bytes 589856 | tf_op jit(solution)/shard_map/ppermute | solution.py:223
  233.6 2.9 %ordered.1 = (bf16[2,4,64,256]{3,2,1,0:T(8,128)(2,1)S(1)}, bf16[2,4,64,256]{3,2,1,0:T(8,128)(2,1)}) custom-call(s32[2]{0:T(128)S(1)} %copy-done.5, bf16[4,288,256]{2,1,0:T(8,128)(2,1)S(1)} %get-tuple-element.64.refs_0_, bf16[4,288,256]{2,1,0:T(8,128)(2,1)S(1)} %copy-done.4, bf16[4,288,256]{2,1,0:T(8,128)(2,1)} %collective-permute-done.7.refs_2_, ...), custom_call_target="tpu_custom_call" | custom-call | flops 2000000 | bytes 2000000 | tf_op jit(solution)/shard_map/ordered/pallas_call | solution.py:165
  238.4 12.5 %all_to_all.77 = bf16[4,4,64,256]{3,2,1,0:T(8,128)(2,1)S(1)} all-to-all(bf16[4,4,64,256]{3,2,1,0:T(8,128)(2,1)S(1)} %maximum_select_fusion), channel_id=1, replica_groups=mesh['z'=8,'y'=4,'x'=4,'c'=2] {'x'}, dimensions={0} | all-to-all | bytes 1048576 | tf_op jit(solution)/shard_map/all_to_all | solution.py:323
  (111 shorter events, 38.6 us)
Async XLA Ops:
  1.9 21.9 %collective-permute-start = (f32[8,256]{1,0:T(8,128)S(1)}, f32[8,256]{1,0:T(8,128)S(1)}, u32[]{:S(2)}, u32[]{:S(2)}) collective-permute-start(f32[8,256]{1,0:T(8,128)S(1)} %concatenate.21.par_ref), channel_id=1, source_target_pairs={{64,32},{192,224},{65,33},{193,225},{66,34},{194,226},{67,35},{195... | collective-permute-start | bytes 24584 | tf_op jit(solution)/shard_map/ppermute | solution.py:223
  2.5 21.2 %collective-permute-start.1 = (f32[8,256]{1,0:T(8,128)S(1)}, f32[8,256]{1,0:T(8,128)S(1)}, u32[]{:S(2)}, u32[]{:S(2)}) collective-permute-start(f32[8,256]{1,0:T(8,128)S(1)} %concatenate.21.par_ref), channel_id=1, source_target_pairs={{96,32},{160,224},{97,33},{161,225},{98,34},{162,226},{99,35},{163... | collective-permute-start | bytes 24584 | tf_op jit(solution)/shard_map/ppermute | solution.py:223
  3.2 20.5 %collective-permute-start.2 = (f32[8,256]{1,0:T(8,128)S(1)}, f32[8,256]{1,0:T(8,128)S(1)}, u32[]{:S(2)}, u32[]{:S(2)}) collective-permute-start(f32[8,256]{1,0:T(8,128)S(1)} %concatenate.21.par_ref), channel_id=1, source_target_pairs={{128,32},{129,33},{130,34},{131,35},{132,36},{133,37},{134,38},{13... | collective-permute-start | bytes 24584 | tf_op jit(solution)/shard_map/ppermute | solution.py:223
  7.8 14.7 %all-to-all-start = ((f32[32,1,256]{2,1,0:T(1,128)}), f32[32,1,256]{2,1,0:T(1,128)S(1)}, u32[]{:S(2)}, u32[]{:S(2)}) async-start(f32[32,1,256]{2,1,0:T(1,128)} %all_to_all.42), calls=%async_computation | async-start | bytes 65536 | tf_op jit(solution)/shard_map/all_to_all | solution.py:244
  15.8 8.0 %copy-start.1 = (bf16[1,2,3,3,256,256]{5,4,3,2,1,0:T(8,128)(2,1)S(1)}, bf16[1,2,3,3,256,256]{5,4,3,2,1,0:T(8,128)(2,1)}, u32[]{:S(2)}) copy-start(bf16[1,2,3,3,256,256]{5,4,3,2,1,0:T(8,128)(2,1)} %param.14) | copy-start | bytes 7077892
  18.5 30.9 %collective-permute-start.5 = (bf16[2,1152,256]{2,1,0:T(8,128)(2,1)}, bf16[2,1152,256]{2,1,0:T(8,128)(2,1)}, u32[]{:S(2)}, u32[]{:S(2)}) collective-permute-start(bf16[2,1152,256]{2,1,0:T(8,128)(2,1)} %get-tuple-element.87), channel_id=1, source_target_pairs={{64,32},{192,224},{65,33},{193,225},{66,34},{194,226},{67,35},{195... | collective-permute-start | bytes 3538952 | tf_op jit(solution)/shard_map/ppermute | solution.py:223
  33.9 10.7 %copy-start.17 = (bf16[2,1152,256]{2,1,0:T(8,128)(2,1)S(1)}, bf16[2,1152,256]{2,1,0:T(8,128)(2,1)}, u32[]{:S(2)}) copy-start(bf16[2,1152,256]{2,1,0:T(8,128)(2,1)} %get-tuple-element.87) | copy-start | bytes 3538948
  36.2 0.7 collective-permute-start.4
  44.6 12.6 %collective-permute-start.8 = (bf16[2,1152,256]{2,1,0:T(8,128)(2,1)S(1)}, bf16[2,1152,256]{2,1,0:T(8,128)(2,1)}, u32[]{:S(2)}, u32[]{:S(2)}) collective-permute-start(bf16[2,1152,256]{2,1,0:T(8,128)(2,1)S(1)} %copy-done.17), channel_id=1, source_target_pairs={{96,32},{97,33},{98,34},{99,35},{100,36},{101,37},{102,38},{103,39... | collective-permute-start | bytes 3538952 | tf_op jit(solution)/shard_map/ppermute | solution.py:223
  46.2 11.4 %copy-start.18 = (bf16[1,1152,256]{2,1,0:T(8,128)(2,1)S(1)}, bf16[1,1152,256]{2,1,0:T(8,128)(2,1)}, u32[]{:S(2)}) copy-start(bf16[1,1152,256]{2,1,0:T(8,128)(2,1)} %get-tuple-element.93) | copy-start | bytes 1769476
  46.2 0.8 collective-permute-start.3
  57.2 41.1 %collective-permute-start.6 = (bf16[2,1152,256]{2,1,0:T(8,128)(2,1)}, bf16[2,1152,256]{2,1,0:T(8,128)(2,1)S(1)}, u32[]{:S(2)}, u32[]{:S(2)}) collective-permute-start(bf16[2,1152,256]{2,1,0:T(8,128)(2,1)} %collective-permute-done.5.refs_0_), channel_id=1, source_target_pairs={{0,1},{1,0},{2,3},{3,2},{4,5},{5,4},{6,7},{7,6},{8,9},{9,8},{10,11... | collective-permute-start | bytes 3538952 | tf_op jit(solution)/shard_map/ppermute | solution.py:223
  57.2 73.6 %collective-permute-start.9 = (bf16[2,1152,256]{2,1,0:T(8,128)(2,1)}, bf16[2,1152,256]{2,1,0:T(8,128)(2,1)}, u32[]{:S(2)}, u32[]{:S(2)}) collective-permute-start(bf16[2,1152,256]{2,1,0:T(8,128)(2,1)} %collective-permute-done.8.refs_0_), channel_id=1, source_target_pairs={{0,1},{1,0},{2,3},{3,2},{4,5},{5,4},{6,7},{7,6},{8,9},{9,8},{10,11... | collective-permute-start | bytes 3538952 | tf_op jit(solution)/shard_map/ppermute | solution.py:223
  57.7 36.9 %collective-permute-start.11 = (bf16[1,1152,256]{2,1,0:T(8,128)(2,1)S(1)}, bf16[1,1152,256]{2,1,0:T(8,128)(2,1)}, u32[]{:S(2)}, u32[]{:S(2)}) collective-permute-start(bf16[1,1152,256]{2,1,0:T(8,128)(2,1)S(1)} %copy-done.18), channel_id=1, source_target_pairs={{128,32},{129,33},{130,34},{131,35},{132,36},{133,37},{134,38},{13... | collective-permute-start | bytes 1769480 | tf_op jit(solution)/shard_map/ppermute | solution.py:223
  94.6 54.1 %collective-permute-start.12 = (bf16[1,1152,256]{2,1,0:T(8,128)(2,1)}, bf16[1,1152,256]{2,1,0:T(8,128)(2,1)}, u32[]{:S(2)}, u32[]{:S(2)}) collective-permute-start(bf16[1,1152,256]{2,1,0:T(8,128)(2,1)} %collective-permute-done.11.refs_0_), channel_id=1, source_target_pairs={{0,1},{1,0},{2,3},{3,2},{4,5},{5,4},{6,7},{7,6},{8,9},{9,8},{10,11... | collective-permute-start | bytes 1769480 | tf_op jit(solution)/shard_map/ppermute | solution.py:223
  99.3 8.6 %all-to-all-start.4 = ((f32[8,2,256]{2,1,0:T(2,128)}), f32[8,2,256]{2,1,0:T(2,128)S(1)}, u32[]{:S(2)}, u32[]{:S(2)}) async-start(f32[8,2,256]{2,1,0:T(2,128)} %get-tuple-element.79), calls=%async_computation.4 | async-start | bytes 32768 | tf_op jit(solution)/shard_map/all_to_all | solution.py:279
  102.6 55.8 %collective-permute-start.16 = (bf16[1,1152,256]{2,1,0:T(8,128)(2,1)}, bf16[1,1152,256]{2,1,0:T(8,128)(2,1)}, u32[]{:S(2)}, u32[]{:S(2)}) collective-permute-start(bf16[1,1152,256]{2,1,0:T(8,128)(2,1)} %get-tuple-element.93), channel_id=1, source_target_pairs={{160,224},{161,225},{162,226},{163,227},{164,228},{165,229},{166,2... | collective-permute-start | bytes 1769480 | tf_op jit(solution)/shard_map/ppermute | solution.py:223
  110.2 10.3 %copy-start.8 = (bf16[2,1152,256]{2,1,0:T(8,128)(2,1)S(1)}, bf16[2,1152,256]{2,1,0:T(8,128)(2,1)}, u32[]{:S(2)}) copy-start(bf16[2,1152,256]{2,1,0:T(8,128)(2,1)} %copy-done.6) | copy-start | bytes 3538948
  123.0 10.4 %copy-start.10 = (bf16[4,288,256]{2,1,0:T(8,128)(2,1)}, bf16[4,288,256]{2,1,0:T(8,128)(2,1)S(1)}, u32[]{:S(2)}) copy-start(bf16[4,288,256]{2,1,0:T(8,128)(2,1)S(1)} %get-tuple-element.84.h_ref) | copy-start | bytes 1769476
  145.3 8.6 %all-to-all-start.8 = ((f32[8,2,256]{2,1,0:T(2,128)}), f32[8,2,256]{2,1,0:T(2,128)S(1)}, u32[]{:S(2)}, u32[]{:S(2)}) async-start(f32[8,2,256]{2,1,0:T(2,128)} %get-tuple-element.91), calls=%async_computation.8 | async-start | bytes 32768 | tf_op jit(solution)/shard_map/all_to_all | solution.py:279
  157.7 9.2 %collective-permute-start.14 = (bf16[4,288,256]{2,1,0:T(8,128)(2,1)S(1)}, bf16[4,288,256]{2,1,0:T(8,128)(2,1)S(1)}, u32[]{:S(2)}, u32[]{:S(2)}) collective-permute-start(bf16[4,288,256]{2,1,0:T(8,128)(2,1)S(1)} %get-tuple-element.94), channel_id=1, source_target_pairs={{32,224},{33,225},{34,226},{35,227},{36,228},{37,229},{38,230},{39... | collective-permute-start | bytes 1769480 | tf_op jit(solution)/shard_map/ppermute | solution.py:223
  158.4 8.5 %collective-permute-start.17 = (bf16[1,1152,256]{2,1,0:T(8,128)(2,1)}, bf16[1,1152,256]{2,1,0:T(8,128)(2,1)S(1)}, u32[]{:S(2)}, u32[]{:S(2)}) collective-permute-start(bf16[1,1152,256]{2,1,0:T(8,128)(2,1)} %collective-permute-done.16.refs_0_), channel_id=1, source_target_pairs={{0,1},{1,0},{2,3},{3,2},{4,5},{5,4},{6,7},{7,6},{8,9},{9,8},{10,11... | collective-permute-start | bytes 1769480 | tf_op jit(solution)/shard_map/ppermute | solution.py:223
  158.5 0.7 collective-permute-start.15
  170.9 9.1 %all-to-all-start.10 = ((f32[8,2,256]{2,1,0:T(2,128)}), f32[8,2,256]{2,1,0:T(2,128)S(1)}, u32[]{:S(2)}, u32[]{:S(2)}) async-start(f32[8,2,256]{2,1,0:T(2,128)} %get-tuple-element.99), calls=%async_computation.10 | async-start | bytes 32768 | tf_op jit(solution)/shard_map/all_to_all | solution.py:279
  174.3 24.2 %collective-permute-start.7 = (bf16[4,288,256]{2,1,0:T(8,128)(2,1)}, bf16[4,288,256]{2,1,0:T(8,128)(2,1)}, u32[]{:S(2)}, u32[]{:S(2)}) collective-permute-start(bf16[4,288,256]{2,1,0:T(8,128)(2,1)} %copy-done.10), channel_id=1, source_target_pairs={{32,64},{33,65},{34,66},{35,67},{36,68},{37,69},{38,70},{39,71},{4... | collective-permute-start | bytes 1769480 | tf_op jit(solution)/shard_map/ppermute | solution.py:223
  175.8 22.7 %collective-permute-start.10 = (bf16[4,288,256]{2,1,0:T(8,128)(2,1)}, bf16[4,288,256]{2,1,0:T(8,128)(2,1)}, u32[]{:S(2)}, u32[]{:S(2)}) collective-permute-start(bf16[4,288,256]{2,1,0:T(8,128)(2,1)} %copy-done.11), channel_id=1, source_target_pairs={{32,96},{33,97},{34,98},{35,99},{36,100},{37,101},{38,102},{39,103... | collective-permute-start | bytes 1769480 | tf_op jit(solution)/shard_map/ppermute | solution.py:223
  177.3 56.3 %collective-permute-start.13 = (bf16[4,288,256]{2,1,0:T(8,128)(2,1)}, bf16[4,288,256]{2,1,0:T(8,128)(2,1)}, u32[]{:S(2)}, u32[]{:S(2)}) collective-permute-start(bf16[4,288,256]{2,1,0:T(8,128)(2,1)} %copy-done.13), channel_id=1, source_target_pairs={{32,128},{33,129},{34,130},{35,131},{36,132},{37,133},{38,134},{39... | collective-permute-start | bytes 1769480 | tf_op jit(solution)/shard_map/ppermute | solution.py:223
  178.5 55.0 %collective-permute-start.18 = (bf16[4,288,256]{2,1,0:T(8,128)(2,1)}, bf16[4,288,256]{2,1,0:T(8,128)(2,1)}, u32[]{:S(2)}, u32[]{:S(2)}) collective-permute-start(bf16[4,288,256]{2,1,0:T(8,128)(2,1)} %copy-done.14), channel_id=1, source_target_pairs={{224,160},{225,161},{226,162},{227,163},{228,164},{229,165},{230,1... | collective-permute-start | bytes 1769480 | tf_op jit(solution)/shard_map/ppermute | solution.py:223
  184.9 48.7 %collective-permute-start.19 = (bf16[4,288,256]{2,1,0:T(8,128)(2,1)S(1)}, bf16[4,288,256]{2,1,0:T(8,128)(2,1)S(1)}, u32[]{:S(2)}, u32[]{:S(2)}) collective-permute-start(bf16[4,288,256]{2,1,0:T(8,128)(2,1)S(1)} %get-tuple-element.100.h_ref), channel_id=1, source_target_pairs={{224,192},{225,193},{226,194},{227,195},{228,196},{229,197},{230,1... | collective-permute-start | bytes 1769480 | tf_op jit(solution)/shard_map/ppermute | solution.py:223
  195.5 38.1 %copy-start.4 = (bf16[4,288,256]{2,1,0:T(8,128)(2,1)S(1)}, bf16[4,288,256]{2,1,0:T(8,128)(2,1)}, u32[]{:S(2)}) copy-start(bf16[4,288,256]{2,1,0:T(8,128)(2,1)} %copy-done.2) | copy-start | bytes 1769476
  195.5 38.1 %copy-start.5 = (s32[2]{0:T(128)S(1)}, s32[2]{0:T(128)}, u32[]{:S(2)}) copy-start(s32[2]{0:T(128)} %pad_add_fusion.where) | copy-start | bytes 28
  236.5 1.8 collective-permute-start.20
  (12 other events, 16.5 us)

commit v2 on v1

--- a/solution.py
+++ b/solution.py
@@ -34,7 +34,7 @@
     return x
 
 
-def layer_kernel(index, slot, first, last, split, core, h_ref, part_ref, par_ref, valid_ref, own_ref, *refs):
+def layer_kernel(index, slot, base, first, last, split, core, h_ref, part_ref, par_ref, valid_ref, own_ref, *refs):
     weights, rest = refs[: 1 + split], refs[1 + split :]
     out_ref, sums_ref = rest[:2]
     act, w_ref, sem = rest[2:]
@@ -51,7 +51,7 @@
         fetch.start()
     sums = jnp.sum(part_ref[...], axis=0)
     total, square = sums[0:1], sums[1:2]
-    gain, bias, temb = par_ref[2 * index : 2 * index + 1], par_ref[2 * index + 1 : 2 * index + 2], par_ref[4:5]
+    gain, bias, temb = (par_ref[base + r : base + r + 1] for r in (2 * index, 2 * index + 1, 4))
     if first:
         square = square + 2.0 * temb * total + POSITIONS * temb * temb
         total = total + POSITIONS * temb
@@ -113,7 +113,7 @@
         sums_ref[n] = sums
 
 
-def layer(index, first, last, core, h, part, par, valid, own, weights):
+def layer(index, base, first, last, core, h, part, par, valid, own, weights):
     vmem = pl.BlockSpec(memory_space=pltpu.VMEM)
     hbm = pl.BlockSpec(memory_space=pltpu.HBM)
     out_shape = [
@@ -121,7 +121,7 @@
         jax.ShapeDtypeStruct((NY * NC, 2, C), jnp.float32),
     ]
     return pl.pallas_call(
-        functools.partial(layer_kernel, index, min(index, weights[0].shape[0] - 1), first, last, len(weights) - 1),
+        functools.partial(layer_kernel, index, min(index, weights[0].shape[0] - 1), base, first, last, len(weights) - 1),
         out_shape=tuple(out_shape),
         in_specs=[pl.BlockSpec(memory_space=pltpu.SMEM)] + [vmem] * 5 + [hbm] * len(weights),
         out_specs=(vmem, vmem),
@@ -136,17 +136,17 @@
     )(core, h, part, par, valid, own, *weights)
 
 
-def ordered_kernel(where, *refs):
+def ordered_kernel(plane, half, *refs):
     sources, (keep_ref, send_ref, x_ref, wide, line, sem) = refs[:NZ], refs[NZ:]
     for z in range(NZ):
 
-        @pl.when(where[0] == z)
+        @pl.when(plane[0] == z)
         def _():
             copy = pltpu.make_async_copy(sources[z], x_ref, sem)
             copy.start()
             copy.wait()
 
-    core = where[1]
+    core = half[0]
     for f in range(FR):
         for lane in range(0, C, 128):
             wide[...] = x_ref[f, :, lane : lane + 128].astype(jnp.float32)
@@ -159,13 +159,13 @@
                 send_ref[k, f, :, lane : lane + 128] = line[pl.ds(lo, 64)].astype(jnp.bfloat16)
 
 
-def ordered(where, sources):
+def ordered(plane, core, sources):
     vmem = pl.BlockSpec(memory_space=pltpu.VMEM)
     half = jax.ShapeDtypeStruct((2, FR, 64, C), jnp.bfloat16)
     return pl.pallas_call(
         ordered_kernel,
         out_shape=(half, half),
-        in_specs=[pl.BlockSpec(memory_space=pltpu.SMEM)] + [pl.BlockSpec(memory_space=pl.ANY)] * NZ,
+        in_specs=[pl.BlockSpec(memory_space=pltpu.SMEM)] * 2 + [pl.BlockSpec(memory_space=pl.ANY)] * NZ,
         out_specs=(vmem, vmem),
         scratch_shapes=[
             pltpu.VMEM((FR, ROWS, C), jnp.bfloat16),
@@ -176,47 +176,50 @@
         compiler_params=pltpu.CompilerParams(vmem_limit_bytes=8 * 1024 * 1024),
         cost_estimate=pl.CostEstimate(flops=2000000, bytes_accessed=2000000, transcendentals=0),
         name="ordered",
-    )(where, *sources)
-
-
-def halves_kernel(where, w_hbm, two_hbm, one_hbm, held, sem):
+    )(plane, core, *sources)
+
+
+def halves_kernel(plane, half, w_hbm, two_hbm, one_hbm, held, sem):
     size = K // 2
-    z, core = where[0], where[1]
+    z, core = plane[0], half[0]
     rows = pl.ds(pl.multiple_of(core * size, size), size)
 
-    def carry(index, target):
-        take = pltpu.make_async_copy(w_hbm.at[index, rows], held.at[index], sem.at[index])
-        take.start()
-        take.wait()
-        give = pltpu.make_async_copy(held.at[index], target.at[index], sem.at[index])
-        give.start()
-        give.wait()
-
-    @pl.when((z == 2) | (z == 3) | (z == 6))
-    def _():
-        carry(0, two_hbm)
+    def carry(layers, target):
+        takes = [pltpu.make_async_copy(w_hbm.at[i, rows], held.at[i], sem.at[i]) for i in range(layers)]
+        gives = [pltpu.make_async_copy(held.at[i], target.at[i], sem.at[2 + i]) for i in range(layers)]
+        for take in takes:
+            take.start()
+        for take, give in zip(takes, gives):
+            take.wait()
+            give.start()
+        for give in gives:
+            give.wait()
 
     @pl.when((z == 2) | (z == 3))
     def _():
+        carry(2, two_hbm)
+
+    @pl.when(z == 6)
+    def _():
         carry(1, two_hbm)
 
     @pl.when((z == 4) | (z == 5))
     def _():
-        carry(0, one_hbm)
-
-
-def halves(where, weight):
+        carry(1, one_hbm)
+
+
+def halves(plane, core, weight):
     hbm = pl.BlockSpec(memory_space=pltpu.HBM)
     return pl.pallas_call(
         halves_kernel,
         out_shape=tuple(jax.ShapeDtypeStruct((n, K // 2, C), jnp.bfloat16) for n in (2, 1)),
-        in_specs=[pl.BlockSpec(memory_space=pltpu.SMEM), hbm],
+        in_specs=[pl.BlockSpec(memory_space=pltpu.SMEM)] * 2 + [hbm],
         out_specs=(hbm, hbm),
-        scratch_shapes=[pltpu.VMEM((2, K // 2, C), jnp.bfloat16), pltpu.SemaphoreType.DMA((2,))],
+        scratch_shapes=[pltpu.VMEM((2, K // 2, C), jnp.bfloat16), pltpu.SemaphoreType.DMA((4,))],
         compiler_params=pltpu.CompilerParams(vmem_limit_bytes=60 * 1024 * 1024),
         cost_estimate=pl.CostEstimate(flops=1000000, bytes_accessed=5000000, transcendentals=0),
         name="halves",
-    )(where, weight)
+    )(plane, core, weight)
 
 
 def moved(value, moves, axis="z"):
@@ -232,8 +235,8 @@
     place = 2 * y + c
     core = c.reshape(1).astype(jnp.int32)
     own_w = conv_weight[0].reshape(2, K, C)
-    where = jnp.stack([z, c]).astype(jnp.int32)
-    half, one = halves(where, own_w)
+    plane = z.reshape(1).astype(jnp.int32)
+    half, one = halves(plane, core, own_w)
     near = moved(half, [(2, 1), (6, 7)])
 
     steps_f = timestep.astype(jnp.float32)
@@ -264,15 +267,11 @@
     own_p = jnp.concatenate(
         [norm_gain[0, 0:1], norm_bias[0, 0:1], norm_gain[0, 1:2], norm_bias[0, 1:2], temb, jnp.zeros((3, C), jnp.float32)]
     )
-    p2 = moved(own_p, [(2, 1), (6, 7)])
-    p3 = moved(own_p, [(3, 1), (5, 7)])
-    p4 = moved(own_p, [(4, 1)])
-    h, part, valid, own, own_p, p2, p3, p4, where, core = lax.optimization_barrier(
-        (h, part, valid, own, own_p, p2, p3, p4, where, core)
-    )
-
-    def run(index, last, h, part, p, weights):
-        return layer(index, index == 0, last, core, h, part, p, valid, own, weights)
+    p2 = moved(own_p, [(2, 1), (6, 7), (4, 3)])
+    h, part, valid, own, own_p, core = lax.optimization_barrier((h, part, valid, own, own_p, core))
+
+    def run(index, last, h, part, p, weights, base=0):
+        return layer(index, base, index == 0, last, core, h, part, p, valid, own, weights)
 
     def stats(part, *settled):
         part, *settled = lax.optimization_barrier((part, *settled))
@@ -283,33 +282,35 @@
     h, part = run(0, False, h, part, own_p, own_w)
     h, part = run(1, True, h, stats(part), own_p, own_w)
     ret0 = h
+    hopped = moved(h, [(0, 1)])
+    part, p2 = stats(part, p2)
+    part, half, sent_p = lax.optimization_barrier((part, half, own_p))
     part = moved(part, [(0, 1)])
-    hopped = moved(h, [(0, 1)])
-    part, half, one = lax.optimization_barrier((stats(part), half, one))
+    p3 = moved(jnp.concatenate([sent_p, p2]), [(3, 1), (5, 7)])
     mid = moved(half, [(3, 1)])
+    h, part = lax.optimization_barrier((hopped, part))
+    h, part = run(0, False, h, part, own_p, own_w)
+    h, part = run(1, True, h, stats(part), own_p, own_w)
+    ret1 = h
+    near = (near, swapped(near))
+    part = stats(part)
+    part, one = lax.optimization_barrier((part, one))
     w4 = moved(one, [(4, 1)])
     w5 = moved(one, [(5, 7)])
-    h, part = lax.optimization_barrier((hopped, part))
-    h, part = run(0, False, h, part, own_p, own_w)
-    part, near = stats(part, near)
-    part, near = lax.optimization_barrier((part, near))
-    h, part = run(1, True, h, part, own_p, own_w)
-    ret1 = h
-    nears = swapped(near)
-    part, nears = stats(part, nears)
-    near = (near, nears)
     h, part = run(0, False, h, part, p2, near)
     h, part = run(1, True, h, stats(part), p2, near)
     ret2 = moved(h, [(1, 2)])
     mid = (mid, swapped(mid))
-    h, part = run(0, False, h, stats(part), p3, mid)
+    part, p3 = stats(part, p3)
+    h, part = run(0, False, h, part, p3, mid)
     h, part = run(1, True, h, stats(part), p3, mid)
     ret3 = moved(h, [(1, 3)])
-    h, part = run(0, True, h, stats(part), p4, (w4, swapped(w4)))
+    h, part = run(0, True, h, stats(part), p3, (w4, swapped(w4)), 8)
     w5s = swapped(w5)
-    part = moved(part, [(1, 7)])
+    hopped = moved(h, [(1, 7)])
+    part = moved(stats(part), [(1, 7)])
     ret4 = moved(h, [(1, 4)])
-    h, part = lax.optimization_barrier((moved(h, [(1, 7)]), stats(part)))
+    h, part = lax.optimization_barrier((hopped, part))
     h, part = run(0, True, h, part, p3, (w5, w5s))
     ret5 = moved(h, [(7, 5)])
     h, part = run(0, True, h, stats(part), p2, near)
@@ -317,7 +318,7 @@
     h, part = run(0, True, h, stats(part), own_p, own_w)
     ret7 = h
 
-    keep, send = ordered(where, [ret0, ret1, ret2, ret3, ret4, ret5, ret6, ret7])
+    keep, send = ordered(plane, core, [ret0, ret1, ret2, ret3, ret4, ret5, ret6, ret7])
     got = swapped(send)
     blocks = jnp.where(c == 0, jnp.concatenate([keep, got]), jnp.concatenate([got, keep]))
     return lax.all_to_all(blocks, "x", 0, 0, tiled=True)[None]

time: 253 us -> 258 us (1.020)
  starting transfers between devices: 60.4 us -> 76.8 us
  blocking collectives: 76.4 us -> 70 us
  waiting for transfers between devices: 60.3 us -> 55.3 us
    ppermute x21 -> x20, starting transfers between devices: 43.1 us -> 56 us  [moved(): return lax.ppermute(value, axis, moves)]
    ppermute x21 -> x20, waiting for transfers between devices: 49.3 us -> 39.6 us  [moved(): return lax.ppermute(value, axis, moves)]
    all_to_all x8 -> x7, blocking collectives: 63.9 us -> 56.2 us  [stats(): part = lax.all_to_all(part, ROW, 0, 0, tiled=True)]
    all_to_all x3 -> x4, waiting for transfers between devices: 9 us -> 12.9 us  [stats(): part = lax.all_to_all(part, ROW, 0, 0, tiled=True)]
    all_to_all x3 -> x4, starting transfers between devices: 10 us -> 13.3 us  [stats(): part = lax.all_to_all(part, ROW, 0, 0, tiled=True)]
    unnamed x39 -> x45, local copies, waits for them, and re-layouts: 10.1 us -> 11.8 us
  transfers between devices with their start and end apart: 25 -> 25, of which waited for: 6 -> 7; matrix products, arithmetic and copies ran while one was open for 1% -> 1% of each run, Pallas kernels for 13% -> 12%
where the time goes in v2:
time: 258 us; the launch traced here: 256 us
  starting transfers between devices  76.8 us (30%)
  blocking collectives  70 us (27%)
  waiting for transfers between devices  55.3 us (21%)
  Pallas kernels  37.4 us (14%)
  local copies, waits for them, and re-layouts  13.1 us (5%)
  other arithmetic  2.66 us (1%)
    all_to_all x7, blocking collectives, stats(): part = lax.all_to_all(part, ROW, 0, 0, tiled=True)  56.2 us
    ppermute x20, starting transfers between devices, moved(): return lax.ppermute(value, axis, moves)  56 us
    ppermute x20, waiting for transfers between devices, moved(): return lax.ppermute(value, axis, moves)  39.6 us
    pallas_call x12, Pallas kernels, layer(): pl.pallas_call(functools.partial(layer_kernel, index, min(index, weights[...  33 us
    all_to_all x1, blocking collectives, program(): return lax.all_to_all(blocks, 'x', 0, 0, tiled=True)[None]  13.8 us
    all_to_all x4, starting transfers between devices, stats(): part = lax.all_to_all(part, ROW, 0, 0, tiled=True)  13.3 us
    all_to_all x4, waiting for transfers between devices, stats(): part = lax.all_to_all(part, ROW, 0, 0, tiled=True)  12.9 us
    unnamed x45, local copies, waits for them, and re-layouts  11.8 us
  transfers between devices with their start and end apart: 25, of which 7 were waited for; matrix products, arithmetic and copies ran while one was open for 1% of the time, Pallas kernels for 12%

profile of v2, /device:TPU:128, one launch (start us, length us, event | category | flops | bytes accessed | tf_op | source)
XLA Modules:
  0.0 256.1 jit_solution(4248288352433499748)
XLA Ops:
  2.3 7.5 %all-to-all-start = ((f32[32,1,256]{2,1,0:T(1,128)}), f32[32,1,256]{2,1,0:T(1,128)S(1)}, u32[]{:S(2)}, u32[]{:S(2)}) async-start(f32[32,1,256]{2,1,0:T(1,128)} %all_to_all.42), calls=%async_computation | async-start | bytes 65536 | tf_op jit(solution)/shard_map/all_to_all | solution.py:247
  14.4 2.8 %all-to-all-done = f32[32,1,256]{2,1,0:T(1,128)S(1)} async-done(((f32[32,1,256]{2,1,0:T(1,128)}), f32[32,1,256]{2,1,0:T(1,128)S(1)}, u32[]{:S(2)}, u32[]{:S(2)}) %all-to-all-start) | async-done | bytes 32800 | tf_op jit(solution)/shard_map/all_to_all | solution.py:247
  18.3 2.9 %layer.12 = (f32[4,288,256]{2,1,0:T(8,128)S(1)}, f32[8,2,256]{2,1,0:T(2,128)}) custom-call(s32[1]{0:T(128)} %bitcast.11.core.half, bf16[4,288,256]{2,1,0:T(8,128)(2,1)S(1)} %multiply_convert_fusion.h_ref, f32[1,2,256]{2,1,0:T(2,128)S(1)} %maximum_multiply_fusion.part_ref, f32[8,256]{1,0:T(8,128)S(1)} %concatenate.24.par_ref, ...), custom_call_target="tpu_custom_call" | custom-call | flops 1200000000 | bytes 4000000 | tf_op jit(solution)/shard_map/layer/pallas_call | solution.py:123
  22.3 3.3 %all-to-all-start.1 = ((f32[8,2,256]{2,1,0:T(2,128)}), f32[8,2,256]{2,1,0:T(2,128)S(1)}, u32[]{:S(2)}, u32[]{:S(2)}) async-start(f32[8,2,256]{2,1,0:T(2,128)} %get-tuple-element.58), calls=%async_computation.1 | async-start | bytes 32768 | tf_op jit(solution)/shard_map/all_to_all | solution.py:278
  27.6 3.3 %all-to-all-done.1.part_ref = f32[8,2,256]{2,1,0:T(2,128)S(1)} async-done(((f32[8,2,256]{2,1,0:T(2,128)}), f32[8,2,256]{2,1,0:T(2,128)S(1)}, u32[]{:S(2)}, u32[]{:S(2)}) %all-to-all-start.1) | async-done | bytes 16416 | tf_op jit(solution)/shard_map/all_to_all | solution.py:278
  32.2 2.3 layer.13
  34.5 7.7 %all_to_all.69 = f32[8,2,256]{2,1,0:T(2,128)S(1)} all-to-all(f32[8,2,256]{2,1,0:T(2,128)S(1)} %get-tuple-element.61), channel_id=1, replica_groups=mesh['z'=8,'y'=4,'x'=4,'c'=2] {'y','c'}, dimensions={0} | all-to-all | bytes 32768 | tf_op jit(solution)/shard_map/all_to_all | solution.py:278
  46.0 2.3 layer.14
  48.3 7.7 %all_to_all.70.part_ref = f32[8,2,256]{2,1,0:T(2,128)S(1)} all-to-all(f32[8,2,256]{2,1,0:T(2,128)S(1)} %get-tuple-element.67), channel_id=1, replica_groups=mesh['z'=8,'y'=4,'x'=4,'c'=2] {'y','c'}, dimensions={0} | all-to-all | bytes 32768 | tf_op jit(solution)/shard_map/all_to_all | solution.py:278
  58.3 7.7 %all_to_all.71.part_ref = f32[8,2,256]{2,1,0:T(2,128)S(1)} all-to-all(f32[8,2,256]{2,1,0:T(2,128)S(1)} %get-tuple-element.69), channel_id=1, replica_groups=mesh['z'=8,'y'=4,'x'=4,'c'=2] {'y','c'}, dimensions={0} | all-to-all | bytes 32768 | tf_op jit(solution)/shard_map/all_to_all | solution.py:278
  66.0 38.2 %collective-permute-start.10 = (bf16[1,1152,256]{2,1,0:T(8,128)(2,1)}, bf16[1,1152,256]{2,1,0:T(8,128)(2,1)}, u32[]{:S(2)}, u32[]{:S(2)}) collective-permute-start(bf16[1,1152,256]{2,1,0:T(8,128)(2,1)} %get-tuple-element.85), channel_id=1, source_target_pairs={{128,32},{129,33},{130,34},{131,35},{132,36},{133,37},{134,38},{13... | collective-permute-start | bytes 1769480 | tf_op jit(solution)/shard_map/ppermute | solution.py:226
  105.8 10.4 %collective-permute-done.10.refs_0_ = bf16[1,1152,256]{2,1,0:T(8,128)(2,1)} collective-permute-done((bf16[1,1152,256]{2,1,0:T(8,128)(2,1)}, bf16[1,1152,256]{2,1,0:T(8,128)(2,1)}, u32[]{:S(2)}, u32[]{:S(2)}) %collective-permute-start.10) | collective-permute-done | bytes 589856 | tf_op jit(solution)/shard_map/ppermute | solution.py:226
  116.2 3.5 %layer.16 = (f32[4,288,256]{2,1,0:T(8,128)S(1)}, f32[8,2,256]{2,1,0:T(2,128)}) custom-call(s32[1]{0:T(128)} %bitcast.11.core.half, bf16[4,288,256]{2,1,0:T(8,128)(2,1)S(1)} %get-tuple-element.68.h_ref.refs_1_, f32[8,2,256]{2,1,0:T(2,128)S(1)} %all_to_all.71.part_ref, f32[8,256]{1,0:T(8,128)S(1)} %collective-permute-done.1.par_ref, ...), custom_call_target="tpu_custom_call" | custom-call | flops 1200000000 | bytes 4000000 | tf_op jit(solution)/shard_map/layer/pallas_call | solution.py:123
  120.8 3.3 %all-to-all-start.5 = ((f32[8,2,256]{2,1,0:T(2,128)}), f32[8,2,256]{2,1,0:T(2,128)S(1)}, u32[]{:S(2)}, u32[]{:S(2)}) async-start(f32[8,2,256]{2,1,0:T(2,128)} %get-tuple-element.74), calls=%async_computation.5 | async-start | bytes 32768 | tf_op jit(solution)/shard_map/all_to_all | solution.py:278
  125.0 4.4 %all-to-all-done.5.part_ref = f32[8,2,256]{2,1,0:T(2,128)S(1)} async-done(((f32[8,2,256]{2,1,0:T(2,128)}), f32[8,2,256]{2,1,0:T(2,128)S(1)}, u32[]{:S(2)}, u32[]{:S(2)}) %all-to-all-start.5) | async-done | bytes 16416 | tf_op jit(solution)/shard_map/all_to_all | solution.py:278
  131.9 2.5 layer.17
  134.5 7.7 %all_to_all.72.part_ref = f32[8,2,256]{2,1,0:T(2,128)S(1)} all-to-all(f32[8,2,256]{2,1,0:T(2,128)S(1)} %get-tuple-element.78), channel_id=1, replica_groups=mesh['z'=8,'y'=4,'x'=4,'c'=2] {'y','c'}, dimensions={0} | all-to-all | bytes 32768 | tf_op jit(solution)/shard_map/all_to_all | solution.py:278
  142.2 2.6 %layer.18 = (f32[4,288,256]{2,1,0:T(8,128)S(1)}, f32[8,2,256]{2,1,0:T(2,128)S(1)}) custom-call(s32[1]{0:T(128)} %bitcast.11.core.half, bf16[4,288,256]{2,1,0:T(8,128)(2,1)S(1)} %get-tuple-element.75.h_ref, f32[8,2,256]{2,1,0:T(2,128)S(1)} %all_to_all.72.part_ref, f32[16,256]{1,0:T(8,128)S(1)} %collective-permute-done.6.par_ref, ...), custom_call_target="tpu_custom_call" | custom-call | flops 1200000000 | bytes 4000000 | tf_op jit(solution)/shard_map/layer/pallas_call | solution.py:123
  144.8 7.7 %all_to_all.73.part_ref = f32[8,2,256]{2,1,0:T(2,128)S(1)} all-to-all(f32[8,2,256]{2,1,0:T(2,128)S(1)} %get-tuple-element.82), channel_id=1, replica_groups=mesh['z'=8,'y'=4,'x'=4,'c'=2] {'y','c'}, dimensions={0} | all-to-all | bytes 32768 | tf_op jit(solution)/shard_map/all_to_all | solution.py:278
  152.6 3.3 %layer.19 = (bf16[4,288,256]{2,1,0:T(8,128)(2,1)S(1)}, f32[8,2,256]{2,1,0:T(2,128)}) custom-call(s32[1]{0:T(128)} %bitcast.11.core.half, f32[4,288,256]{2,1,0:T(8,128)S(1)} %get-tuple-element.81.h_ref, f32[8,2,256]{2,1,0:T(2,128)S(1)} %all_to_all.73.part_ref, f32[16,256]{1,0:T(8,128)S(1)} %collective-permute-done.6.par_ref, ...), custom_call_target="tpu_custom_call" | custom-call | flops 1200000000 | bytes 4000000 | tf_op jit(solution)/shard_map/layer/pallas_call | solution.py:123
  156.7 3.3 %all-to-all-start.8 = ((f32[8,2,256]{2,1,0:T(2,128)}), f32[8,2,256]{2,1,0:T(2,128)S(1)}, u32[]{:S(2)}, u32[]{:S(2)}) async-start(f32[8,2,256]{2,1,0:T(2,128)} %get-tuple-element.84), calls=%async_computation.8 | async-start | bytes 32768 | tf_op jit(solution)/shard_map/all_to_all | solution.py:278
  160.1 5.3 %all-to-all-done.8.part_ref = f32[8,2,256]{2,1,0:T(2,128)S(1)} async-done(((f32[8,2,256]{2,1,0:T(2,128)}), f32[8,2,256]{2,1,0:T(2,128)S(1)}, u32[]{:S(2)}, u32[]{:S(2)}) %all-to-all-start.8) | async-done | bytes 16416 | tf_op jit(solution)/shard_map/all_to_all | solution.py:278
  166.4 2.7 %layer.20 = (bf16[4,288,256]{2,1,0:T(8,128)(2,1)S(1)}, f32[8,2,256]{2,1,0:T(2,128)S(1)}) custom-call(s32[1]{0:T(128)} %bitcast.11.core.half, bf16[4,288,256]{2,1,0:T(8,128)(2,1)S(1)} %copy-done.9, f32[8,2,256]{2,1,0:T(2,128)S(1)} %all-to-all-done.8.part_ref, f32[16,256]{1,0:T(8,128)S(1)} %collective-permute-done.6.par_ref, ...), custom_call_target="tpu_custom_call" | custom-call | flops 1200000000 | bytes 4000000 | tf_op jit(solution)/shard_map/layer/pallas_call | solution.py:123
  169.9 7.7 %all_to_all.74 = f32[8,2,256]{2,1,0:T(2,128)S(1)} all-to-all(f32[8,2,256]{2,1,0:T(2,128)S(1)} %get-tuple-element.87), channel_id=1, replica_groups=mesh['z'=8,'y'=4,'x'=4,'c'=2] {'y','c'}, dimensions={0} | all-to-all | bytes 32768 | tf_op jit(solution)/shard_map/all_to_all | solution.py:278
  178.3 3.1 %layer.21 = (bf16[4,288,256]{2,1,0:T(8,128)(2,1)S(1)}, f32[8,2,256]{2,1,0:T(2,128)}) custom-call(s32[1]{0:T(128)} %bitcast.11.core.half, bf16[4,288,256]{2,1,0:T(8,128)(2,1)S(1)} %collective-permute-done.13.h_ref, f32[8,2,256]{2,1,0:T(2,128)S(1)} %collective-permute-done.14.part_ref, f32[16,256]{1,0:T(8,128)S(1)} %collective-permute-done.6.par_ref, ...), custom_call_target="tpu_custom_call" | custom-call | flops 1200000000 | bytes 4000000 | tf_op jit(solution)/shard_map/layer/pallas_call | solution.py:123
  182.3 3.3 %all-to-all-start.10 = ((f32[8,2,256]{2,1,0:T(2,128)}), f32[8,2,256]{2,1,0:T(2,128)S(1)}, u32[]{:S(2)}, u32[]{:S(2)}) async-start(f32[8,2,256]{2,1,0:T(2,128)} %get-tuple-element.91), calls=%async_computation.10 | async-start | bytes 32768 | tf_op jit(solution)/shard_map/all_to_all | solution.py:278
  193.7 2.5 layer.22
  196.9 9.9 %all_to_all.75.part_ref = f32[8,2,256]{2,1,0:T(2,128)S(1)} all-to-all(f32[8,2,256]{2,1,0:T(2,128)S(1)} %get-tuple-element.93), channel_id=1, replica_groups=mesh['z'=8,'y'=4,'x'=4,'c'=2] {'y','c'}, dimensions={0} | all-to-all | bytes 32768 | tf_op jit(solution)/shard_map/all_to_all | solution.py:278
  206.8 3.0 %layer.23 = (bf16[4,288,256]{2,1,0:T(8,128)(2,1)S(1)}, f32[8,2,256]{2,1,0:T(2,128)}) custom-call(s32[1]{0:T(128)} %bitcast.11.core.half, bf16[4,288,256]{2,1,0:T(8,128)(2,1)S(1)} %get-tuple-element.92.h_ref, f32[8,2,256]{2,1,0:T(2,128)S(1)} %all_to_all.75.part_ref, f32[8,256]{1,0:T(8,128)S(1)} %concatenate.24.par_ref, ...), custom_call_target="tpu_custom_call" | custom-call | flops 1200000000 | bytes 4000000 | tf_op jit(solution)/shard_map/layer/pallas_call | solution.py:123
  209.8 27.4 %collective-permute-done.12.refs_4_ = bf16[4,288,256]{2,1,0:T(8,128)(2,1)} collective-permute-done((bf16[4,288,256]{2,1,0:T(8,128)(2,1)}, bf16[4,288,256]{2,1,0:T(8,128)(2,1)}, u32[]{:S(2)}, u32[]{:S(2)}) %collective-permute-start.12) | collective-permute-done | bytes 589856 | tf_op jit(solution)/shard_map/ppermute | solution.py:226
  237.2 2.3 ordered.1
  241.4 13.8 %all_to_all.76 = bf16[4,4,64,256]{3,2,1,0:T(8,128)(2,1)S(1)} all-to-all(bf16[4,4,64,256]{3,2,1,0:T(8,128)(2,1)S(1)} %maximum_select_fusion), channel_id=1, replica_groups=mesh['z'=8,'y'=4,'x'=4,'c'=2] {'x'}, dimensions={0} | all-to-all | bytes 1048576 | tf_op jit(solution)/shard_map/all_to_all | solution.py:324
  (116 shorter events, 39.8 us)
Async XLA Ops:
  0.0 13.8 %copy-start = (bf16[1,256,256]{2,1,0:T(8,128)(2,1)S(1)}, bf16[1,256,256]{2,1,0:T(8,128)(2,1)}, u32[]{:S(2)}) copy-start(bf16[1,256,256]{2,1,0:T(8,128)(2,1)} %param.15) | copy-start | bytes 393220
  2.3 11.3 %copy-start.21 = (s32[4]{0:T(128)S(1)}, s32[4]{0:T(128)}, u32[]{:S(2)}) copy-start(s32[4]{0:T(128)} %param.10) | copy-start | bytes 52
  2.3 14.9 %all-to-all-start = ((f32[32,1,256]{2,1,0:T(1,128)}), f32[32,1,256]{2,1,0:T(1,128)S(1)}, u32[]{:S(2)}, u32[]{:S(2)}) async-start(f32[32,1,256]{2,1,0:T(1,128)} %all_to_all.42), calls=%async_computation | async-start | bytes 65536 | tf_op jit(solution)/shard_map/all_to_all | solution.py:247
  11.9 32.7 %collective-permute-start.3 = (bf16[2,1152,256]{2,1,0:T(8,128)(2,1)}, bf16[2,1152,256]{2,1,0:T(8,128)(2,1)}, u32[]{:S(2)}, u32[]{:S(2)}) collective-permute-start(bf16[2,1152,256]{2,1,0:T(8,128)(2,1)} %get-tuple-element.80), channel_id=1, source_target_pairs={{64,32},{192,224},{65,33},{193,225},{66,34},{194,226},{67,35},{195... | collective-permute-start | bytes 3538952 | tf_op jit(solution)/shard_map/ppermute | solution.py:226
  22.3 8.6 %all-to-all-start.1 = ((f32[8,2,256]{2,1,0:T(2,128)}), f32[8,2,256]{2,1,0:T(2,128)S(1)}, u32[]{:S(2)}, u32[]{:S(2)}) async-start(f32[8,2,256]{2,1,0:T(2,128)} %get-tuple-element.58), calls=%async_computation.1 | async-start | bytes 32768 | tf_op jit(solution)/shard_map/all_to_all | solution.py:278
  25.6 8.9 %collective-permute-start.1 = (f32[8,256]{1,0:T(8,128)S(1)}, f32[8,256]{1,0:T(8,128)S(1)}, u32[]{:S(2)}, u32[]{:S(2)}) collective-permute-start(f32[8,256]{1,0:T(8,128)S(1)} %concatenate.24.par_ref), channel_id=1, source_target_pairs={{64,32},{192,224},{128,96},{65,33},{193,225},{129,97},{66,34},{194... | collective-permute-start | bytes 24584 | tf_op jit(solution)/shard_map/ppermute | solution.py:226
  32.2 10.0 %copy-start.20 = (bf16[2,1152,256]{2,1,0:T(8,128)(2,1)S(1)}, bf16[2,1152,256]{2,1,0:T(8,128)(2,1)}, u32[]{:S(2)}) copy-start(bf16[2,1152,256]{2,1,0:T(8,128)(2,1)} %get-tuple-element.80) | copy-start | bytes 3538948
  42.2 3.2 %collective-permute-start.7 = (bf16[2,1152,256]{2,1,0:T(8,128)(2,1)S(1)}, bf16[2,1152,256]{2,1,0:T(8,128)(2,1)}, u32[]{:S(2)}, u32[]{:S(2)}) collective-permute-start(bf16[2,1152,256]{2,1,0:T(8,128)(2,1)S(1)} %copy-done.20), channel_id=1, source_target_pairs={{96,32},{97,33},{98,34},{99,35},{100,36},{101,37},{102,38},{103,39... | collective-permute-start | bytes 3538952 | tf_op jit(solution)/shard_map/ppermute | solution.py:226
  43.9 1.5 collective-permute-start
  44.6 71.6 %collective-permute-start.4 = (bf16[2,1152,256]{2,1,0:T(8,128)(2,1)}, bf16[2,1152,256]{2,1,0:T(8,128)(2,1)S(1)}, u32[]{:S(2)}, u32[]{:S(2)}) collective-permute-start(bf16[2,1152,256]{2,1,0:T(8,128)(2,1)} %collective-permute-done.3.refs_0_), channel_id=1, source_target_pairs={{0,1},{1,0},{2,3},{3,2},{4,5},{5,4},{6,7},{7,6},{8,9},{9,8},{10,11... | collective-permute-start | bytes 3538952 | tf_op jit(solution)/shard_map/ppermute | solution.py:226
  44.7 0.7 collective-permute-start.2
  45.4 96.8 %collective-permute-start.8 = (bf16[2,1152,256]{2,1,0:T(8,128)(2,1)}, bf16[2,1152,256]{2,1,0:T(8,128)(2,1)}, u32[]{:S(2)}, u32[]{:S(2)}) collective-permute-start(bf16[2,1152,256]{2,1,0:T(8,128)(2,1)} %collective-permute-done.7.refs_0_), channel_id=1, source_target_pairs={{0,1},{1,0},{2,3},{3,2},{4,5},{5,4},{6,7},{7,6},{8,9},{9,8},{10,11... | collective-permute-start | bytes 3538952 | tf_op jit(solution)/shard_map/ppermute | solution.py:226
  58.3 61.4 %copy-start.2 = (bf16[4,288,256]{2,1,0:T(8,128)(2,1)}, bf16[4,288,256]{2,1,0:T(8,128)(2,1)S(1)}, u32[]{:S(2)}) copy-start(bf16[4,288,256]{2,1,0:T(8,128)(2,1)S(1)} %get-tuple-element.68.h_ref.refs_1_) | copy-start | bytes 1769476
  66.0 50.2 %collective-permute-start.10 = (bf16[1,1152,256]{2,1,0:T(8,128)(2,1)}, bf16[1,1152,256]{2,1,0:T(8,128)(2,1)}, u32[]{:S(2)}, u32[]{:S(2)}) collective-permute-start(bf16[1,1152,256]{2,1,0:T(8,128)(2,1)} %get-tuple-element.85), channel_id=1, source_target_pairs={{128,32},{129,33},{130,34},{131,35},{132,36},{133,37},{134,38},{13... | collective-permute-start | bytes 1769480 | tf_op jit(solution)/shard_map/ppermute | solution.py:226
  104.3 65.5 %collective-permute-start.15 = (bf16[1,1152,256]{2,1,0:T(8,128)(2,1)}, bf16[1,1152,256]{2,1,0:T(8,128)(2,1)}, u32[]{:S(2)}, u32[]{:S(2)}) collective-permute-start(bf16[1,1152,256]{2,1,0:T(8,128)(2,1)} %get-tuple-element.85), channel_id=1, source_target_pairs={{160,224},{161,225},{162,226},{163,227},{164,228},{165,229},{166,2... | collective-permute-start | bytes 1769480 | tf_op jit(solution)/shard_map/ppermute | solution.py:226
  116.2 43.8 %collective-permute-start.11 = (bf16[1,1152,256]{2,1,0:T(8,128)(2,1)}, bf16[1,1152,256]{2,1,0:T(8,128)(2,1)}, u32[]{:S(2)}, u32[]{:S(2)}) collective-permute-start(bf16[1,1152,256]{2,1,0:T(8,128)(2,1)} %collective-permute-done.10.refs_0_), channel_id=1, source_target_pairs={{0,1},{1,0},{2,3},{3,2},{4,5},{5,4},{6,7},{7,6},{8,9},{9,8},{10,11... | collective-permute-start | bytes 1769480 | tf_op jit(solution)/shard_map/ppermute | solution.py:226
  120.8 8.6 %all-to-all-start.5 = ((f32[8,2,256]{2,1,0:T(2,128)}), f32[8,2,256]{2,1,0:T(2,128)S(1)}, u32[]{:S(2)}, u32[]{:S(2)}) async-start(f32[8,2,256]{2,1,0:T(2,128)} %get-tuple-element.74), calls=%async_computation.5 | async-start | bytes 32768 | tf_op jit(solution)/shard_map/all_to_all | solution.py:278
  124.1 10.3 %collective-permute-start.6 = (f32[16,256]{1,0:T(8,128)S(1)}, f32[16,256]{1,0:T(8,128)S(1)}, u32[]{:S(2)}, u32[]{:S(2)}) collective-permute-start(f32[16,256]{1,0:T(8,128)S(1)} %pad_maximum_fusion), channel_id=1, source_target_pairs={{96,32},{160,224},{97,33},{161,225},{98,34},{162,226},{99,35},{163... | collective-permute-start | bytes 49160 | tf_op jit(solution)/shard_map/ppermute | solution.py:226
  134.4 10.4 %copy-start.7 = (bf16[4,288,256]{2,1,0:T(8,128)(2,1)}, bf16[4,288,256]{2,1,0:T(8,128)(2,1)S(1)}, u32[]{:S(2)}) copy-start(bf16[4,288,256]{2,1,0:T(8,128)(2,1)S(1)} %get-tuple-element.75.h_ref) | copy-start | bytes 1769476
  156.7 8.6 %all-to-all-start.8 = ((f32[8,2,256]{2,1,0:T(2,128)}), f32[8,2,256]{2,1,0:T(2,128)S(1)}, u32[]{:S(2)}, u32[]{:S(2)}) async-start(f32[8,2,256]{2,1,0:T(2,128)} %get-tuple-element.84), calls=%async_computation.8 | async-start | bytes 32768 | tf_op jit(solution)/shard_map/all_to_all | solution.py:278
  169.1 8.5 %copy-start.10 = (bf16[4,288,256]{2,1,0:T(8,128)(2,1)}, bf16[4,288,256]{2,1,0:T(8,128)(2,1)S(1)}, u32[]{:S(2)}) copy-start(bf16[4,288,256]{2,1,0:T(8,128)(2,1)S(1)} %get-tuple-element.86) | copy-start | bytes 1769476
  169.1 9.2 %collective-permute-start.13 = (bf16[4,288,256]{2,1,0:T(8,128)(2,1)S(1)}, bf16[4,288,256]{2,1,0:T(8,128)(2,1)S(1)}, u32[]{:S(2)}, u32[]{:S(2)}) collective-permute-start(bf16[4,288,256]{2,1,0:T(8,128)(2,1)S(1)} %get-tuple-element.86), channel_id=1, source_target_pairs={{32,224},{33,225},{34,226},{35,227},{36,228},{37,229},{38,230},{39... | collective-permute-start | bytes 1769480 | tf_op jit(solution)/shard_map/ppermute | solution.py:226
  169.8 8.5 %collective-permute-start.16 = (bf16[1,1152,256]{2,1,0:T(8,128)(2,1)}, bf16[1,1152,256]{2,1,0:T(8,128)(2,1)S(1)}, u32[]{:S(2)}, u32[]{:S(2)}) collective-permute-start(bf16[1,1152,256]{2,1,0:T(8,128)(2,1)} %collective-permute-done.15.refs_0_), channel_id=1, source_target_pairs={{0,1},{1,0},{2,3},{3,2},{4,5},{5,4},{6,7},{7,6},{8,9},{9,8},{10,11... | collective-permute-start | bytes 1769480 | tf_op jit(solution)/shard_map/ppermute | solution.py:226
  177.6 0.7 collective-permute-start.14
  182.3 9.1 %all-to-all-start.10 = ((f32[8,2,256]{2,1,0:T(2,128)}), f32[8,2,256]{2,1,0:T(2,128)S(1)}, u32[]{:S(2)}, u32[]{:S(2)}) async-start(f32[8,2,256]{2,1,0:T(2,128)} %get-tuple-element.91), calls=%async_computation.10 | async-start | bytes 32768 | tf_op jit(solution)/shard_map/all_to_all | solution.py:278
  185.7 24.1 %collective-permute-start.5 = (bf16[4,288,256]{2,1,0:T(8,128)(2,1)}, bf16[4,288,256]{2,1,0:T(8,128)(2,1)}, u32[]{:S(2)}, u32[]{:S(2)}) collective-permute-start(bf16[4,288,256]{2,1,0:T(8,128)(2,1)} %copy-done.7), channel_id=1, source_target_pairs={{32,64},{33,65},{34,66},{35,67},{36,68},{37,69},{38,70},{39,71},{4... | collective-permute-start | bytes 1769480 | tf_op jit(solution)/shard_map/ppermute | solution.py:226
  187.1 22.7 %collective-permute-start.9 = (bf16[4,288,256]{2,1,0:T(8,128)(2,1)}, bf16[4,288,256]{2,1,0:T(8,128)(2,1)}, u32[]{:S(2)}, u32[]{:S(2)}) collective-permute-start(bf16[4,288,256]{2,1,0:T(8,128)(2,1)} %copy-done.8), channel_id=1, source_target_pairs={{32,96},{33,97},{34,98},{35,99},{36,100},{37,101},{38,102},{39,103... | collective-permute-start | bytes 1769480 | tf_op jit(solution)/shard_map/ppermute | solution.py:226
  188.6 48.6 %collective-permute-start.12 = (bf16[4,288,256]{2,1,0:T(8,128)(2,1)}, bf16[4,288,256]{2,1,0:T(8,128)(2,1)}, u32[]{:S(2)}, u32[]{:S(2)}) collective-permute-start(bf16[4,288,256]{2,1,0:T(8,128)(2,1)} %copy-done.10), channel_id=1, source_target_pairs={{32,128},{33,129},{34,130},{35,131},{36,132},{37,133},{38,134},{39... | collective-permute-start | bytes 1769480 | tf_op jit(solution)/shard_map/ppermute | solution.py:226
  189.9 47.3 %collective-permute-start.17 = (bf16[4,288,256]{2,1,0:T(8,128)(2,1)}, bf16[4,288,256]{2,1,0:T(8,128)(2,1)}, u32[]{:S(2)}, u32[]{:S(2)}) collective-permute-start(bf16[4,288,256]{2,1,0:T(8,128)(2,1)} %copy-done.11), channel_id=1, source_target_pairs={{224,160},{225,161},{226,162},{227,163},{228,164},{229,165},{230,1... | collective-permute-start | bytes 1769480 | tf_op jit(solution)/shard_map/ppermute | solution.py:226
  196.2 40.9 %collective-permute-start.18 = (bf16[4,288,256]{2,1,0:T(8,128)(2,1)S(1)}, bf16[4,288,256]{2,1,0:T(8,128)(2,1)S(1)}, u32[]{:S(2)}, u32[]{:S(2)}) collective-permute-start(bf16[4,288,256]{2,1,0:T(8,128)(2,1)S(1)} %get-tuple-element.92.h_ref), channel_id=1, source_target_pairs={{224,192},{225,193},{226,194},{227,195},{228,196},{229,197},{230,1... | collective-permute-start | bytes 1769480 | tf_op jit(solution)/shard_map/ppermute | solution.py:226
  206.8 30.4 %copy-start.3 = (bf16[4,288,256]{2,1,0:T(8,128)(2,1)S(1)}, bf16[4,288,256]{2,1,0:T(8,128)(2,1)}, u32[]{:S(2)}) copy-start(bf16[4,288,256]{2,1,0:T(8,128)(2,1)} %copy-done.2) | copy-start | bytes 1769476
  239.5 1.8 collective-permute-start.19
  (15 other events, 35.6 us)

commit v3 on v2

--- a/solution.py
+++ b/solution.py
@@ -58,16 +58,15 @@
     both = group_total(jnp.concatenate([total, square, jnp.zeros((6, C), jnp.float32)], axis=0))
     mean = both[0:1] / COUNT
     var = both[1:2] / COUNT - mean * mean
-    scale = lax.rsqrt(var + 1e-05) * gain
+    scale = 0.5 * lax.rsqrt(var + 1e-05) * gain
+    shift = 0.5 * bias
+    centre = mean - temb if first else mean
 
     def activate(f, _):
         for lo in range(0, ROWS, 2 * STRIPS):
             hi = lo + 2 * STRIPS
             h = h_ref[f, lo:hi].astype(jnp.float32)
-            if first:
-                h = h + temb
-            x = (h - mean) * scale + bias
-            half = 0.5 * x
+            half = (h - centre) * scale + shift
             valid = valid_ref[lo:hi]
             a = (half + half * jnp.tanh(half)) * jnp.concatenate([valid, valid], axis=1)
             b = a.astype(jnp.bfloat16)
@@ -199,11 +198,7 @@
     def _():
         carry(2, two_hbm)
 
-    @pl.when(z == 6)
-    def _():
-        carry(1, two_hbm)
-
-    @pl.when((z == 4) | (z == 5))
+    @pl.when((z == 4) | (z == 5) | (z == 6))
     def _():
         carry(1, one_hbm)
 
@@ -237,7 +232,7 @@
     own_w = conv_weight[0].reshape(2, K, C)
     plane = z.reshape(1).astype(jnp.int32)
     half, one = halves(plane, core, own_w)
-    near = moved(half, [(2, 1), (6, 7)])
+    near = moved(half, [(2, 1)])
 
     steps_f = timestep.astype(jnp.float32)
     level = jnp.cos(math.pi / 2.0 * (steps_f / STEPS + 0.008) / 1.008) ** 2
@@ -284,36 +279,36 @@
     ret0 = h
     hopped = moved(h, [(0, 1)])
     part, p2 = stats(part, p2)
-    part, half, sent_p = lax.optimization_barrier((part, half, own_p))
+    part, half, one, sent_p = lax.optimization_barrier((part, half, one, own_p))
     part = moved(part, [(0, 1)])
     p3 = moved(jnp.concatenate([sent_p, p2]), [(3, 1), (5, 7)])
     mid = moved(half, [(3, 1)])
+    w46 = moved(one, [(4, 1), (6, 7)])
+    w5 = moved(one, [(5, 7)])
     h, part = lax.optimization_barrier((hopped, part))
     h, part = run(0, False, h, part, own_p, own_w)
     h, part = run(1, True, h, stats(part), own_p, own_w)
     ret1 = h
     near = (near, swapped(near))
-    part = stats(part)
-    part, one = lax.optimization_barrier((part, one))
-    w4 = moved(one, [(4, 1)])
-    w5 = moved(one, [(5, 7)])
-    h, part = run(0, False, h, part, p2, near)
+    h, part = run(0, False, h, stats(part), p2, near)
     h, part = run(1, True, h, stats(part), p2, near)
     ret2 = moved(h, [(1, 2)])
     mid = (mid, swapped(mid))
     part, p3 = stats(part, p3)
     h, part = run(0, False, h, part, p3, mid)
     h, part = run(1, True, h, stats(part), p3, mid)
-    ret3 = moved(h, [(1, 3)])
-    h, part = run(0, True, h, stats(part), p3, (w4, swapped(w4)), 8)
+    back3 = h
+    w46 = (w46, swapped(w46))
+    h, part = run(0, True, h, stats(part), p3, w46, 8)
     w5s = swapped(w5)
     hopped = moved(h, [(1, 7)])
     part = moved(stats(part), [(1, 7)])
+    ret3 = moved(back3, [(1, 3)])
     ret4 = moved(h, [(1, 4)])
     h, part = lax.optimization_barrier((hopped, part))
     h, part = run(0, True, h, part, p3, (w5, w5s))
     ret5 = moved(h, [(7, 5)])
-    h, part = run(0, True, h, stats(part), p2, near)
+    h, part = run(0, True, h, stats(part), p2, w46)
     ret6 = moved(h, [(7, 6)])
     h, part = run(0, True, h, stats(part), own_p, own_w)
     ret7 = h

time: 258 us -> 246 us (0.953)
  waiting for transfers between devices: 55.3 us -> 47.6 us
  blocking collectives: 70 us -> 62.5 us
  starting transfers between devices: 76.8 us -> 81.1 us
    ppermute x20, waiting for transfers between devices: 39.6 us -> 28.2 us  [moved(): return lax.ppermute(value, axis, moves)]
    all_to_all x7 -> x6, blocking collectives: 56.2 us -> 48.6 us  [stats(): part = lax.all_to_all(part, ROW, 0, 0, tiled=True)]
    all_to_all x4 -> x5, waiting for transfers between devices: 12.9 us -> 16.5 us  [stats(): part = lax.all_to_all(part, ROW, 0, 0, tiled=True)]
    all_to_all x4 -> x5, starting transfers between devices: 13.3 us -> 16.7 us  [stats(): part = lax.all_to_all(part, ROW, 0, 0, tiled=True)]
    unnamed x45 -> x41, local copies, waits for them, and re-layouts: 11.8 us -> 11.1 us
  transfers between devices with their start and end apart: 25 -> 26, of which waited for: 7 -> 7; matrix products, arithmetic and copies ran while one was open for 1% -> 1% of each run, Pallas kernels for 12% -> 13%
where the time goes in v3:
time: 246 us; the launch traced here: 245 us
  starting transfers between devices  81.1 us (33%)
  blocking collectives  62.5 us (25%)
  waiting for transfers between devices  47.6 us (19%)
  Pallas kernels  37.9 us (15%)
  local copies, waits for them, and re-layouts  12.4 us (5%)
  other arithmetic  2.66 us (1%)
    ppermute x20, starting transfers between devices, moved(): return lax.ppermute(value, axis, moves)  57 us
    all_to_all x6, blocking collectives, stats(): part = lax.all_to_all(part, ROW, 0, 0, tiled=True)  48.6 us
    pallas_call x12, Pallas kernels, layer(): pl.pallas_call(functools.partial(layer_kernel, index, min(index, weights[...  33.5 us
    ppermute x20, waiting for transfers between devices, moved(): return lax.ppermute(value, axis, moves)  28.2 us
    all_to_all x5, starting transfers between devices, stats(): part = lax.all_to_all(part, ROW, 0, 0, tiled=True)  16.7 us
    all_to_all x5, waiting for transfers between devices, stats(): part = lax.all_to_all(part, ROW, 0, 0, tiled=True)  16.5 us
    all_to_all x1, blocking collectives, program(): return lax.all_to_all(blocks, 'x', 0, 0, tiled=True)[None]  13.8 us
    unnamed x41, local copies, waits for them, and re-layouts  11.1 us
  transfers between devices with their start and end apart: 26, of which 7 were waited for; matrix products, arithmetic and copies ran while one was open for 1% of the time, Pallas kernels for 13%

profile of v3, /device:TPU:128, one launch (start us, length us, event | category | flops | bytes accessed | tf_op | source)
XLA Modules:
  0.0 244.8 jit_solution(1631978856858066453)
XLA Ops:
  2.3 7.5 %all-to-all-start = ((f32[32,1,256]{2,1,0:T(1,128)}), f32[32,1,256]{2,1,0:T(1,128)S(1)}, u32[]{:S(2)}, u32[]{:S(2)}) async-start(f32[32,1,256]{2,1,0:T(1,128)} %all_to_all.42), calls=%async_computation | async-start | bytes 65536 | tf_op jit(solution)/shard_map/all_to_all | solution.py:242
  14.4 2.8 %all-to-all-done = f32[32,1,256]{2,1,0:T(1,128)S(1)} async-done(((f32[32,1,256]{2,1,0:T(1,128)}), f32[32,1,256]{2,1,0:T(1,128)S(1)}, u32[]{:S(2)}, u32[]{:S(2)}) %all-to-all-start) | async-done | bytes 32800 | tf_op jit(solution)/shard_map/all_to_all | solution.py:242
  18.3 2.8 %layer.12 = (f32[4,288,256]{2,1,0:T(8,128)S(1)}, f32[8,2,256]{2,1,0:T(2,128)}) custom-call(s32[1]{0:T(128)} %bitcast.11.core.half, bf16[4,288,256]{2,1,0:T(8,128)(2,1)S(1)} %multiply_convert_fusion.h_ref, f32[1,2,256]{2,1,0:T(2,128)S(1)} %maximum_multiply_fusion.part_ref, f32[8,256]{1,0:T(8,128)S(1)} %concatenate.24.par_ref, ...), custom_call_target="tpu_custom_call" | custom-call | flops 1200000000 | bytes 4000000 | tf_op jit(solution)/shard_map/layer/pallas_call | solution.py:122
  22.2 3.3 %all-to-all-start.1 = ((f32[8,2,256]{2,1,0:T(2,128)}), f32[8,2,256]{2,1,0:T(2,128)S(1)}, u32[]{:S(2)}, u32[]{:S(2)}) async-start(f32[8,2,256]{2,1,0:T(2,128)} %get-tuple-element.57), calls=%async_computation.1 | async-start | bytes 32768 | tf_op jit(solution)/shard_map/all_to_all | solution.py:273
  27.6 3.3 %all-to-all-done.1.part_ref = f32[8,2,256]{2,1,0:T(2,128)S(1)} async-done(((f32[8,2,256]{2,1,0:T(2,128)}), f32[8,2,256]{2,1,0:T(2,128)S(1)}, u32[]{:S(2)}, u32[]{:S(2)}) %all-to-all-start.1) | async-done | bytes 16416 | tf_op jit(solution)/shard_map/all_to_all | solution.py:273
  34.4 7.7 %all_to_all.69 = f32[8,2,256]{2,1,0:T(2,128)S(1)} all-to-all(f32[8,2,256]{2,1,0:T(2,128)S(1)} %get-tuple-element.60), channel_id=1, replica_groups=mesh['z'=8,'y'=4,'x'=4,'c'=2] {'y','c'}, dimensions={0} | all-to-all | bytes 32768 | tf_op jit(solution)/shard_map/all_to_all | solution.py:273
  45.0 39.1 %collective-permute-start.10 = (bf16[1,1152,256]{2,1,0:T(8,128)(2,1)}, bf16[1,1152,256]{2,1,0:T(8,128)(2,1)}, u32[]{:S(2)}, u32[]{:S(2)}) collective-permute-start(bf16[1,1152,256]{2,1,0:T(8,128)(2,1)} %get-tuple-element.83), channel_id=1, source_target_pairs={{128,32},{192,224},{129,33},{193,225},{130,34},{194,226},{131,35},... | collective-permute-start | bytes 1769480 | tf_op jit(solution)/shard_map/ppermute | solution.py:221
  84.9 2.2 layer.14
  87.1 7.7 %all_to_all.70.part_ref = f32[8,2,256]{2,1,0:T(2,128)S(1)} all-to-all(f32[8,2,256]{2,1,0:T(2,128)S(1)} %get-tuple-element.67), channel_id=1, replica_groups=mesh['z'=8,'y'=4,'x'=4,'c'=2] {'y','c'}, dimensions={0} | all-to-all | bytes 32768 | tf_op jit(solution)/shard_map/all_to_all | solution.py:273
  94.8 2.8 %layer.15 = (bf16[4,288,256]{2,1,0:T(8,128)(2,1)S(1)}, f32[8,2,256]{2,1,0:T(2,128)}) custom-call(s32[1]{0:T(128)} %bitcast.11.core.half, f32[4,288,256]{2,1,0:T(8,128)S(1)} %get-tuple-element.66.h_ref, f32[8,2,256]{2,1,0:T(2,128)S(1)} %all_to_all.70.part_ref, f32[8,256]{1,0:T(8,128)S(1)} %concatenate.24.par_ref, f32[288,128]{1,0:T(8,128)S(1)} %get-tuple-element.54.valid_ref, ...), custom_call_target="tpu_custom_call" | custom-call | flops 1200000000 | bytes 4000000 | tf_op jit(solution)/shard_map/layer/pallas_call | solution.py:122
  98.5 3.3 %all-to-all-start.4 = ((f32[8,2,256]{2,1,0:T(2,128)}), f32[8,2,256]{2,1,0:T(2,128)S(1)}, u32[]{:S(2)}, u32[]{:S(2)}) async-start(f32[8,2,256]{2,1,0:T(2,128)} %get-tuple-element.69), calls=%async_computation.4 | async-start | bytes 32768 | tf_op jit(solution)/shard_map/all_to_all | solution.py:273
  103.7 3.4 %all-to-all-done.4.part_ref = f32[8,2,256]{2,1,0:T(2,128)S(1)} async-done(((f32[8,2,256]{2,1,0:T(2,128)}), f32[8,2,256]{2,1,0:T(2,128)S(1)}, u32[]{:S(2)}, u32[]{:S(2)}) %all-to-all-start.4) | async-done | bytes 16416 | tf_op jit(solution)/shard_map/all_to_all | solution.py:273
  108.2 3.2 %layer.16 = (f32[4,288,256]{2,1,0:T(8,128)S(1)}, f32[8,2,256]{2,1,0:T(2,128)}) custom-call(s32[1]{0:T(128)} %bitcast.11.core.half, bf16[4,288,256]{2,1,0:T(8,128)(2,1)S(1)} %copy-done.3, f32[8,2,256]{2,1,0:T(2,128)S(1)} %all-to-all-done.4.part_ref, f32[8,256]{1,0:T(8,128)S(1)} %collective-permute-done.1.par_ref, f32[288,128]{1,0:T(8,128)S(1)} %get-tuple-element.54.valid_ref, ...), custom_call_target="tpu_custom_call" | custom-call | flops 1200000000 | bytes 4000000 | tf_op jit(solution)/shard_map/layer/pallas_call | solution.py:122
  112.5 3.3 %all-to-all-start.5 = ((f32[8,2,256]{2,1,0:T(2,128)}), f32[8,2,256]{2,1,0:T(2,128)S(1)}, u32[]{:S(2)}, u32[]{:S(2)}) async-start(f32[8,2,256]{2,1,0:T(2,128)} %get-tuple-element.72), calls=%async_computation.5 | async-start | bytes 32768 | tf_op jit(solution)/shard_map/all_to_all | solution.py:273
  116.5 4.6 %all-to-all-done.5.part_ref = f32[8,2,256]{2,1,0:T(2,128)S(1)} async-done(((f32[8,2,256]{2,1,0:T(2,128)}), f32[8,2,256]{2,1,0:T(2,128)S(1)}, u32[]{:S(2)}, u32[]{:S(2)}) %all-to-all-start.5) | async-done | bytes 16416 | tf_op jit(solution)/shard_map/all_to_all | solution.py:273
  122.4 2.7 %layer.17 = (bf16[4,288,256]{2,1,0:T(8,128)(2,1)S(1)}, f32[8,2,256]{2,1,0:T(2,128)S(1)}) custom-call(s32[1]{0:T(128)} %bitcast.11.core.half, f32[4,288,256]{2,1,0:T(8,128)S(1)} %copy-done.12, f32[8,2,256]{2,1,0:T(2,128)S(1)} %all-to-all-done.5.part_ref, f32[8,256]{1,0:T(8,128)S(1)} %collective-permute-done.1.par_ref, ...), custom_call_target="tpu_custom_call" | custom-call | flops 1200000000 | bytes 4000000 | tf_op jit(solution)/shard_map/layer/pallas_call | solution.py:122
  125.1 7.9 %all_to_all.71.part_ref = f32[8,2,256]{2,1,0:T(2,128)S(1)} all-to-all(f32[8,2,256]{2,1,0:T(2,128)S(1)} %get-tuple-element.76), channel_id=1, replica_groups=mesh['z'=8,'y'=4,'x'=4,'c'=2] {'y','c'}, dimensions={0} | all-to-all | bytes 32768 | tf_op jit(solution)/shard_map/all_to_all | solution.py:273
  133.0 2.6 %layer.18 = (f32[4,288,256]{2,1,0:T(8,128)S(1)}, f32[8,2,256]{2,1,0:T(2,128)S(1)}) custom-call(s32[1]{0:T(128)} %bitcast.11.core.half, bf16[4,288,256]{2,1,0:T(8,128)(2,1)S(1)} %get-tuple-element.73.h_ref, f32[8,2,256]{2,1,0:T(2,128)S(1)} %all_to_all.71.part_ref, f32[16,256]{1,0:T(8,128)S(1)} %collective-permute-done.6.par_ref, ...), custom_call_target="tpu_custom_call" | custom-call | flops 1200000000 | bytes 4000000 | tf_op jit(solution)/shard_map/layer/pallas_call | solution.py:122
  135.7 7.7 %all_to_all.72.part_ref = f32[8,2,256]{2,1,0:T(2,128)S(1)} all-to-all(f32[8,2,256]{2,1,0:T(2,128)S(1)} %get-tuple-element.80), channel_id=1, replica_groups=mesh['z'=8,'y'=4,'x'=4,'c'=2] {'y','c'}, dimensions={0} | all-to-all | bytes 32768 | tf_op jit(solution)/shard_map/all_to_all | solution.py:273
  143.4 3.3 %layer.19 = (bf16[4,288,256]{2,1,0:T(8,128)(2,1)S(1)}, f32[8,2,256]{2,1,0:T(2,128)}) custom-call(s32[1]{0:T(128)} %bitcast.11.core.half, f32[4,288,256]{2,1,0:T(8,128)S(1)} %get-tuple-element.79.h_ref, f32[8,2,256]{2,1,0:T(2,128)S(1)} %all_to_all.72.part_ref, f32[16,256]{1,0:T(8,128)S(1)} %collective-permute-done.6.par_ref, ...), custom_call_target="tpu_custom_call" | custom-call | flops 1200000000 | bytes 4000000 | tf_op jit(solution)/shard_map/layer/pallas_call | solution.py:122
  147.6 3.3 %all-to-all-start.8 = ((f32[8,2,256]{2,1,0:T(2,128)}), f32[8,2,256]{2,1,0:T(2,128)S(1)}, u32[]{:S(2)}, u32[]{:S(2)}) async-start(f32[8,2,256]{2,1,0:T(2,128)} %get-tuple-element.82), calls=%async_computation.8 | async-start | bytes 32768 | tf_op jit(solution)/shard_map/all_to_all | solution.py:273
  150.9 5.3 %all-to-all-done.8.part_ref = f32[8,2,256]{2,1,0:T(2,128)S(1)} async-done(((f32[8,2,256]{2,1,0:T(2,128)}), f32[8,2,256]{2,1,0:T(2,128)S(1)}, u32[]{:S(2)}, u32[]{:S(2)}) %all-to-all-start.8) | async-done | bytes 16416 | tf_op jit(solution)/shard_map/all_to_all | solution.py:273
  157.2 2.7 %layer.20 = (bf16[4,288,256]{2,1,0:T(8,128)(2,1)S(1)}, f32[8,2,256]{2,1,0:T(2,128)S(1)}) custom-call(s32[1]{0:T(128)} %bitcast.11.core.half, bf16[4,288,256]{2,1,0:T(8,128)(2,1)S(1)} %copy-done.7, f32[8,2,256]{2,1,0:T(2,128)S(1)} %all-to-all-done.8.part_ref, f32[16,256]{1,0:T(8,128)S(1)} %collective-permute-done.6.par_ref, ...), custom_call_target="tpu_custom_call" | custom-call | flops 1200000000 | bytes 4000000 | tf_op jit(solution)/shard_map/layer/pallas_call | solution.py:122
  160.8 7.7 %all_to_all.73 = f32[8,2,256]{2,1,0:T(2,128)S(1)} all-to-all(f32[8,2,256]{2,1,0:T(2,128)S(1)} %get-tuple-element.85), channel_id=1, replica_groups=mesh['z'=8,'y'=4,'x'=4,'c'=2] {'y','c'}, dimensions={0} | all-to-all | bytes 32768 | tf_op jit(solution)/shard_map/all_to_all | solution.py:273
  169.2 3.1 %layer.21 = (bf16[4,288,256]{2,1,0:T(8,128)(2,1)S(1)}, f32[8,2,256]{2,1,0:T(2,128)}) custom-call(s32[1]{0:T(128)} %bitcast.11.core.half, bf16[4,288,256]{2,1,0:T(8,128)(2,1)S(1)} %collective-permute-done.13.h_ref, f32[8,2,256]{2,1,0:T(2,128)S(1)} %collective-permute-done.14.part_ref, f32[16,256]{1,0:T(8,128)S(1)} %collective-permute-done.6.par_ref, ...), custom_call_target="tpu_custom_call" | custom-call | flops 1200000000 | bytes 4000000 | tf_op jit(solution)/shard_map/layer/pallas_call | solution.py:122
  173.1 3.3 %all-to-all-start.10 = ((f32[8,2,256]{2,1,0:T(2,128)}), f32[8,2,256]{2,1,0:T(2,128)S(1)}, u32[]{:S(2)}, u32[]{:S(2)}) async-start(f32[8,2,256]{2,1,0:T(2,128)} %get-tuple-element.89), calls=%async_computation.10 | async-start | bytes 32768 | tf_op jit(solution)/shard_map/all_to_all | solution.py:273
  183.3 2.7 %layer.22 = (bf16[4,288,256]{2,1,0:T(8,128)(2,1)S(1)}, f32[8,2,256]{2,1,0:T(2,128)S(1)}) custom-call(s32[1]{0:T(128)} %bitcast.11.core.half, bf16[4,288,256]{2,1,0:T(8,128)(2,1)S(1)} %copy-done.10, f32[8,2,256]{2,1,0:T(2,128)S(1)} %all-to-all-done.10.part_ref, f32[8,256]{1,0:T(8,128)S(1)} %collective-permute-done.1.par_ref, ...), custom_call_target="tpu_custom_call" | custom-call | flops 1200000000 | bytes 4000000 | tf_op jit(solution)/shard_map/layer/pallas_call | solution.py:122
  186.7 9.9 %all_to_all.74.part_ref = f32[8,2,256]{2,1,0:T(2,128)S(1)} all-to-all(f32[8,2,256]{2,1,0:T(2,128)S(1)} %get-tuple-element.91), channel_id=1, replica_groups=mesh['z'=8,'y'=4,'x'=4,'c'=2] {'y','c'}, dimensions={0} | all-to-all | bytes 32768 | tf_op jit(solution)/shard_map/all_to_all | solution.py:273
  196.5 2.9 %layer.23 = (bf16[4,288,256]{2,1,0:T(8,128)(2,1)S(1)}, f32[8,2,256]{2,1,0:T(2,128)}) custom-call(s32[1]{0:T(128)} %bitcast.11.core.half, bf16[4,288,256]{2,1,0:T(8,128)(2,1)S(1)} %get-tuple-element.90.h_ref, f32[8,2,256]{2,1,0:T(2,128)S(1)} %all_to_all.74.part_ref, f32[8,256]{1,0:T(8,128)S(1)} %concatenate.24.par_ref, ...), custom_call_target="tpu_custom_call" | custom-call | flops 1200000000 | bytes 4000000 | tf_op jit(solution)/shard_map/layer/pallas_call | solution.py:122
  199.5 26.5 %collective-permute-done.12.refs_4_ = bf16[4,288,256]{2,1,0:T(8,128)(2,1)} collective-permute-done((bf16[4,288,256]{2,1,0:T(8,128)(2,1)}, bf16[4,288,256]{2,1,0:T(8,128)(2,1)}, u32[]{:S(2)}, u32[]{:S(2)}) %collective-permute-start.12) | collective-permute-done | bytes 589856 | tf_op jit(solution)/shard_map/ppermute | solution.py:221
  225.9 2.3 ordered.1
  230.2 13.8 %all_to_all.75 = bf16[4,4,64,256]{3,2,1,0:T(8,128)(2,1)S(1)} all-to-all(bf16[4,4,64,256]{3,2,1,0:T(8,128)(2,1)S(1)} %maximum_select_fusion), channel_id=1, replica_groups=mesh['z'=8,'y'=4,'x'=4,'c'=2] {'x'}, dimensions={0} | all-to-all | bytes 1048576 | tf_op jit(solution)/shard_map/all_to_all | solution.py:319
  (113 shorter events, 39.1 us)
Async XLA Ops:
  0.0 13.8 %copy-start = (bf16[1,256,256]{2,1,0:T(8,128)(2,1)S(1)}, bf16[1,256,256]{2,1,0:T(8,128)(2,1)}, u32[]{:S(2)}) copy-start(bf16[1,256,256]{2,1,0:T(8,128)(2,1)} %param.15) | copy-start | bytes 393220
  2.3 11.3 %copy-start.19 = (s32[4]{0:T(128)S(1)}, s32[4]{0:T(128)}, u32[]{:S(2)}) copy-start(s32[4]{0:T(128)} %param.10) | copy-start | bytes 52
  2.3 14.9 %all-to-all-start = ((f32[32,1,256]{2,1,0:T(1,128)}), f32[32,1,256]{2,1,0:T(1,128)S(1)}, u32[]{:S(2)}, u32[]{:S(2)}) async-start(f32[32,1,256]{2,1,0:T(1,128)} %all_to_all.42), calls=%async_computation | async-start | bytes 65536 | tf_op jit(solution)/shard_map/all_to_all | solution.py:242
  11.9 31.8 %collective-permute-start.3 = (bf16[2,1152,256]{2,1,0:T(8,128)(2,1)}, bf16[2,1152,256]{2,1,0:T(8,128)(2,1)}, u32[]{:S(2)}, u32[]{:S(2)}) collective-permute-start(bf16[2,1152,256]{2,1,0:T(8,128)(2,1)} %get-tuple-element.78), channel_id=1, source_target_pairs={{64,32},{65,33},{66,34},{67,35},{68,36},{69,37},{70,38},{71,39},{7... | collective-permute-start | bytes 3538952 | tf_op jit(solution)/shard_map/ppermute | solution.py:221
  22.2 8.6 %all-to-all-start.1 = ((f32[8,2,256]{2,1,0:T(2,128)}), f32[8,2,256]{2,1,0:T(2,128)S(1)}, u32[]{:S(2)}, u32[]{:S(2)}) async-start(f32[8,2,256]{2,1,0:T(2,128)} %get-tuple-element.57), calls=%async_computation.1 | async-start | bytes 32768 | tf_op jit(solution)/shard_map/all_to_all | solution.py:273
  25.5 8.8 %collective-permute-start.1 = (f32[8,256]{1,0:T(8,128)S(1)}, f32[8,256]{1,0:T(8,128)S(1)}, u32[]{:S(2)}, u32[]{:S(2)}) collective-permute-start(f32[8,256]{1,0:T(8,128)S(1)} %concatenate.24.par_ref), channel_id=1, source_target_pairs={{64,32},{192,224},{128,96},{65,33},{193,225},{129,97},{66,34},{194... | collective-permute-start | bytes 24584 | tf_op jit(solution)/shard_map/ppermute | solution.py:221
  32.1 10.0 %copy-start.18 = (bf16[2,1152,256]{2,1,0:T(8,128)(2,1)S(1)}, bf16[2,1152,256]{2,1,0:T(8,128)(2,1)}, u32[]{:S(2)}) copy-start(bf16[2,1152,256]{2,1,0:T(8,128)(2,1)} %get-tuple-element.78) | copy-start | bytes 3538948
  42.1 2.4 collective-permute-start.7
  43.7 63.4 %collective-permute-start.4 = (bf16[2,1152,256]{2,1,0:T(8,128)(2,1)}, bf16[2,1152,256]{2,1,0:T(8,128)(2,1)}, u32[]{:S(2)}, u32[]{:S(2)}) collective-permute-start(bf16[2,1152,256]{2,1,0:T(8,128)(2,1)} %collective-permute-done.3.refs_0_), channel_id=1, source_target_pairs={{0,1},{1,0},{2,3},{3,2},{4,5},{5,4},{6,7},{7,6},{8,9},{9,8},{10,11... | collective-permute-start | bytes 3538952 | tf_op jit(solution)/shard_map/ppermute | solution.py:221
  43.7 41.1 %collective-permute-start = (bf16[4,288,256]{2,1,0:T(8,128)(2,1)S(1)}, bf16[4,288,256]{2,1,0:T(8,128)(2,1)S(1)}, u32[]{:S(2)}, u32[]{:S(2)}) collective-permute-start(bf16[4,288,256]{2,1,0:T(8,128)(2,1)S(1)} %get-tuple-element.58.refs_0_), channel_id=1, source_target_pairs={{0,32},{1,33},{2,34},{3,35},{4,36},{5,37},{6,38},{7,39},{8,40},{9,... | collective-permute-start | bytes 1769480 | tf_op jit(solution)/shard_map/ppermute | solution.py:221
  44.5 88.6 %collective-permute-start.8 = (bf16[2,1152,256]{2,1,0:T(8,128)(2,1)}, bf16[2,1152,256]{2,1,0:T(8,128)(2,1)}, u32[]{:S(2)}, u32[]{:S(2)}) collective-permute-start(bf16[2,1152,256]{2,1,0:T(8,128)(2,1)} %collective-permute-done.7.refs_0_), channel_id=1, source_target_pairs={{0,1},{1,0},{2,3},{3,2},{4,5},{5,4},{6,7},{7,6},{8,9},{9,8},{10,11... | collective-permute-start | bytes 3538952 | tf_op jit(solution)/shard_map/ppermute | solution.py:221
  45.0 58.3 %collective-permute-start.10 = (bf16[1,1152,256]{2,1,0:T(8,128)(2,1)}, bf16[1,1152,256]{2,1,0:T(8,128)(2,1)}, u32[]{:S(2)}, u32[]{:S(2)}) collective-permute-start(bf16[1,1152,256]{2,1,0:T(8,128)(2,1)} %get-tuple-element.83), channel_id=1, source_target_pairs={{128,32},{192,224},{129,33},{193,225},{130,34},{194,226},{131,35},... | collective-permute-start | bytes 1769480 | tf_op jit(solution)/shard_map/ppermute | solution.py:221
  84.2 0.7 collective-permute-start.2
  98.5 8.6 %all-to-all-start.4 = ((f32[8,2,256]{2,1,0:T(2,128)}), f32[8,2,256]{2,1,0:T(2,128)S(1)}, u32[]{:S(2)}, u32[]{:S(2)}) async-start(f32[8,2,256]{2,1,0:T(2,128)} %get-tuple-element.69), calls=%async_computation.4 | async-start | bytes 32768 | tf_op jit(solution)/shard_map/all_to_all | solution.py:273
  101.8 58.8 %collective-permute-start.15 = (bf16[1,1152,256]{2,1,0:T(8,128)(2,1)}, bf16[1,1152,256]{2,1,0:T(8,128)(2,1)}, u32[]{:S(2)}, u32[]{:S(2)}) collective-permute-start(bf16[1,1152,256]{2,1,0:T(8,128)(2,1)} %get-tuple-element.83), channel_id=1, source_target_pairs={{160,224},{161,225},{162,226},{163,227},{164,228},{165,229},{166,2... | collective-permute-start | bytes 1769480 | tf_op jit(solution)/shard_map/ppermute | solution.py:221
  103.3 47.6 %collective-permute-start.11 = (bf16[1,1152,256]{2,1,0:T(8,128)(2,1)}, bf16[1,1152,256]{2,1,0:T(8,128)(2,1)}, u32[]{:S(2)}, u32[]{:S(2)}) collective-permute-start(bf16[1,1152,256]{2,1,0:T(8,128)(2,1)} %collective-permute-done.10.refs_0_), channel_id=1, source_target_pairs={{0,1},{1,0},{2,3},{3,2},{4,5},{5,4},{6,7},{7,6},{8,9},{9,8},{10,11... | collective-permute-start | bytes 1769480 | tf_op jit(solution)/shard_map/ppermute | solution.py:221
  112.5 8.6 %all-to-all-start.5 = ((f32[8,2,256]{2,1,0:T(2,128)}), f32[8,2,256]{2,1,0:T(2,128)S(1)}, u32[]{:S(2)}, u32[]{:S(2)}) async-start(f32[8,2,256]{2,1,0:T(2,128)} %get-tuple-element.72), calls=%async_computation.5 | async-start | bytes 32768 | tf_op jit(solution)/shard_map/all_to_all | solution.py:273
  115.9 9.3 %collective-permute-start.6 = (f32[16,256]{1,0:T(8,128)S(1)}, f32[16,256]{1,0:T(8,128)S(1)}, u32[]{:S(2)}, u32[]{:S(2)}) collective-permute-start(f32[16,256]{1,0:T(8,128)S(1)} %pad_maximum_fusion), channel_id=1, source_target_pairs={{96,32},{160,224},{97,33},{161,225},{98,34},{162,226},{99,35},{163... | collective-permute-start | bytes 49160 | tf_op jit(solution)/shard_map/ppermute | solution.py:221
  125.1 10.6 %copy-start.5 = (bf16[4,288,256]{2,1,0:T(8,128)(2,1)}, bf16[4,288,256]{2,1,0:T(8,128)(2,1)S(1)}, u32[]{:S(2)}) copy-start(bf16[4,288,256]{2,1,0:T(8,128)(2,1)S(1)} %get-tuple-element.73.h_ref) | copy-start | bytes 1769476
  147.6 8.6 %all-to-all-start.8 = ((f32[8,2,256]{2,1,0:T(2,128)}), f32[8,2,256]{2,1,0:T(2,128)S(1)}, u32[]{:S(2)}, u32[]{:S(2)}) async-start(f32[8,2,256]{2,1,0:T(2,128)} %get-tuple-element.82), calls=%async_computation.8 | async-start | bytes 32768 | tf_op jit(solution)/shard_map/all_to_all | solution.py:273
  159.9 8.5 %copy-start.8 = (bf16[4,288,256]{2,1,0:T(8,128)(2,1)}, bf16[4,288,256]{2,1,0:T(8,128)(2,1)S(1)}, u32[]{:S(2)}) copy-start(bf16[4,288,256]{2,1,0:T(8,128)(2,1)S(1)} %get-tuple-element.84) | copy-start | bytes 1769476
  159.9 9.2 %collective-permute-start.13 = (bf16[4,288,256]{2,1,0:T(8,128)(2,1)S(1)}, bf16[4,288,256]{2,1,0:T(8,128)(2,1)S(1)}, u32[]{:S(2)}, u32[]{:S(2)}) collective-permute-start(bf16[4,288,256]{2,1,0:T(8,128)(2,1)S(1)} %get-tuple-element.84), channel_id=1, source_target_pairs={{32,224},{33,225},{34,226},{35,227},{36,228},{37,229},{38,230},{39... | collective-permute-start | bytes 1769480 | tf_op jit(solution)/shard_map/ppermute | solution.py:221
  160.7 8.5 %collective-permute-start.16 = (bf16[1,1152,256]{2,1,0:T(8,128)(2,1)}, bf16[1,1152,256]{2,1,0:T(8,128)(2,1)S(1)}, u32[]{:S(2)}, u32[]{:S(2)}) collective-permute-start(bf16[1,1152,256]{2,1,0:T(8,128)(2,1)} %collective-permute-done.15.refs_0_), channel_id=1, source_target_pairs={{0,1},{1,0},{2,3},{3,2},{4,5},{5,4},{6,7},{7,6},{8,9},{9,8},{10,11... | collective-permute-start | bytes 1769480 | tf_op jit(solution)/shard_map/ppermute | solution.py:221
  168.5 0.7 collective-permute-start.14
  173.1 9.1 %all-to-all-start.10 = ((f32[8,2,256]{2,1,0:T(2,128)}), f32[8,2,256]{2,1,0:T(2,128)S(1)}, u32[]{:S(2)}, u32[]{:S(2)}) async-start(f32[8,2,256]{2,1,0:T(2,128)} %get-tuple-element.89), calls=%async_computation.10 | async-start | bytes 32768 | tf_op jit(solution)/shard_map/all_to_all | solution.py:273
  176.5 23.0 %collective-permute-start.5 = (bf16[4,288,256]{2,1,0:T(8,128)(2,1)}, bf16[4,288,256]{2,1,0:T(8,128)(2,1)}, u32[]{:S(2)}, u32[]{:S(2)}) collective-permute-start(bf16[4,288,256]{2,1,0:T(8,128)(2,1)} %copy-done.5), channel_id=1, source_target_pairs={{32,64},{33,65},{34,66},{35,67},{36,68},{37,69},{38,70},{39,71},{4... | collective-permute-start | bytes 1769480 | tf_op jit(solution)/shard_map/ppermute | solution.py:221
  178.0 21.5 %collective-permute-start.9 = (bf16[4,288,256]{2,1,0:T(8,128)(2,1)}, bf16[4,288,256]{2,1,0:T(8,128)(2,1)}, u32[]{:S(2)}, u32[]{:S(2)}) collective-permute-start(bf16[4,288,256]{2,1,0:T(8,128)(2,1)} %copy-done.6), channel_id=1, source_target_pairs={{32,96},{33,97},{34,98},{35,99},{36,100},{37,101},{38,102},{39,103... | collective-permute-start | bytes 1769480 | tf_op jit(solution)/shard_map/ppermute | solution.py:221
  179.4 46.5 %collective-permute-start.12 = (bf16[4,288,256]{2,1,0:T(8,128)(2,1)}, bf16[4,288,256]{2,1,0:T(8,128)(2,1)}, u32[]{:S(2)}, u32[]{:S(2)}) collective-permute-start(bf16[4,288,256]{2,1,0:T(8,128)(2,1)} %copy-done.8), channel_id=1, source_target_pairs={{32,128},{33,129},{34,130},{35,131},{36,132},{37,133},{38,134},{39... | collective-permute-start | bytes 1769480 | tf_op jit(solution)/shard_map/ppermute | solution.py:221
  180.7 45.2 %collective-permute-start.17 = (bf16[4,288,256]{2,1,0:T(8,128)(2,1)}, bf16[4,288,256]{2,1,0:T(8,128)(2,1)}, u32[]{:S(2)}, u32[]{:S(2)}) collective-permute-start(bf16[4,288,256]{2,1,0:T(8,128)(2,1)} %copy-done.9), channel_id=1, source_target_pairs={{224,160},{225,161},{226,162},{227,163},{228,164},{229,165},{230,1... | collective-permute-start | bytes 1769480 | tf_op jit(solution)/shard_map/ppermute | solution.py:221
  186.0 40.0 %collective-permute-start.18 = (bf16[4,288,256]{2,1,0:T(8,128)(2,1)S(1)}, bf16[4,288,256]{2,1,0:T(8,128)(2,1)S(1)}, u32[]{:S(2)}, u32[]{:S(2)}) collective-permute-start(bf16[4,288,256]{2,1,0:T(8,128)(2,1)S(1)} %get-tuple-element.90.h_ref), channel_id=1, source_target_pairs={{224,192},{225,193},{226,194},{227,195},{228,196},{229,197},{230,1... | collective-permute-start | bytes 1769480 | tf_op jit(solution)/shard_map/ppermute | solution.py:221
  196.5 29.4 %copy-start.4 = (bf16[4,288,256]{2,1,0:T(8,128)(2,1)S(1)}, bf16[4,288,256]{2,1,0:T(8,128)(2,1)}, u32[]{:S(2)}) copy-start(bf16[4,288,256]{2,1,0:T(8,128)(2,1)} %copy-done.2) | copy-start | bytes 1769476
  228.3 1.8 collective-permute-start.19
  (14 other events, 31.4 us)

commit v4 on v3

--- a/solution.py
+++ b/solution.py
@@ -178,14 +178,14 @@
     )(plane, core, *sources)
 
 
-def halves_kernel(plane, half, w_hbm, two_hbm, one_hbm, held, sem):
+def halves_kernel(plane, half, w_hbm, two_hbm, one_hbm, last_hbm, held, sem):
     size = K // 2
     z, core = plane[0], half[0]
     rows = pl.ds(pl.multiple_of(core * size, size), size)
 
-    def carry(layers, target):
-        takes = [pltpu.make_async_copy(w_hbm.at[i, rows], held.at[i], sem.at[i]) for i in range(layers)]
-        gives = [pltpu.make_async_copy(held.at[i], target.at[i], sem.at[2 + i]) for i in range(layers)]
+    def carry(*targets):
+        takes = [pltpu.make_async_copy(w_hbm.at[i, rows], held.at[i], sem.at[i]) for i in range(len(targets))]
+        gives = [pltpu.make_async_copy(held.at[i], target, sem.at[2 + i]) for i, target in enumerate(targets)]
         for take in takes:
             take.start()
         for take, give in zip(takes, gives):
@@ -194,22 +194,26 @@
         for give in gives:
             give.wait()
 
-    @pl.when((z == 2) | (z == 3))
+    @pl.when(z == 2)
     def _():
-        carry(2, two_hbm)
+        carry(two_hbm.at[0], two_hbm.at[1])
+
+    @pl.when(z == 3)
+    def _():
+        carry(one_hbm.at[0], last_hbm.at[0])
 
     @pl.when((z == 4) | (z == 5) | (z == 6))
     def _():
-        carry(1, one_hbm)
+        carry(one_hbm.at[0])
 
 
 def halves(plane, core, weight):
     hbm = pl.BlockSpec(memory_space=pltpu.HBM)
     return pl.pallas_call(
         halves_kernel,
-        out_shape=tuple(jax.ShapeDtypeStruct((n, K // 2, C), jnp.bfloat16) for n in (2, 1)),
+        out_shape=tuple(jax.ShapeDtypeStruct((n, K // 2, C), jnp.bfloat16) for n in (2, 1, 1)),
         in_specs=[pl.BlockSpec(memory_space=pltpu.SMEM)] * 2 + [hbm],
-        out_specs=(hbm, hbm),
+        out_specs=(hbm, hbm, hbm),
         scratch_shapes=[pltpu.VMEM((2, K // 2, C), jnp.bfloat16), pltpu.SemaphoreType.DMA((4,))],
         compiler_params=pltpu.CompilerParams(vmem_limit_bytes=60 * 1024 * 1024),
         cost_estimate=pl.CostEstimate(flops=1000000, bytes_accessed=5000000, transcendentals=0),
@@ -231,7 +235,7 @@
     core = c.reshape(1).astype(jnp.int32)
     own_w = conv_weight[0].reshape(2, K, C)
     plane = z.reshape(1).astype(jnp.int32)
-    half, one = halves(plane, core, own_w)
+    half, one, other = halves(plane, core, own_w)
     near = moved(half, [(2, 1)])
 
     steps_f = timestep.astype(jnp.float32)
@@ -279,12 +283,12 @@
     ret0 = h
     hopped = moved(h, [(0, 1)])
     part, p2 = stats(part, p2)
-    part, half, one, sent_p = lax.optimization_barrier((part, half, one, own_p))
+    part, one, other, sent_p = lax.optimization_barrier((part, one, other, own_p))
     part = moved(part, [(0, 1)])
     p3 = moved(jnp.concatenate([sent_p, p2]), [(3, 1), (5, 7)])
-    mid = moved(half, [(3, 1)])
+    w35 = moved(one, [(3, 1), (5, 7)])
+    w3b = moved(other, [(3, 1)])
     w46 = moved(one, [(4, 1), (6, 7)])
-    w5 = moved(one, [(5, 7)])
     h, part = lax.optimization_barrier((hopped, part))
     h, part = run(0, False, h, part, own_p, own_w)
     h, part = run(1, True, h, stats(part), own_p, own_w)
@@ -293,20 +297,20 @@
     h, part = run(0, False, h, stats(part), p2, near)
     h, part = run(1, True, h, stats(part), p2, near)
     ret2 = moved(h, [(1, 2)])
-    mid = (mid, swapped(mid))
+    w35 = (w35, swapped(w35))
     part, p3 = stats(part, p3)
-    h, part = run(0, False, h, part, p3, mid)
-    h, part = run(1, True, h, stats(part), p3, mid)
+    h, part = run(0, False, h, part, p3, w35)
+    w3b = (w3b, swapped(w3b))
+    h, part = run(1, True, h, stats(part), p3, w3b)
     back3 = h
     w46 = (w46, swapped(w46))
     h, part = run(0, True, h, stats(part), p3, w46, 8)
-    w5s = swapped(w5)
     hopped = moved(h, [(1, 7)])
     part = moved(stats(part), [(1, 7)])
     ret3 = moved(back3, [(1, 3)])
     ret4 = moved(h, [(1, 4)])
     h, part = lax.optimization_barrier((hopped, part))
-    h, part = run(0, True, h, part, p3, (w5, w5s))
+    h, part = run(0, True, h, part, p3, w35)
     ret5 = moved(h, [(7, 5)])
     h, part = run(0, True, h, stats(part), p2, w46)
     ret6 = moved(h, [(7, 6)])

time: 246 us -> 268 us (1.089)
  blocking collectives: 62.5 us -> 31.4 us
  waiting for transfers between devices: 47.6 us -> 77.9 us
  starting transfers between devices: 81.1 us -> 93.1 us
  local copies, waits for them, and re-layouts: 12.4 us -> 18.9 us
  Pallas kernels: 37.9 us -> 41.5 us
    all_to_all x6 -> x2, blocking collectives: 48.6 us -> 17.6 us  [stats(): part = lax.all_to_all(part, ROW, 0, 0, tiled=True)]
    all_to_all x5 -> x9, waiting for transfers between devices: 16.5 us -> 37 us  [stats(): part = lax.all_to_all(part, ROW, 0, 0, tiled=True)]
    all_to_all x5 -> x9, starting transfers between devices: 16.7 us -> 31.2 us  [stats(): part = lax.all_to_all(part, ROW, 0, 0, tiled=True)]
    ppermute x20, waiting for transfers between devices: 28.2 us -> 38.1 us  [moved(): return lax.ppermute(value, axis, moves)]
    unnamed x41 -> x49, local copies, waits for them, and re-layouts: 11.1 us -> 17.6 us
    pallas_call x12, Pallas kernels: 33.5 us -> 37.1 us  [layer(): pl.pallas_call(functools.partial(layer_kernel, index, min(index, weights[...]
  transfers between devices with their start and end apart: 26 -> 30, of which waited for: 7 -> 11; matrix products, arithmetic and copies ran while one was open for 1% -> 1% of each run, Pallas kernels for 13% -> 12%
where the time goes in v4:
time: 268 us; the launch traced here: 266 us
  starting transfers between devices  93.1 us (35%)
  waiting for transfers between devices  77.9 us (29%)
  Pallas kernels  41.5 us (15%)
  blocking collectives  31.4 us (12%)
  local copies, waits for them, and re-layouts  18.9 us (7%)
    ppermute x20, starting transfers between devices, moved(): return lax.ppermute(value, axis, moves)  54.4 us
    ppermute x20, waiting for transfers between devices, moved(): return lax.ppermute(value, axis, moves)  38.1 us
    pallas_call x12, Pallas kernels, layer(): pl.pallas_call(functools.partial(layer_kernel, index, min(index, weights[...  37.1 us
    all_to_all x9, waiting for transfers between devices, stats(): part = lax.all_to_all(part, ROW, 0, 0, tiled=True)  37 us
    all_to_all x9, starting transfers between devices, stats(): part = lax.all_to_all(part, ROW, 0, 0, tiled=True)  31.2 us
    all_to_all x2, blocking collectives, stats(): part = lax.all_to_all(part, ROW, 0, 0, tiled=True)  17.6 us
    unnamed x49, local copies, waits for them, and re-layouts  17.6 us
    all_to_all x1, blocking collectives, program(): return lax.all_to_all(blocks, 'x', 0, 0, tiled=True)[None]  13.8 us
  transfers between devices with their start and end apart: 30, of which 11 were waited for; matrix products, arithmetic and copies ran while one was open for 1% of the time, Pallas kernels for 12%

profile of v4, /device:TPU:128, one launch (start us, length us, event | category | flops | bytes accessed | tf_op | source)
XLA Modules:
  0.0 266.2 jit_solution(9466390210919971729)
XLA Ops:
  2.3 7.5 %all-to-all-start = ((f32[32,1,256]{2,1,0:T(1,128)}), f32[32,1,256]{2,1,0:T(1,128)S(1)}, u32[]{:S(2)}, u32[]{:S(2)}) async-start(f32[32,1,256]{2,1,0:T(1,128)} %all_to_all.42), calls=%async_computation | async-start | bytes 65536 | tf_op jit(solution)/shard_map/all_to_all | solution.py:246
  22.4 3.3 %all-to-all-start.1 = ((f32[8,2,256]{2,1,0:T(2,128)}), f32[8,2,256]{2,1,0:T(2,128)S(1)}, u32[]{:S(2)}, u32[]{:S(2)}) async-start(f32[8,2,256]{2,1,0:T(2,128)} %get-tuple-element.58), calls=%async_computation.1 | async-start | bytes 32768 | tf_op jit(solution)/shard_map/all_to_all | solution.py:277
  27.8 3.3 %all-to-all-done.1.part_ref = f32[8,2,256]{2,1,0:T(2,128)S(1)} async-done(((f32[8,2,256]{2,1,0:T(2,128)}), f32[8,2,256]{2,1,0:T(2,128)S(1)}, u32[]{:S(2)}, u32[]{:S(2)}) %all-to-all-start.1) | async-done | bytes 16416 | tf_op jit(solution)/shard_map/all_to_all | solution.py:277
  32.3 2.8 %layer.13 = (bf16[4,288,256]{2,1,0:T(8,128)(2,1)S(1)}, f32[8,2,256]{2,1,0:T(2,128)}) custom-call(s32[1]{0:T(128)} %bitcast.11.core.half, f32[4,288,256]{2,1,0:T(8,128)S(1)} %copy-done.17, f32[8,2,256]{2,1,0:T(2,128)S(1)} %all-to-all-done.1.part_ref, f32[8,256]{1,0:T(8,128)S(1)} %concatenate.24.par_ref, f32[288,128]{1,0:T(8,128)S(1)} %get-tuple-element.55.valid_ref, ...), custom_call_target="tpu_custom_call" | custom-call | flops 1200000000 | bytes 4000000 | tf_op jit(solution)/shard_map/layer/pallas_call | solution.py:122
  35.2 3.3 %all-to-all-start.2 = ((f32[8,2,256]{2,1,0:T(2,128)}), f32[8,2,256]{2,1,0:T(2,128)S(1)}, u32[]{:S(2)}, u32[]{:S(2)}) async-start(f32[8,2,256]{2,1,0:T(2,128)} %get-tuple-element.61), calls=%async_computation.2 | async-start | bytes 32768 | tf_op jit(solution)/shard_map/all_to_all | solution.py:277
  40.0 3.8 %all-to-all-done.2 = f32[8,2,256]{2,1,0:T(2,128)S(1)} async-done(((f32[8,2,256]{2,1,0:T(2,128)}), f32[8,2,256]{2,1,0:T(2,128)S(1)}, u32[]{:S(2)}, u32[]{:S(2)}) %all-to-all-start.2) | async-done | bytes 16416 | tf_op jit(solution)/shard_map/all_to_all | solution.py:277
  47.5 35.7 %collective-permute-start.12 = (bf16[1,1152,256]{2,1,0:T(8,128)(2,1)}, bf16[1,1152,256]{2,1,0:T(8,128)(2,1)}, u32[]{:S(2)}, u32[]{:S(2)}) collective-permute-start(bf16[1,1152,256]{2,1,0:T(8,128)(2,1)} %get-tuple-element.80), channel_id=1, source_target_pairs={{128,32},{192,224},{129,33},{193,225},{130,34},{194,226},{131,35},... | collective-permute-start | bytes 1769480 | tf_op jit(solution)/shard_map/ppermute | solution.py:225
  83.2 3.9 %layer.14 = (f32[4,288,256]{2,1,0:T(8,128)S(1)}, f32[8,2,256]{2,1,0:T(2,128)}) custom-call(s32[1]{0:T(128)} %bitcast.11.core.half, bf16[4,288,256]{2,1,0:T(8,128)(2,1)} %collective-permute-done.h_ref, f32[8,2,256]{2,1,0:T(2,128)S(1)} %collective-permute-done.2.part_ref, f32[8,256]{1,0:T(8,128)S(1)} %concatenate.24.par_ref, ...), custom_call_target="tpu_custom_call" | custom-call | flops 1200000000 | bytes 4000000 | tf_op jit(solution)/shard_map/layer/pallas_call | solution.py:122
  88.1 4.5 %all-to-all-start.3 = ((f32[8,2,256]{2,1,0:T(2,128)}), f32[8,2,256]{2,1,0:T(2,128)S(1)}, u32[]{:S(2)}, u32[]{:S(2)}) async-start(f32[8,2,256]{2,1,0:T(2,128)} %get-tuple-element.68), calls=%async_computation.3 | async-start | bytes 32768 | tf_op jit(solution)/shard_map/all_to_all | solution.py:277
  93.2 4.8 %all-to-all-done.3.part_ref = f32[8,2,256]{2,1,0:T(2,128)S(1)} async-done(((f32[8,2,256]{2,1,0:T(2,128)}), f32[8,2,256]{2,1,0:T(2,128)S(1)}, u32[]{:S(2)}, u32[]{:S(2)}) %all-to-all-start.3) | async-done | bytes 16416 | tf_op jit(solution)/shard_map/all_to_all | solution.py:277
  99.3 2.8 %layer.15 = (bf16[4,288,256]{2,1,0:T(8,128)(2,1)S(1)}, f32[8,2,256]{2,1,0:T(2,128)}) custom-call(s32[1]{0:T(128)} %bitcast.11.core.half, f32[4,288,256]{2,1,0:T(8,128)S(1)} %copy-done.13, f32[8,2,256]{2,1,0:T(2,128)S(1)} %all-to-all-done.3.part_ref, f32[8,256]{1,0:T(8,128)S(1)} %concatenate.24.par_ref, f32[288,128]{1,0:T(8,128)S(1)} %get-tuple-element.55.valid_ref, ...), custom_call_target="tpu_custom_call" | custom-call | flops 1200000000 | bytes 4000000 | tf_op jit(solution)/shard_map/layer/pallas_call | solution.py:122
  103.0 3.3 %all-to-all-start.4 = ((f32[8,2,256]{2,1,0:T(2,128)}), f32[8,2,256]{2,1,0:T(2,128)S(1)}, u32[]{:S(2)}, u32[]{:S(2)}) async-start(f32[8,2,256]{2,1,0:T(2,128)} %get-tuple-element.70), calls=%async_computation.4 | async-start | bytes 32768 | tf_op jit(solution)/shard_map/all_to_all | solution.py:277
  106.8 4.9 %all-to-all-done.4.part_ref = f32[8,2,256]{2,1,0:T(2,128)S(1)} async-done(((f32[8,2,256]{2,1,0:T(2,128)}), f32[8,2,256]{2,1,0:T(2,128)S(1)}, u32[]{:S(2)}, u32[]{:S(2)}) %all-to-all-start.4) | async-done | bytes 16416 | tf_op jit(solution)/shard_map/all_to_all | solution.py:277
  112.7 3.2 %layer.16 = (f32[4,288,256]{2,1,0:T(8,128)S(1)}, f32[8,2,256]{2,1,0:T(2,128)}) custom-call(s32[1]{0:T(128)} %bitcast.11.core.half, bf16[4,288,256]{2,1,0:T(8,128)(2,1)S(1)} %copy-done.3, f32[8,2,256]{2,1,0:T(2,128)S(1)} %all-to-all-done.4.part_ref, f32[8,256]{1,0:T(8,128)S(1)} %collective-permute-done.1.par_ref, f32[288,128]{1,0:T(8,128)S(1)} %get-tuple-element.55.valid_ref, ...), custom_call_target="tpu_custom_call" | custom-call | flops 1200000000 | bytes 4000000 | tf_op jit(solution)/shard_map/layer/pallas_call | solution.py:122
  117.0 3.3 %all-to-all-start.5 = ((f32[8,2,256]{2,1,0:T(2,128)}), f32[8,2,256]{2,1,0:T(2,128)S(1)}, u32[]{:S(2)}, u32[]{:S(2)}) async-start(f32[8,2,256]{2,1,0:T(2,128)} %get-tuple-element.74), calls=%async_computation.5 | async-start | bytes 32768 | tf_op jit(solution)/shard_map/all_to_all | solution.py:277
  121.2 4.4 %all-to-all-done.5.part_ref = f32[8,2,256]{2,1,0:T(2,128)S(1)} async-done(((f32[8,2,256]{2,1,0:T(2,128)}), f32[8,2,256]{2,1,0:T(2,128)S(1)}, u32[]{:S(2)}, u32[]{:S(2)}) %all-to-all-start.5) | async-done | bytes 16416 | tf_op jit(solution)/shard_map/all_to_all | solution.py:277
  126.9 3.3 %layer.17 = (bf16[4,288,256]{2,1,0:T(8,128)(2,1)S(1)}, f32[8,2,256]{2,1,0:T(2,128)}) custom-call(s32[1]{0:T(128)} %bitcast.11.core.half, f32[4,288,256]{2,1,0:T(8,128)S(1)} %copy-done.15, f32[8,2,256]{2,1,0:T(2,128)S(1)} %all-to-all-done.5.part_ref, f32[8,256]{1,0:T(8,128)S(1)} %collective-permute-done.1.par_ref, ...), custom_call_target="tpu_custom_call" | custom-call | flops 1200000000 | bytes 4000000 | tf_op jit(solution)/shard_map/layer/pallas_call | solution.py:122
  131.0 3.3 %all-to-all-start.6 = ((f32[8,2,256]{2,1,0:T(2,128)}), f32[8,2,256]{2,1,0:T(2,128)S(1)}, u32[]{:S(2)}, u32[]{:S(2)}) async-start(f32[8,2,256]{2,1,0:T(2,128)} %get-tuple-element.78), calls=%async_computation.6 | async-start | bytes 32768 | tf_op jit(solution)/shard_map/all_to_all | solution.py:277
  134.4 5.3 %all-to-all-done.6.part_ref = f32[8,2,256]{2,1,0:T(2,128)S(1)} async-done(((f32[8,2,256]{2,1,0:T(2,128)}), f32[8,2,256]{2,1,0:T(2,128)S(1)}, u32[]{:S(2)}, u32[]{:S(2)}) %all-to-all-start.6) | async-done | bytes 16416 | tf_op jit(solution)/shard_map/all_to_all | solution.py:277
  140.7 3.2 %layer.18 = (f32[4,288,256]{2,1,0:T(8,128)S(1)}, f32[8,2,256]{2,1,0:T(2,128)}) custom-call(s32[1]{0:T(128)} %bitcast.11.core.half, bf16[4,288,256]{2,1,0:T(8,128)(2,1)S(1)} %copy-done.6, f32[8,2,256]{2,1,0:T(2,128)S(1)} %all-to-all-done.6.part_ref, f32[16,256]{1,0:T(8,128)S(1)} %collective-permute-done.6.par_ref, ...), custom_call_target="tpu_custom_call" | custom-call | flops 1200000000 | bytes 4000000 | tf_op jit(solution)/shard_map/layer/pallas_call | solution.py:122
  145.0 3.3 %all-to-all-start.7 = ((f32[8,2,256]{2,1,0:T(2,128)}), f32[8,2,256]{2,1,0:T(2,128)S(1)}, u32[]{:S(2)}, u32[]{:S(2)}) async-start(f32[8,2,256]{2,1,0:T(2,128)} %get-tuple-element.82), calls=%async_computation.7 | async-start | bytes 32768 | tf_op jit(solution)/shard_map/all_to_all | solution.py:277
  148.4 5.3 %all-to-all-done.7.part_ref = f32[8,2,256]{2,1,0:T(2,128)S(1)} async-done(((f32[8,2,256]{2,1,0:T(2,128)}), f32[8,2,256]{2,1,0:T(2,128)S(1)}, u32[]{:S(2)}, u32[]{:S(2)}) %all-to-all-start.7) | async-done | bytes 16416 | tf_op jit(solution)/shard_map/all_to_all | solution.py:277
  154.9 3.3 %layer.19 = (bf16[4,288,256]{2,1,0:T(8,128)(2,1)S(1)}, f32[8,2,256]{2,1,0:T(2,128)}) custom-call(s32[1]{0:T(128)} %bitcast.11.core.half, f32[4,288,256]{2,1,0:T(8,128)S(1)} %copy-done.19, f32[8,2,256]{2,1,0:T(2,128)S(1)} %all-to-all-done.7.part_ref, f32[16,256]{1,0:T(8,128)S(1)} %collective-permute-done.6.par_ref, ...), custom_call_target="tpu_custom_call" | custom-call | flops 1200000000 | bytes 4000000 | tf_op jit(solution)/shard_map/layer/pallas_call | solution.py:122
  159.0 3.3 %all-to-all-start.8 = ((f32[8,2,256]{2,1,0:T(2,128)}), f32[8,2,256]{2,1,0:T(2,128)S(1)}, u32[]{:S(2)}, u32[]{:S(2)}) async-start(f32[8,2,256]{2,1,0:T(2,128)} %get-tuple-element.85), calls=%async_computation.8 | async-start | bytes 32768 | tf_op jit(solution)/shard_map/all_to_all | solution.py:277
  162.4 5.3 %all-to-all-done.8.part_ref = f32[8,2,256]{2,1,0:T(2,128)S(1)} async-done(((f32[8,2,256]{2,1,0:T(2,128)}), f32[8,2,256]{2,1,0:T(2,128)S(1)}, u32[]{:S(2)}, u32[]{:S(2)}) %all-to-all-start.8) | async-done | bytes 16416 | tf_op jit(solution)/shard_map/all_to_all | solution.py:277
  172.1 7.7 %all_to_all.69 = f32[8,2,256]{2,1,0:T(2,128)S(1)} all-to-all(f32[8,2,256]{2,1,0:T(2,128)S(1)} %get-tuple-element.87), channel_id=1, replica_groups=mesh['z'=8,'y'=4,'x'=4,'c'=2] {'y','c'}, dimensions={0} | all-to-all | bytes 32768 | tf_op jit(solution)/shard_map/all_to_all | solution.py:277
  180.5 3.3 %layer.21 = (bf16[4,288,256]{2,1,0:T(8,128)(2,1)S(1)}, f32[8,2,256]{2,1,0:T(2,128)}) custom-call(s32[1]{0:T(128)} %bitcast.11.core.half, bf16[4,288,256]{2,1,0:T(8,128)(2,1)S(1)} %collective-permute-done.15.h_ref, f32[8,2,256]{2,1,0:T(2,128)S(1)} %collective-permute-done.16.part_ref, f32[16,256]{1,0:T(8,128)S(1)} %collective-permute-done.6.par_ref, ...), custom_call_target="tpu_custom_call" | custom-call | flops 1200000000 | bytes 4000000 | tf_op jit(solution)/shard_map/layer/pallas_call | solution.py:122
  184.6 3.3 %all-to-all-start.10 = ((f32[8,2,256]{2,1,0:T(2,128)}), f32[8,2,256]{2,1,0:T(2,128)S(1)}, u32[]{:S(2)}, u32[]{:S(2)}) async-start(f32[8,2,256]{2,1,0:T(2,128)} %get-tuple-element.91), calls=%async_computation.10 | async-start | bytes 32768 | tf_op jit(solution)/shard_map/all_to_all | solution.py:277
  198.2 9.9 %all_to_all.70.part_ref = f32[8,2,256]{2,1,0:T(2,128)S(1)} all-to-all(f32[8,2,256]{2,1,0:T(2,128)S(1)} %get-tuple-element.93), channel_id=1, replica_groups=mesh['z'=8,'y'=4,'x'=4,'c'=2] {'y','c'}, dimensions={0} | all-to-all | bytes 32768 | tf_op jit(solution)/shard_map/all_to_all | solution.py:277
  208.1 2.9 %layer.23 = (bf16[4,288,256]{2,1,0:T(8,128)(2,1)S(1)}, f32[8,2,256]{2,1,0:T(2,128)}) custom-call(s32[1]{0:T(128)} %bitcast.11.core.half, bf16[4,288,256]{2,1,0:T(8,128)(2,1)S(1)} %get-tuple-element.92.h_ref, f32[8,2,256]{2,1,0:T(2,128)S(1)} %all_to_all.70.part_ref, f32[8,256]{1,0:T(8,128)S(1)} %concatenate.24.par_ref, ...), custom_call_target="tpu_custom_call" | custom-call | flops 1200000000 | bytes 4000000 | tf_op jit(solution)/shard_map/layer/pallas_call | solution.py:122
  211.0 36.3 %collective-permute-done.14.refs_4_ = bf16[4,288,256]{2,1,0:T(8,128)(2,1)} collective-permute-done((bf16[4,288,256]{2,1,0:T(8,128)(2,1)}, bf16[4,288,256]{2,1,0:T(8,128)(2,1)}, u32[]{:S(2)}, u32[]{:S(2)}) %collective-permute-start.14) | collective-permute-done | bytes 589856 | tf_op jit(solution)/shard_map/ppermute | solution.py:225
  251.6 13.8 %all_to_all.71 = bf16[4,4,64,256]{3,2,1,0:T(8,128)(2,1)S(1)} all-to-all(bf16[4,4,64,256]{3,2,1,0:T(8,128)(2,1)S(1)} %maximum_select_fusion), channel_id=1, replica_groups=mesh['z'=8,'y'=4,'x'=4,'c'=2] {'x'}, dimensions={0} | all-to-all | bytes 1048576 | tf_op jit(solution)/shard_map/all_to_all | solution.py:323
  (125 shorter events, 57.6 us)
Async XLA Ops:
  0.0 13.8 %copy-start = (bf16[1,256,256]{2,1,0:T(8,128)(2,1)S(1)}, bf16[1,256,256]{2,1,0:T(8,128)(2,1)}, u32[]{:S(2)}) copy-start(bf16[1,256,256]{2,1,0:T(8,128)(2,1)} %param.15) | copy-start | bytes 393220
  2.3 14.9 %all-to-all-start = ((f32[32,1,256]{2,1,0:T(1,128)}), f32[32,1,256]{2,1,0:T(1,128)S(1)}, u32[]{:S(2)}, u32[]{:S(2)}) async-start(f32[32,1,256]{2,1,0:T(1,128)} %all_to_all.42), calls=%async_computation | async-start | bytes 65536 | tf_op jit(solution)/shard_map/all_to_all | solution.py:246
  11.9 6.4 %collective-permute-start.3 = (bf16[2,1152,256]{2,1,0:T(8,128)(2,1)}, bf16[2,1152,256]{2,1,0:T(8,128)(2,1)}, u32[]{:S(2)}, u32[]{:S(2)}) collective-permute-start(bf16[2,1152,256]{2,1,0:T(8,128)(2,1)} %get-tuple-element.72), channel_id=1, source_target_pairs={{64,32},{65,33},{66,34},{67,35},{68,36},{69,37},{70,38},{71,39},{7... | collective-permute-start | bytes 3538952 | tf_op jit(solution)/shard_map/ppermute | solution.py:225
  18.3 93.4 %collective-permute-start.4 = (bf16[2,1152,256]{2,1,0:T(8,128)(2,1)}, bf16[2,1152,256]{2,1,0:T(8,128)(2,1)}, u32[]{:S(2)}, u32[]{:S(2)}) collective-permute-start(bf16[2,1152,256]{2,1,0:T(8,128)(2,1)} %collective-permute-done.3.refs_0_), channel_id=1, source_target_pairs={{0,1},{1,0},{2,3},{3,2},{4,5},{5,4},{6,7},{7,6},{8,9},{9,8},{10,11... | collective-permute-start | bytes 3538952 | tf_op jit(solution)/shard_map/ppermute | solution.py:225
  22.4 8.6 %all-to-all-start.1 = ((f32[8,2,256]{2,1,0:T(2,128)}), f32[8,2,256]{2,1,0:T(2,128)S(1)}, u32[]{:S(2)}, u32[]{:S(2)}) async-start(f32[8,2,256]{2,1,0:T(2,128)} %get-tuple-element.58), calls=%async_computation.1 | async-start | bytes 32768 | tf_op jit(solution)/shard_map/all_to_all | solution.py:277
  25.8 9.4 %collective-permute-start.1 = (f32[8,256]{1,0:T(8,128)S(1)}, f32[8,256]{1,0:T(8,128)S(1)}, u32[]{:S(2)}, u32[]{:S(2)}) collective-permute-start(f32[8,256]{1,0:T(8,128)S(1)} %concatenate.24.par_ref), channel_id=1, source_target_pairs={{64,32},{192,224},{128,96},{65,33},{193,225},{129,97},{66,34},{194... | collective-permute-start | bytes 24584 | tf_op jit(solution)/shard_map/ppermute | solution.py:225
  35.2 8.6 %all-to-all-start.2 = ((f32[8,2,256]{2,1,0:T(2,128)}), f32[8,2,256]{2,1,0:T(2,128)S(1)}, u32[]{:S(2)}, u32[]{:S(2)}) async-start(f32[8,2,256]{2,1,0:T(2,128)} %get-tuple-element.61), calls=%async_computation.2 | async-start | bytes 32768 | tf_op jit(solution)/shard_map/all_to_all | solution.py:277
  38.5 44.6 %collective-permute-start = (bf16[4,288,256]{2,1,0:T(8,128)(2,1)S(1)}, bf16[4,288,256]{2,1,0:T(8,128)(2,1)}, u32[]{:S(2)}, u32[]{:S(2)}) collective-permute-start(bf16[4,288,256]{2,1,0:T(8,128)(2,1)S(1)} %get-tuple-element.59.refs_0_), channel_id=1, source_target_pairs={{0,32},{1,33},{2,34},{3,35},{4,36},{5,37},{6,38},{7,39},{8,40},{9,... | collective-permute-start | bytes 1769480 | tf_op jit(solution)/shard_map/ppermute | solution.py:225
  43.8 39.4 %collective-permute-start.7 = (bf16[1,1152,256]{2,1,0:T(8,128)(2,1)}, bf16[1,1152,256]{2,1,0:T(8,128)(2,1)}, u32[]{:S(2)}, u32[]{:S(2)}) collective-permute-start(bf16[1,1152,256]{2,1,0:T(8,128)(2,1)} %get-tuple-element.80), channel_id=1, source_target_pairs={{96,32},{160,224},{97,33},{161,225},{98,34},{162,226},{99,35},{163... | collective-permute-start | bytes 1769480 | tf_op jit(solution)/shard_map/ppermute | solution.py:225
  45.3 47.4 %collective-permute-start.9 = (bf16[1,1152,256]{2,1,0:T(8,128)(2,1)}, bf16[1,1152,256]{2,1,0:T(8,128)(2,1)}, u32[]{:S(2)}, u32[]{:S(2)}) collective-permute-start(bf16[1,1152,256]{2,1,0:T(8,128)(2,1)} %get-tuple-element.83), channel_id=1, source_target_pairs={{96,32},{97,33},{98,34},{99,35},{100,36},{101,37},{102,38},{103,39... | collective-permute-start | bytes 1769480 | tf_op jit(solution)/shard_map/ppermute | solution.py:225
  46.8 0.7 collective-permute-start.2
  47.5 58.9 %collective-permute-start.12 = (bf16[1,1152,256]{2,1,0:T(8,128)(2,1)}, bf16[1,1152,256]{2,1,0:T(8,128)(2,1)}, u32[]{:S(2)}, u32[]{:S(2)}) collective-permute-start(bf16[1,1152,256]{2,1,0:T(8,128)(2,1)} %get-tuple-element.80), channel_id=1, source_target_pairs={{128,32},{192,224},{129,33},{193,225},{130,34},{194,226},{131,35},... | collective-permute-start | bytes 1769480 | tf_op jit(solution)/shard_map/ppermute | solution.py:225
  83.2 51.2 %collective-permute-start.8 = (bf16[1,1152,256]{2,1,0:T(8,128)(2,1)}, bf16[1,1152,256]{2,1,0:T(8,128)(2,1)}, u32[]{:S(2)}, u32[]{:S(2)}) collective-permute-start(bf16[1,1152,256]{2,1,0:T(8,128)(2,1)} %collective-permute-done.7.refs_0_), channel_id=1, source_target_pairs={{0,1},{1,0},{2,3},{3,2},{4,5},{5,4},{6,7},{7,6},{8,9},{9,8},{10,11... | collective-permute-start | bytes 1769480 | tf_op jit(solution)/shard_map/ppermute | solution.py:225
  88.1 9.9 %all-to-all-start.3 = ((f32[8,2,256]{2,1,0:T(2,128)}), f32[8,2,256]{2,1,0:T(2,128)S(1)}, u32[]{:S(2)}, u32[]{:S(2)}) async-start(f32[8,2,256]{2,1,0:T(2,128)} %get-tuple-element.68), calls=%async_computation.3 | async-start | bytes 32768 | tf_op jit(solution)/shard_map/all_to_all | solution.py:277
  92.7 55.7 %collective-permute-start.10 = (bf16[1,1152,256]{2,1,0:T(8,128)(2,1)}, bf16[1,1152,256]{2,1,0:T(8,128)(2,1)}, u32[]{:S(2)}, u32[]{:S(2)}) collective-permute-start(bf16[1,1152,256]{2,1,0:T(8,128)(2,1)} %collective-permute-done.9.refs_0_), channel_id=1, source_target_pairs={{0,1},{1,0},{2,3},{3,2},{4,5},{5,4},{6,7},{7,6},{8,9},{9,8},{10,11... | collective-permute-start | bytes 1769480 | tf_op jit(solution)/shard_map/ppermute | solution.py:225
  103.0 8.6 %all-to-all-start.4 = ((f32[8,2,256]{2,1,0:T(2,128)}), f32[8,2,256]{2,1,0:T(2,128)S(1)}, u32[]{:S(2)}, u32[]{:S(2)}) async-start(f32[8,2,256]{2,1,0:T(2,128)} %get-tuple-element.70), calls=%async_computation.4 | async-start | bytes 32768 | tf_op jit(solution)/shard_map/all_to_all | solution.py:277
  106.4 56.0 %collective-permute-start.13 = (bf16[1,1152,256]{2,1,0:T(8,128)(2,1)}, bf16[1,1152,256]{2,1,0:T(8,128)(2,1)}, u32[]{:S(2)}, u32[]{:S(2)}) collective-permute-start(bf16[1,1152,256]{2,1,0:T(8,128)(2,1)} %collective-permute-done.12.refs_0_), channel_id=1, source_target_pairs={{0,1},{1,0},{2,3},{3,2},{4,5},{5,4},{6,7},{7,6},{8,9},{9,8},{10,11... | collective-permute-start | bytes 1769480 | tf_op jit(solution)/shard_map/ppermute | solution.py:225
  117.0 8.6 %all-to-all-start.5 = ((f32[8,2,256]{2,1,0:T(2,128)}), f32[8,2,256]{2,1,0:T(2,128)S(1)}, u32[]{:S(2)}, u32[]{:S(2)}) async-start(f32[8,2,256]{2,1,0:T(2,128)} %get-tuple-element.74), calls=%async_computation.5 | async-start | bytes 32768 | tf_op jit(solution)/shard_map/all_to_all | solution.py:277
  120.3 10.7 %collective-permute-start.6 = (f32[16,256]{1,0:T(8,128)S(1)}, f32[16,256]{1,0:T(8,128)S(1)}, u32[]{:S(2)}, u32[]{:S(2)}) collective-permute-start(f32[16,256]{1,0:T(8,128)S(1)} %pad_maximum_fusion), channel_id=1, source_target_pairs={{96,32},{160,224},{97,33},{161,225},{98,34},{162,226},{99,35},{163... | collective-permute-start | bytes 49160 | tf_op jit(solution)/shard_map/ppermute | solution.py:225
  131.0 8.6 %all-to-all-start.6 = ((f32[8,2,256]{2,1,0:T(2,128)}), f32[8,2,256]{2,1,0:T(2,128)S(1)}, u32[]{:S(2)}, u32[]{:S(2)}) async-start(f32[8,2,256]{2,1,0:T(2,128)} %get-tuple-element.78), calls=%async_computation.6 | async-start | bytes 32768 | tf_op jit(solution)/shard_map/all_to_all | solution.py:277
  145.0 8.6 %all-to-all-start.7 = ((f32[8,2,256]{2,1,0:T(2,128)}), f32[8,2,256]{2,1,0:T(2,128)S(1)}, u32[]{:S(2)}, u32[]{:S(2)}) async-start(f32[8,2,256]{2,1,0:T(2,128)} %get-tuple-element.82), calls=%async_computation.7 | async-start | bytes 32768 | tf_op jit(solution)/shard_map/all_to_all | solution.py:277
  159.0 8.6 %all-to-all-start.8 = ((f32[8,2,256]{2,1,0:T(2,128)}), f32[8,2,256]{2,1,0:T(2,128)S(1)}, u32[]{:S(2)}, u32[]{:S(2)}) async-start(f32[8,2,256]{2,1,0:T(2,128)} %get-tuple-element.85), calls=%async_computation.8 | async-start | bytes 32768 | tf_op jit(solution)/shard_map/all_to_all | solution.py:277
  171.4 9.1 %collective-permute-start.15 = (bf16[4,288,256]{2,1,0:T(8,128)(2,1)S(1)}, bf16[4,288,256]{2,1,0:T(8,128)(2,1)S(1)}, u32[]{:S(2)}, u32[]{:S(2)}) collective-permute-start(bf16[4,288,256]{2,1,0:T(8,128)(2,1)S(1)} %get-tuple-element.86), channel_id=1, source_target_pairs={{32,224},{33,225},{34,226},{35,227},{36,228},{37,229},{38,230},{39... | collective-permute-start | bytes 1769480 | tf_op jit(solution)/shard_map/ppermute | solution.py:225
  179.8 0.7 collective-permute-start.16
  184.6 9.1 %all-to-all-start.10 = ((f32[8,2,256]{2,1,0:T(2,128)}), f32[8,2,256]{2,1,0:T(2,128)S(1)}, u32[]{:S(2)}, u32[]{:S(2)}) async-start(f32[8,2,256]{2,1,0:T(2,128)} %get-tuple-element.91), calls=%async_computation.10 | async-start | bytes 32768 | tf_op jit(solution)/shard_map/all_to_all | solution.py:277
  188.0 23.0 %collective-permute-start.5 = (bf16[4,288,256]{2,1,0:T(8,128)(2,1)}, bf16[4,288,256]{2,1,0:T(8,128)(2,1)}, u32[]{:S(2)}, u32[]{:S(2)}) collective-permute-start(bf16[4,288,256]{2,1,0:T(8,128)(2,1)} %copy-done.5), channel_id=1, source_target_pairs={{32,64},{33,65},{34,66},{35,67},{36,68},{37,69},{38,70},{39,71},{4... | collective-permute-start | bytes 1769480 | tf_op jit(solution)/shard_map/ppermute | solution.py:225
  189.5 21.5 %collective-permute-start.11 = (bf16[4,288,256]{2,1,0:T(8,128)(2,1)}, bf16[4,288,256]{2,1,0:T(8,128)(2,1)}, u32[]{:S(2)}, u32[]{:S(2)}) collective-permute-start(bf16[4,288,256]{2,1,0:T(8,128)(2,1)} %copy-done.7), channel_id=1, source_target_pairs={{32,96},{33,97},{34,98},{35,99},{36,100},{37,101},{38,102},{39,103... | collective-permute-start | bytes 1769480 | tf_op jit(solution)/shard_map/ppermute | solution.py:225
  191.0 56.3 %collective-permute-start.14 = (bf16[4,288,256]{2,1,0:T(8,128)(2,1)}, bf16[4,288,256]{2,1,0:T(8,128)(2,1)}, u32[]{:S(2)}, u32[]{:S(2)}) collective-permute-start(bf16[4,288,256]{2,1,0:T(8,128)(2,1)} %copy-done.9), channel_id=1, source_target_pairs={{32,128},{33,129},{34,130},{35,131},{36,132},{37,133},{38,134},{39... | collective-permute-start | bytes 1769480 | tf_op jit(solution)/shard_map/ppermute | solution.py:225
  192.3 55.1 %collective-permute-start.17 = (bf16[4,288,256]{2,1,0:T(8,128)(2,1)}, bf16[4,288,256]{2,1,0:T(8,128)(2,1)}, u32[]{:S(2)}, u32[]{:S(2)}) collective-permute-start(bf16[4,288,256]{2,1,0:T(8,128)(2,1)} %copy-done.10), channel_id=1, source_target_pairs={{224,160},{225,161},{226,162},{227,163},{228,164},{229,165},{230,1... | collective-permute-start | bytes 1769480 | tf_op jit(solution)/shard_map/ppermute | solution.py:225
  197.5 49.8 %collective-permute-start.18 = (bf16[4,288,256]{2,1,0:T(8,128)(2,1)S(1)}, bf16[4,288,256]{2,1,0:T(8,128)(2,1)S(1)}, u32[]{:S(2)}, u32[]{:S(2)}) collective-permute-start(bf16[4,288,256]{2,1,0:T(8,128)(2,1)S(1)} %get-tuple-element.92.h_ref), channel_id=1, source_target_pairs={{224,192},{225,193},{226,194},{227,195},{228,196},{229,197},{230,1... | collective-permute-start | bytes 1769480 | tf_op jit(solution)/shard_map/ppermute | solution.py:225
  208.1 39.2 %copy-start.4 = (bf16[4,288,256]{2,1,0:T(8,128)(2,1)S(1)}, bf16[4,288,256]{2,1,0:T(8,128)(2,1)}, u32[]{:S(2)}) copy-start(bf16[4,288,256]{2,1,0:T(8,128)(2,1)} %copy-done.2) | copy-start | bytes 1769476
  249.7 1.8 collective-permute-start.19
  (22 other events, 57.8 us)

commit v5 on v4

--- a/solution.py
+++ b/solution.py
@@ -34,7 +34,7 @@
     return x
 
 
-def layer_kernel(index, slot, base, first, last, split, core, h_ref, part_ref, par_ref, valid_ref, own_ref, *refs):
+def layer_kernel(level_plane, index, slot, base, first, last, split, plane, core, h_ref, part_ref, par_ref, valid_ref, own_ref, *refs):
     weights, rest = refs[: 1 + split], refs[1 + split :]
     out_ref, sums_ref = rest[:2]
     act, w_ref, sem = rest[2:]
@@ -83,7 +83,7 @@
                 act[f, ROWS - STRIPS : ROWS, 2 * C : 3 * C] = pltpu.roll(a[:STRIPS], STRIPS - 1, 0).astype(jnp.bfloat16)
         return 0
 
-    lax.fori_loop(0, FR, activate, 0)
+    lax.fori_loop(0, jnp.where(plane[0] == level_plane, FR, 0), activate, 0)
     for fetch in fetches:
         fetch.wait()
     total = jnp.zeros((8, C), jnp.float32)
@@ -112,7 +112,7 @@
         sums_ref[n] = sums
 
 
-def layer(index, base, first, last, core, h, part, par, valid, own, weights):
+def layer(level_plane, index, base, first, last, plane, core, h, part, par, valid, own, weights):
     vmem = pl.BlockSpec(memory_space=pltpu.VMEM)
     hbm = pl.BlockSpec(memory_space=pltpu.HBM)
     out_shape = [
@@ -120,9 +120,9 @@
         jax.ShapeDtypeStruct((NY * NC, 2, C), jnp.float32),
     ]
     return pl.pallas_call(
-        functools.partial(layer_kernel, index, min(index, weights[0].shape[0] - 1), base, first, last, len(weights) - 1),
+        functools.partial(layer_kernel, level_plane, index, min(index, weights[0].shape[0] - 1), base, first, last, len(weights) - 1),
         out_shape=tuple(out_shape),
-        in_specs=[pl.BlockSpec(memory_space=pltpu.SMEM)] + [vmem] * 5 + [hbm] * len(weights),
+        in_specs=[pl.BlockSpec(memory_space=pltpu.SMEM)] * 2 + [vmem] * 5 + [hbm] * len(weights),
         out_specs=(vmem, vmem),
         scratch_shapes=[
             pltpu.VMEM((FR, ROWS, 3 * C), jnp.bfloat16),
@@ -132,7 +132,7 @@
         compiler_params=pltpu.CompilerParams(vmem_limit_bytes=16 * 1024 * 1024),
         cost_estimate=pl.CostEstimate(flops=1200000000, bytes_accessed=4000000, transcendentals=300000),
         name="layer",
-    )(core, h, part, par, valid, own, *weights)
+    )(plane, core, h, part, par, valid, own, *weights)
 
 
 def ordered_kernel(plane, half, *refs):
@@ -269,8 +269,8 @@
     p2 = moved(own_p, [(2, 1), (6, 7), (4, 3)])
     h, part, valid, own, own_p, core = lax.optimization_barrier((h, part, valid, own, own_p, core))
 
-    def run(index, last, h, part, p, weights, base=0):
-        return layer(index, base, index == 0, last, core, h, part, p, valid, own, weights)
+    def run(n, index, last, h, part, p, weights, base=0):
+        return layer(0 if n < 2 else 1 if n < 9 else 7, index, base, index == 0, last, plane, core, h, part, p, valid, own, weights)
 
     def stats(part, *settled):
         part, *settled = lax.optimization_barrier((part, *settled))
@@ -278,8 +278,8 @@
         return (part, *settled) if settled else part
 
     own_w = (own_w,)
-    h, part = run(0, False, h, part, own_p, own_w)
-    h, part = run(1, True, h, stats(part), own_p, own_w)
+    h, part = run(0, 0, False, h, part, own_p, own_w)
+    h, part = run(1, 1, True, h, stats(part), own_p, own_w)
     ret0 = h
     hopped = moved(h, [(0, 1)])
     part, p2 = stats(part, p2)
@@ -290,31 +290,31 @@
     w3b = moved(other, [(3, 1)])
     w46 = moved(one, [(4, 1), (6, 7)])
     h, part = lax.optimization_barrier((hopped, part))
-    h, part = run(0, False, h, part, own_p, own_w)
-    h, part = run(1, True, h, stats(part), own_p, own_w)
+    h, part = run(2, 0, False, h, part, own_p, own_w)
+    h, part = run(3, 1, True, h, stats(part), own_p, own_w)
     ret1 = h
     near = (near, swapped(near))
-    h, part = run(0, False, h, stats(part), p2, near)
-    h, part = run(1, True, h, stats(part), p2, near)
+    h, part = run(4, 0, False, h, stats(part), p2, near)
+    h, part = run(5, 1, True, h, stats(part), p2, near)
     ret2 = moved(h, [(1, 2)])
     w35 = (w35, swapped(w35))
     part, p3 = stats(part, p3)
-    h, part = run(0, False, h, part, p3, w35)
+    h, part = run(6, 0, False, h, part, p3, w35)
     w3b = (w3b, swapped(w3b))
-    h, part = run(1, True, h, stats(part), p3, w3b)
+    h, part = run(7, 1, True, h, stats(part), p3, w3b)
     back3 = h
     w46 = (w46, swapped(w46))
-    h, part = run(0, True, h, stats(part), p3, w46, 8)
+    h, part = run(8, 0, True, h, stats(part), p3, w46, 8)
     hopped = moved(h, [(1, 7)])
     part = moved(stats(part), [(1, 7)])
     ret3 = moved(back3, [(1, 3)])
     ret4 = moved(h, [(1, 4)])
     h, part = lax.optimization_barrier((hopped, part))
-    h, part = run(0, True, h, part, p3, w35)
+    h, part = run(9, 0, True, h, part, p3, w35)
     ret5 = moved(h, [(7, 5)])
-    h, part = run(0, True, h, stats(part), p2, w46)
+    h, part = run(10, 0, True, h, stats(part), p2, w46)
     ret6 = moved(h, [(7, 6)])
-    h, part = run(0, True, h, stats(part), own_p, own_w)
+    h, part = run(11, 0, True, h, stats(part), own_p, own_w)
     ret7 = h
 
     keep, send = ordered(plane, core, [ret0, ret1, ret2, ret3, ret4, ret5, ret6, ret7])

time: 268 us -> 267 us (level)
  no operation moved by 1% of the time
where the time goes in v5:
time: 267 us; the launch traced here: 266 us
  starting transfers between devices  92.9 us (35%)
  waiting for transfers between devices  79.2 us (30%)
  Pallas kernels  39.7 us (15%)
  blocking collectives  31.4 us (12%)
  local copies, waits for them, and re-layouts  18.9 us (7%)
    ppermute x20, starting transfers between devices, moved(): return lax.ppermute(value, axis, moves)  54.2 us
    ppermute x20, waiting for transfers between devices, moved(): return lax.ppermute(value, axis, moves)  39.2 us
    all_to_all x9, waiting for transfers between devices, stats(): part = lax.all_to_all(part, ROW, 0, 0, tiled=True)  37.2 us
    pallas_call x12, Pallas kernels, layer(): pl.pallas_call(functools.partial(layer_kernel, level_plane, index, min(in...  35.3 us
    all_to_all x9, starting transfers between devices, stats(): part = lax.all_to_all(part, ROW, 0, 0, tiled=True)  31.2 us
    all_to_all x2, blocking collectives, stats(): part = lax.all_to_all(part, ROW, 0, 0, tiled=True)  17.6 us
    unnamed x49, local copies, waits for them, and re-layouts  17.6 us
    all_to_all x1, blocking collectives, program(): return lax.all_to_all(blocks, 'x', 0, 0, tiled=True)[None]  13.8 us
  transfers between devices with their start and end apart: 30, of which 11 were waited for; matrix products, arithmetic and copies ran while one was open for 1% of the time, Pallas kernels for 12%

profile of v5, /device:TPU:128, one launch (start us, length us, event | category | flops | bytes accessed | tf_op | source)
XLA Modules:
  0.0 265.5 jit_solution(12767576170791551361)
XLA Ops:
  2.3 7.5 %all-to-all-start = ((f32[32,1,256]{2,1,0:T(1,128)}), f32[32,1,256]{2,1,0:T(1,128)S(1)}, u32[]{:S(2)}, u32[]{:S(2)}) async-start(f32[32,1,256]{2,1,0:T(1,128)} %all_to_all.42), calls=%async_computation | async-start | bytes 65536 | tf_op jit(solution)/shard_map/all_to_all | solution.py:246
  14.3 2.8 %all-to-all-done = f32[32,1,256]{2,1,0:T(1,128)S(1)} async-done(((f32[32,1,256]{2,1,0:T(1,128)}), f32[32,1,256]{2,1,0:T(1,128)S(1)}, u32[]{:S(2)}, u32[]{:S(2)}) %all-to-all-start) | async-done | bytes 32800 | tf_op jit(solution)/shard_map/all_to_all | solution.py:246
  22.0 3.3 %all-to-all-start.1 = ((f32[8,2,256]{2,1,0:T(2,128)}), f32[8,2,256]{2,1,0:T(2,128)S(1)}, u32[]{:S(2)}, u32[]{:S(2)}) async-start(f32[8,2,256]{2,1,0:T(2,128)} %get-tuple-element.58), calls=%async_computation.1 | async-start | bytes 32768 | tf_op jit(solution)/shard_map/all_to_all | solution.py:277
  27.4 3.3 %all-to-all-done.1.part_ref = f32[8,2,256]{2,1,0:T(2,128)S(1)} async-done(((f32[8,2,256]{2,1,0:T(2,128)}), f32[8,2,256]{2,1,0:T(2,128)S(1)}, u32[]{:S(2)}, u32[]{:S(2)}) %all-to-all-start.1) | async-done | bytes 16416 | tf_op jit(solution)/shard_map/all_to_all | solution.py:277
  34.5 3.3 %all-to-all-start.2 = ((f32[8,2,256]{2,1,0:T(2,128)}), f32[8,2,256]{2,1,0:T(2,128)S(1)}, u32[]{:S(2)}, u32[]{:S(2)}) async-start(f32[8,2,256]{2,1,0:T(2,128)} %get-tuple-element.61), calls=%async_computation.2 | async-start | bytes 32768 | tf_op jit(solution)/shard_map/all_to_all | solution.py:277
  39.3 3.8 %all-to-all-done.2 = f32[8,2,256]{2,1,0:T(2,128)S(1)} async-done(((f32[8,2,256]{2,1,0:T(2,128)}), f32[8,2,256]{2,1,0:T(2,128)S(1)}, u32[]{:S(2)}, u32[]{:S(2)}) %all-to-all-start.2) | async-done | bytes 16416 | tf_op jit(solution)/shard_map/all_to_all | solution.py:277
  46.7 35.7 %collective-permute-start.12 = (bf16[1,1152,256]{2,1,0:T(8,128)(2,1)}, bf16[1,1152,256]{2,1,0:T(8,128)(2,1)}, u32[]{:S(2)}, u32[]{:S(2)}) collective-permute-start(bf16[1,1152,256]{2,1,0:T(8,128)(2,1)} %get-tuple-element.80), channel_id=1, source_target_pairs={{128,32},{192,224},{129,33},{193,225},{130,34},{194,226},{131,35},... | collective-permute-start | bytes 1769480 | tf_op jit(solution)/shard_map/ppermute | solution.py:225
  82.5 3.5 %layer.14 = (f32[4,288,256]{2,1,0:T(8,128)S(1)}, f32[8,2,256]{2,1,0:T(2,128)}) custom-call(s32[1]{0:T(128)} %bitcast.plane, s32[1]{0:T(128)} %bitcast.11.core.half, bf16[4,288,256]{2,1,0:T(8,128)(2,1)} %collective-permute-done.h_ref, f32[8,2,256]{2,1,0:T(2,128)S(1)} %collective-permute-done.2.part_ref, f32[8,256]{1,0:T(8,128)S(1)} %concatenate.24.par_ref, ...), custom_call_target="tpu_custom_call" | custom-call | flops 1200000000 | bytes 4000000 | tf_op jit(solution)/shard_map/layer/pallas_call | solution.py:122
  87.0 4.5 %all-to-all-start.3 = ((f32[8,2,256]{2,1,0:T(2,128)}), f32[8,2,256]{2,1,0:T(2,128)S(1)}, u32[]{:S(2)}, u32[]{:S(2)}) async-start(f32[8,2,256]{2,1,0:T(2,128)} %get-tuple-element.68), calls=%async_computation.3 | async-start | bytes 32768 | tf_op jit(solution)/shard_map/all_to_all | solution.py:277
  92.1 4.8 %all-to-all-done.3.part_ref = f32[8,2,256]{2,1,0:T(2,128)S(1)} async-done(((f32[8,2,256]{2,1,0:T(2,128)}), f32[8,2,256]{2,1,0:T(2,128)S(1)}, u32[]{:S(2)}, u32[]{:S(2)}) %all-to-all-start.3) | async-done | bytes 16416 | tf_op jit(solution)/shard_map/all_to_all | solution.py:277
  101.6 3.3 %all-to-all-start.4 = ((f32[8,2,256]{2,1,0:T(2,128)}), f32[8,2,256]{2,1,0:T(2,128)S(1)}, u32[]{:S(2)}, u32[]{:S(2)}) async-start(f32[8,2,256]{2,1,0:T(2,128)} %get-tuple-element.70), calls=%async_computation.4 | async-start | bytes 32768 | tf_op jit(solution)/shard_map/all_to_all | solution.py:277
  105.3 4.9 %all-to-all-done.4.part_ref = f32[8,2,256]{2,1,0:T(2,128)S(1)} async-done(((f32[8,2,256]{2,1,0:T(2,128)}), f32[8,2,256]{2,1,0:T(2,128)S(1)}, u32[]{:S(2)}, u32[]{:S(2)}) %all-to-all-start.4) | async-done | bytes 16416 | tf_op jit(solution)/shard_map/all_to_all | solution.py:277
  111.3 3.2 %layer.16 = (f32[4,288,256]{2,1,0:T(8,128)S(1)}, f32[8,2,256]{2,1,0:T(2,128)}) custom-call(s32[1]{0:T(128)} %bitcast.plane, s32[1]{0:T(128)} %bitcast.11.core.half, bf16[4,288,256]{2,1,0:T(8,128)(2,1)S(1)} %copy-done.3, f32[8,2,256]{2,1,0:T(2,128)S(1)} %all-to-all-done.4.part_ref, f32[8,256]{1,0:T(8,128)S(1)} %collective-permute-done.1.par_ref, ...), custom_call_target="tpu_custom_call" | custom-call | flops 1200000000 | bytes 4000000 | tf_op jit(solution)/shard_map/layer/pallas_call | solution.py:122
  115.6 3.3 %all-to-all-start.5 = ((f32[8,2,256]{2,1,0:T(2,128)}), f32[8,2,256]{2,1,0:T(2,128)S(1)}, u32[]{:S(2)}, u32[]{:S(2)}) async-start(f32[8,2,256]{2,1,0:T(2,128)} %get-tuple-element.74), calls=%async_computation.5 | async-start | bytes 32768 | tf_op jit(solution)/shard_map/all_to_all | solution.py:277
  119.6 4.6 %all-to-all-done.5.part_ref = f32[8,2,256]{2,1,0:T(2,128)S(1)} async-done(((f32[8,2,256]{2,1,0:T(2,128)}), f32[8,2,256]{2,1,0:T(2,128)S(1)}, u32[]{:S(2)}, u32[]{:S(2)}) %all-to-all-start.5) | async-done | bytes 16416 | tf_op jit(solution)/shard_map/all_to_all | solution.py:277
  125.4 3.3 %layer.17 = (bf16[4,288,256]{2,1,0:T(8,128)(2,1)S(1)}, f32[8,2,256]{2,1,0:T(2,128)}) custom-call(s32[1]{0:T(128)} %bitcast.plane, s32[1]{0:T(128)} %bitcast.11.core.half, f32[4,288,256]{2,1,0:T(8,128)S(1)} %copy-done.15, f32[8,2,256]{2,1,0:T(2,128)S(1)} %all-to-all-done.5.part_ref, f32[8,256]{1,0:T(8,128)S(1)} %collective-permute-done.1.par_ref, ...), custom_call_target="tpu_custom_call" | custom-call | flops 1200000000 | bytes 4000000 | tf_op jit(solution)/shard_map/layer/pallas_call | solution.py:122
  129.6 3.3 %all-to-all-start.6 = ((f32[8,2,256]{2,1,0:T(2,128)}), f32[8,2,256]{2,1,0:T(2,128)S(1)}, u32[]{:S(2)}, u32[]{:S(2)}) async-start(f32[8,2,256]{2,1,0:T(2,128)} %get-tuple-element.78), calls=%async_computation.6 | async-start | bytes 32768 | tf_op jit(solution)/shard_map/all_to_all | solution.py:277
  133.0 5.3 %all-to-all-done.6.part_ref = f32[8,2,256]{2,1,0:T(2,128)S(1)} async-done(((f32[8,2,256]{2,1,0:T(2,128)}), f32[8,2,256]{2,1,0:T(2,128)S(1)}, u32[]{:S(2)}, u32[]{:S(2)}) %all-to-all-start.6) | async-done | bytes 16416 | tf_op jit(solution)/shard_map/all_to_all | solution.py:277
  139.3 3.2 %layer.18 = (f32[4,288,256]{2,1,0:T(8,128)S(1)}, f32[8,2,256]{2,1,0:T(2,128)}) custom-call(s32[1]{0:T(128)} %bitcast.plane, s32[1]{0:T(128)} %bitcast.11.core.half, bf16[4,288,256]{2,1,0:T(8,128)(2,1)S(1)} %copy-done.6, f32[8,2,256]{2,1,0:T(2,128)S(1)} %all-to-all-done.6.part_ref, f32[16,256]{1,0:T(8,128)S(1)} %collective-permute-done.6.par_ref, ...), custom_call_target="tpu_custom_call" | custom-call | flops 1200000000 | bytes 4000000 | tf_op jit(solution)/shard_map/layer/pallas_call | solution.py:122
  143.6 3.3 %all-to-all-start.7 = ((f32[8,2,256]{2,1,0:T(2,128)}), f32[8,2,256]{2,1,0:T(2,128)S(1)}, u32[]{:S(2)}, u32[]{:S(2)}) async-start(f32[8,2,256]{2,1,0:T(2,128)} %get-tuple-element.82), calls=%async_computation.7 | async-start | bytes 32768 | tf_op jit(solution)/shard_map/all_to_all | solution.py:277
  146.9 5.3 %all-to-all-done.7.part_ref = f32[8,2,256]{2,1,0:T(2,128)S(1)} async-done(((f32[8,2,256]{2,1,0:T(2,128)}), f32[8,2,256]{2,1,0:T(2,128)S(1)}, u32[]{:S(2)}, u32[]{:S(2)}) %all-to-all-start.7) | async-done | bytes 16416 | tf_op jit(solution)/shard_map/all_to_all | solution.py:277
  153.5 3.3 %layer.19 = (bf16[4,288,256]{2,1,0:T(8,128)(2,1)S(1)}, f32[8,2,256]{2,1,0:T(2,128)}) custom-call(s32[1]{0:T(128)} %bitcast.plane, s32[1]{0:T(128)} %bitcast.11.core.half, f32[4,288,256]{2,1,0:T(8,128)S(1)} %copy-done.19, f32[8,2,256]{2,1,0:T(2,128)S(1)} %all-to-all-done.7.part_ref, f32[16,256]{1,0:T(8,128)S(1)} %collective-permute-done.6.par_ref, ...), custom_call_target="tpu_custom_call" | custom-call | flops 1200000000 | bytes 4000000 | tf_op jit(solution)/shard_map/layer/pallas_call | solution.py:122
  157.6 3.3 %all-to-all-start.8 = ((f32[8,2,256]{2,1,0:T(2,128)}), f32[8,2,256]{2,1,0:T(2,128)S(1)}, u32[]{:S(2)}, u32[]{:S(2)}) async-start(f32[8,2,256]{2,1,0:T(2,128)} %get-tuple-element.85), calls=%async_computation.8 | async-start | bytes 32768 | tf_op jit(solution)/shard_map/all_to_all | solution.py:277
  161.0 5.3 %all-to-all-done.8.part_ref = f32[8,2,256]{2,1,0:T(2,128)S(1)} async-done(((f32[8,2,256]{2,1,0:T(2,128)}), f32[8,2,256]{2,1,0:T(2,128)S(1)}, u32[]{:S(2)}, u32[]{:S(2)}) %all-to-all-start.8) | async-done | bytes 16416 | tf_op jit(solution)/shard_map/all_to_all | solution.py:277
  167.3 2.7 %layer.20 = (bf16[4,288,256]{2,1,0:T(8,128)(2,1)S(1)}, f32[8,2,256]{2,1,0:T(2,128)S(1)}) custom-call(s32[1]{0:T(128)} %bitcast.plane, s32[1]{0:T(128)} %bitcast.11.core.half, bf16[4,288,256]{2,1,0:T(8,128)(2,1)S(1)} %copy-done.8, f32[8,2,256]{2,1,0:T(2,128)S(1)} %all-to-all-done.8.part_ref, f32[16,256]{1,0:T(8,128)S(1)} %collective-permute-done.6.par_ref, ...), custom_call_target="tpu_custom_call" | custom-call | flops 1200000000 | bytes 4000000 | tf_op jit(solution)/shard_map/layer/pallas_call | solution.py:122
  170.7 7.7 %all_to_all.69 = f32[8,2,256]{2,1,0:T(2,128)S(1)} all-to-all(f32[8,2,256]{2,1,0:T(2,128)S(1)} %get-tuple-element.87), channel_id=1, replica_groups=mesh['z'=8,'y'=4,'x'=4,'c'=2] {'y','c'}, dimensions={0} | all-to-all | bytes 32768 | tf_op jit(solution)/shard_map/all_to_all | solution.py:277
  179.1 3.3 %layer.21 = (bf16[4,288,256]{2,1,0:T(8,128)(2,1)S(1)}, f32[8,2,256]{2,1,0:T(2,128)}) custom-call(s32[1]{0:T(128)} %bitcast.plane, s32[1]{0:T(128)} %bitcast.11.core.half, bf16[4,288,256]{2,1,0:T(8,128)(2,1)S(1)} %collective-permute-done.15.h_ref, f32[8,2,256]{2,1,0:T(2,128)S(1)} %collective-permute-done.16.part_ref, ...), custom_call_target="tpu_custom_call" | custom-call | flops 1200000000 | bytes 4000000 | tf_op jit(solution)/shard_map/layer/pallas_call | solution.py:122
  183.2 3.3 %all-to-all-start.10 = ((f32[8,2,256]{2,1,0:T(2,128)}), f32[8,2,256]{2,1,0:T(2,128)S(1)}, u32[]{:S(2)}, u32[]{:S(2)}) async-start(f32[8,2,256]{2,1,0:T(2,128)} %get-tuple-element.91), calls=%async_computation.10 | async-start | bytes 32768 | tf_op jit(solution)/shard_map/all_to_all | solution.py:277
  193.4 2.7 %layer.22 = (bf16[4,288,256]{2,1,0:T(8,128)(2,1)S(1)}, f32[8,2,256]{2,1,0:T(2,128)S(1)}) custom-call(s32[1]{0:T(128)} %bitcast.plane, s32[1]{0:T(128)} %bitcast.11.core.half, bf16[4,288,256]{2,1,0:T(8,128)(2,1)S(1)} %copy-done.11, f32[8,2,256]{2,1,0:T(2,128)S(1)} %all-to-all-done.10.part_ref, f32[8,256]{1,0:T(8,128)S(1)} %collective-permute-done.1.par_ref, ...), custom_call_target="tpu_custom_call" | custom-call | flops 1200000000 | bytes 4000000 | tf_op jit(solution)/shard_map/layer/pallas_call | solution.py:122
  196.8 9.9 %all_to_all.70.part_ref = f32[8,2,256]{2,1,0:T(2,128)S(1)} all-to-all(f32[8,2,256]{2,1,0:T(2,128)S(1)} %get-tuple-element.93), channel_id=1, replica_groups=mesh['z'=8,'y'=4,'x'=4,'c'=2] {'y','c'}, dimensions={0} | all-to-all | bytes 32768 | tf_op jit(solution)/shard_map/all_to_all | solution.py:277
  209.2 37.4 %collective-permute-done.14.refs_4_ = bf16[4,288,256]{2,1,0:T(8,128)(2,1)} collective-permute-done((bf16[4,288,256]{2,1,0:T(8,128)(2,1)}, bf16[4,288,256]{2,1,0:T(8,128)(2,1)}, u32[]{:S(2)}, u32[]{:S(2)}) %collective-permute-start.14) | collective-permute-done | bytes 589856 | tf_op jit(solution)/shard_map/ppermute | solution.py:225
  250.9 13.8 %all_to_all.71 = bf16[4,4,64,256]{3,2,1,0:T(8,128)(2,1)S(1)} all-to-all(bf16[4,4,64,256]{3,2,1,0:T(8,128)(2,1)S(1)} %maximum_select_fusion), channel_id=1, replica_groups=mesh['z'=8,'y'=4,'x'=4,'c'=2] {'x'}, dimensions={0} | all-to-all | bytes 1048576 | tf_op jit(solution)/shard_map/all_to_all | solution.py:323
  (125 shorter events, 56.3 us)
Async XLA Ops:
  0.0 13.8 %copy-start = (bf16[1,256,256]{2,1,0:T(8,128)(2,1)S(1)}, bf16[1,256,256]{2,1,0:T(8,128)(2,1)}, u32[]{:S(2)}) copy-start(bf16[1,256,256]{2,1,0:T(8,128)(2,1)} %param.15) | copy-start | bytes 393220
  2.3 14.9 %all-to-all-start = ((f32[32,1,256]{2,1,0:T(1,128)}), f32[32,1,256]{2,1,0:T(1,128)S(1)}, u32[]{:S(2)}, u32[]{:S(2)}) async-start(f32[32,1,256]{2,1,0:T(1,128)} %all_to_all.42), calls=%async_computation | async-start | bytes 65536 | tf_op jit(solution)/shard_map/all_to_all | solution.py:246
  11.9 6.4 %collective-permute-start.3 = (bf16[2,1152,256]{2,1,0:T(8,128)(2,1)}, bf16[2,1152,256]{2,1,0:T(8,128)(2,1)}, u32[]{:S(2)}, u32[]{:S(2)}) collective-permute-start(bf16[2,1152,256]{2,1,0:T(8,128)(2,1)} %get-tuple-element.72), channel_id=1, source_target_pairs={{64,32},{65,33},{66,34},{67,35},{68,36},{69,37},{70,38},{71,39},{7... | collective-permute-start | bytes 3538952 | tf_op jit(solution)/shard_map/ppermute | solution.py:225
  18.3 91.9 %collective-permute-start.4 = (bf16[2,1152,256]{2,1,0:T(8,128)(2,1)}, bf16[2,1152,256]{2,1,0:T(8,128)(2,1)}, u32[]{:S(2)}, u32[]{:S(2)}) collective-permute-start(bf16[2,1152,256]{2,1,0:T(8,128)(2,1)} %collective-permute-done.3.refs_0_), channel_id=1, source_target_pairs={{0,1},{1,0},{2,3},{3,2},{4,5},{5,4},{6,7},{7,6},{8,9},{9,8},{10,11... | collective-permute-start | bytes 3538952 | tf_op jit(solution)/shard_map/ppermute | solution.py:225
  22.0 8.6 %all-to-all-start.1 = ((f32[8,2,256]{2,1,0:T(2,128)}), f32[8,2,256]{2,1,0:T(2,128)S(1)}, u32[]{:S(2)}, u32[]{:S(2)}) async-start(f32[8,2,256]{2,1,0:T(2,128)} %get-tuple-element.58), calls=%async_computation.1 | async-start | bytes 32768 | tf_op jit(solution)/shard_map/all_to_all | solution.py:277
  25.4 9.1 %collective-permute-start.1 = (f32[8,256]{1,0:T(8,128)S(1)}, f32[8,256]{1,0:T(8,128)S(1)}, u32[]{:S(2)}, u32[]{:S(2)}) collective-permute-start(f32[8,256]{1,0:T(8,128)S(1)} %concatenate.24.par_ref), channel_id=1, source_target_pairs={{64,32},{192,224},{128,96},{65,33},{193,225},{129,97},{66,34},{194... | collective-permute-start | bytes 24584 | tf_op jit(solution)/shard_map/ppermute | solution.py:225
  34.5 8.6 %all-to-all-start.2 = ((f32[8,2,256]{2,1,0:T(2,128)}), f32[8,2,256]{2,1,0:T(2,128)S(1)}, u32[]{:S(2)}, u32[]{:S(2)}) async-start(f32[8,2,256]{2,1,0:T(2,128)} %get-tuple-element.61), calls=%async_computation.2 | async-start | bytes 32768 | tf_op jit(solution)/shard_map/all_to_all | solution.py:277
  37.8 44.6 %collective-permute-start = (bf16[4,288,256]{2,1,0:T(8,128)(2,1)S(1)}, bf16[4,288,256]{2,1,0:T(8,128)(2,1)}, u32[]{:S(2)}, u32[]{:S(2)}) collective-permute-start(bf16[4,288,256]{2,1,0:T(8,128)(2,1)S(1)} %get-tuple-element.59.refs_0_), channel_id=1, source_target_pairs={{0,32},{1,33},{2,34},{3,35},{4,36},{5,37},{6,38},{7,39},{8,40},{9,... | collective-permute-start | bytes 1769480 | tf_op jit(solution)/shard_map/ppermute | solution.py:225
  43.1 39.4 %collective-permute-start.7 = (bf16[1,1152,256]{2,1,0:T(8,128)(2,1)}, bf16[1,1152,256]{2,1,0:T(8,128)(2,1)}, u32[]{:S(2)}, u32[]{:S(2)}) collective-permute-start(bf16[1,1152,256]{2,1,0:T(8,128)(2,1)} %get-tuple-element.80), channel_id=1, source_target_pairs={{96,32},{160,224},{97,33},{161,225},{98,34},{162,226},{99,35},{163... | collective-permute-start | bytes 1769480 | tf_op jit(solution)/shard_map/ppermute | solution.py:225
  44.6 47.0 %collective-permute-start.9 = (bf16[1,1152,256]{2,1,0:T(8,128)(2,1)}, bf16[1,1152,256]{2,1,0:T(8,128)(2,1)}, u32[]{:S(2)}, u32[]{:S(2)}) collective-permute-start(bf16[1,1152,256]{2,1,0:T(8,128)(2,1)} %get-tuple-element.83), channel_id=1, source_target_pairs={{96,32},{97,33},{98,34},{99,35},{100,36},{101,37},{102,38},{103,39... | collective-permute-start | bytes 1769480 | tf_op jit(solution)/shard_map/ppermute | solution.py:225
  46.1 0.7 collective-permute-start.2
  46.7 58.2 %collective-permute-start.12 = (bf16[1,1152,256]{2,1,0:T(8,128)(2,1)}, bf16[1,1152,256]{2,1,0:T(8,128)(2,1)}, u32[]{:S(2)}, u32[]{:S(2)}) collective-permute-start(bf16[1,1152,256]{2,1,0:T(8,128)(2,1)} %get-tuple-element.80), channel_id=1, source_target_pairs={{128,32},{192,224},{129,33},{193,225},{130,34},{194,226},{131,35},... | collective-permute-start | bytes 1769480 | tf_op jit(solution)/shard_map/ppermute | solution.py:225
  82.5 50.5 %collective-permute-start.8 = (bf16[1,1152,256]{2,1,0:T(8,128)(2,1)}, bf16[1,1152,256]{2,1,0:T(8,128)(2,1)}, u32[]{:S(2)}, u32[]{:S(2)}) collective-permute-start(bf16[1,1152,256]{2,1,0:T(8,128)(2,1)} %collective-permute-done.7.refs_0_), channel_id=1, source_target_pairs={{0,1},{1,0},{2,3},{3,2},{4,5},{5,4},{6,7},{7,6},{8,9},{9,8},{10,11... | collective-permute-start | bytes 1769480 | tf_op jit(solution)/shard_map/ppermute | solution.py:225
  87.0 9.9 %all-to-all-start.3 = ((f32[8,2,256]{2,1,0:T(2,128)}), f32[8,2,256]{2,1,0:T(2,128)S(1)}, u32[]{:S(2)}, u32[]{:S(2)}) async-start(f32[8,2,256]{2,1,0:T(2,128)} %get-tuple-element.68), calls=%async_computation.3 | async-start | bytes 32768 | tf_op jit(solution)/shard_map/all_to_all | solution.py:277
  91.6 55.3 %collective-permute-start.10 = (bf16[1,1152,256]{2,1,0:T(8,128)(2,1)}, bf16[1,1152,256]{2,1,0:T(8,128)(2,1)}, u32[]{:S(2)}, u32[]{:S(2)}) collective-permute-start(bf16[1,1152,256]{2,1,0:T(8,128)(2,1)} %collective-permute-done.9.refs_0_), channel_id=1, source_target_pairs={{0,1},{1,0},{2,3},{3,2},{4,5},{5,4},{6,7},{7,6},{8,9},{9,8},{10,11... | collective-permute-start | bytes 1769480 | tf_op jit(solution)/shard_map/ppermute | solution.py:225
  101.6 8.6 %all-to-all-start.4 = ((f32[8,2,256]{2,1,0:T(2,128)}), f32[8,2,256]{2,1,0:T(2,128)S(1)}, u32[]{:S(2)}, u32[]{:S(2)}) async-start(f32[8,2,256]{2,1,0:T(2,128)} %get-tuple-element.70), calls=%async_computation.4 | async-start | bytes 32768 | tf_op jit(solution)/shard_map/all_to_all | solution.py:277
  104.9 56.0 %collective-permute-start.13 = (bf16[1,1152,256]{2,1,0:T(8,128)(2,1)}, bf16[1,1152,256]{2,1,0:T(8,128)(2,1)}, u32[]{:S(2)}, u32[]{:S(2)}) collective-permute-start(bf16[1,1152,256]{2,1,0:T(8,128)(2,1)} %collective-permute-done.12.refs_0_), channel_id=1, source_target_pairs={{0,1},{1,0},{2,3},{3,2},{4,5},{5,4},{6,7},{7,6},{8,9},{9,8},{10,11... | collective-permute-start | bytes 1769480 | tf_op jit(solution)/shard_map/ppermute | solution.py:225
  115.6 8.6 %all-to-all-start.5 = ((f32[8,2,256]{2,1,0:T(2,128)}), f32[8,2,256]{2,1,0:T(2,128)S(1)}, u32[]{:S(2)}, u32[]{:S(2)}) async-start(f32[8,2,256]{2,1,0:T(2,128)} %get-tuple-element.74), calls=%async_computation.5 | async-start | bytes 32768 | tf_op jit(solution)/shard_map/all_to_all | solution.py:277
  118.9 10.7 %collective-permute-start.6 = (f32[16,256]{1,0:T(8,128)S(1)}, f32[16,256]{1,0:T(8,128)S(1)}, u32[]{:S(2)}, u32[]{:S(2)}) collective-permute-start(f32[16,256]{1,0:T(8,128)S(1)} %pad_maximum_fusion), channel_id=1, source_target_pairs={{96,32},{160,224},{97,33},{161,225},{98,34},{162,226},{99,35},{163... | collective-permute-start | bytes 49160 | tf_op jit(solution)/shard_map/ppermute | solution.py:225
  129.6 8.6 %all-to-all-start.6 = ((f32[8,2,256]{2,1,0:T(2,128)}), f32[8,2,256]{2,1,0:T(2,128)S(1)}, u32[]{:S(2)}, u32[]{:S(2)}) async-start(f32[8,2,256]{2,1,0:T(2,128)} %get-tuple-element.78), calls=%async_computation.6 | async-start | bytes 32768 | tf_op jit(solution)/shard_map/all_to_all | solution.py:277
  143.6 8.6 %all-to-all-start.7 = ((f32[8,2,256]{2,1,0:T(2,128)}), f32[8,2,256]{2,1,0:T(2,128)S(1)}, u32[]{:S(2)}, u32[]{:S(2)}) async-start(f32[8,2,256]{2,1,0:T(2,128)} %get-tuple-element.82), calls=%async_computation.7 | async-start | bytes 32768 | tf_op jit(solution)/shard_map/all_to_all | solution.py:277
  157.6 8.6 %all-to-all-start.8 = ((f32[8,2,256]{2,1,0:T(2,128)}), f32[8,2,256]{2,1,0:T(2,128)S(1)}, u32[]{:S(2)}, u32[]{:S(2)}) async-start(f32[8,2,256]{2,1,0:T(2,128)} %get-tuple-element.85), calls=%async_computation.8 | async-start | bytes 32768 | tf_op jit(solution)/shard_map/all_to_all | solution.py:277
  170.0 9.1 %collective-permute-start.15 = (bf16[4,288,256]{2,1,0:T(8,128)(2,1)S(1)}, bf16[4,288,256]{2,1,0:T(8,128)(2,1)S(1)}, u32[]{:S(2)}, u32[]{:S(2)}) collective-permute-start(bf16[4,288,256]{2,1,0:T(8,128)(2,1)S(1)} %get-tuple-element.86), channel_id=1, source_target_pairs={{32,224},{33,225},{34,226},{35,227},{36,228},{37,229},{38,230},{39... | collective-permute-start | bytes 1769480 | tf_op jit(solution)/shard_map/ppermute | solution.py:225
  178.4 0.7 collective-permute-start.16
  183.2 9.1 %all-to-all-start.10 = ((f32[8,2,256]{2,1,0:T(2,128)}), f32[8,2,256]{2,1,0:T(2,128)S(1)}, u32[]{:S(2)}, u32[]{:S(2)}) async-start(f32[8,2,256]{2,1,0:T(2,128)} %get-tuple-element.91), calls=%async_computation.10 | async-start | bytes 32768 | tf_op jit(solution)/shard_map/all_to_all | solution.py:277
  186.5 22.6 %collective-permute-start.5 = (bf16[4,288,256]{2,1,0:T(8,128)(2,1)}, bf16[4,288,256]{2,1,0:T(8,128)(2,1)}, u32[]{:S(2)}, u32[]{:S(2)}) collective-permute-start(bf16[4,288,256]{2,1,0:T(8,128)(2,1)} %copy-done.5), channel_id=1, source_target_pairs={{32,64},{33,65},{34,66},{35,67},{36,68},{37,69},{38,70},{39,71},{4... | collective-permute-start | bytes 1769480 | tf_op jit(solution)/shard_map/ppermute | solution.py:225
  188.1 21.1 %collective-permute-start.11 = (bf16[4,288,256]{2,1,0:T(8,128)(2,1)}, bf16[4,288,256]{2,1,0:T(8,128)(2,1)}, u32[]{:S(2)}, u32[]{:S(2)}) collective-permute-start(bf16[4,288,256]{2,1,0:T(8,128)(2,1)} %copy-done.7), channel_id=1, source_target_pairs={{32,96},{33,97},{34,98},{35,99},{36,100},{37,101},{38,102},{39,103... | collective-permute-start | bytes 1769480 | tf_op jit(solution)/shard_map/ppermute | solution.py:225
  189.5 57.1 %collective-permute-start.14 = (bf16[4,288,256]{2,1,0:T(8,128)(2,1)}, bf16[4,288,256]{2,1,0:T(8,128)(2,1)}, u32[]{:S(2)}, u32[]{:S(2)}) collective-permute-start(bf16[4,288,256]{2,1,0:T(8,128)(2,1)} %copy-done.9), channel_id=1, source_target_pairs={{32,128},{33,129},{34,130},{35,131},{36,132},{37,133},{38,134},{39... | collective-permute-start | bytes 1769480 | tf_op jit(solution)/shard_map/ppermute | solution.py:225
  190.8 55.8 %collective-permute-start.17 = (bf16[4,288,256]{2,1,0:T(8,128)(2,1)}, bf16[4,288,256]{2,1,0:T(8,128)(2,1)}, u32[]{:S(2)}, u32[]{:S(2)}) collective-permute-start(bf16[4,288,256]{2,1,0:T(8,128)(2,1)} %copy-done.10), channel_id=1, source_target_pairs={{224,160},{225,161},{226,162},{227,163},{228,164},{229,165},{230,1... | collective-permute-start | bytes 1769480 | tf_op jit(solution)/shard_map/ppermute | solution.py:225
  196.1 50.5 %collective-permute-start.18 = (bf16[4,288,256]{2,1,0:T(8,128)(2,1)S(1)}, bf16[4,288,256]{2,1,0:T(8,128)(2,1)S(1)}, u32[]{:S(2)}, u32[]{:S(2)}) collective-permute-start(bf16[4,288,256]{2,1,0:T(8,128)(2,1)S(1)} %get-tuple-element.92.h_ref), channel_id=1, source_target_pairs={{224,192},{225,193},{226,194},{227,195},{228,196},{229,197},{230,1... | collective-permute-start | bytes 1769480 | tf_op jit(solution)/shard_map/ppermute | solution.py:225
  206.6 40.0 %copy-start.4 = (bf16[4,288,256]{2,1,0:T(8,128)(2,1)S(1)}, bf16[4,288,256]{2,1,0:T(8,128)(2,1)}, u32[]{:S(2)}) copy-start(bf16[4,288,256]{2,1,0:T(8,128)(2,1)} %copy-done.2) | copy-start | bytes 1769476
  249.0 1.8 collective-permute-start.19
  (22 other events, 57.8 us)
